TPU v7x, 32 devices: a whole 2x2x4 slice. The times are simulated.
32 devices in a mesh: section: 2 (over core), dp: 8 (over z, x), rep: 2 (over y).
Axes of the slice: x: 2, y: 2, z: 4, core: 2. Of those that a mesh axis runs over, the one named last changes fastest.
Arguments:
- patches: bfloat16 [64, 196, 768], P(('dp', 'rep'), None, 'section'), may hold values from -6 to 6
- captions: bfloat16 [64, 128, 768], P(('dp', 'rep'), None, 'section'), may hold values from -6 to 6
- tissue_keep: int32 [64, 196], P(('dp', 'rep')), may hold values from 0 to 1, as said below
- caption_mask: int32 [64, 128], P(('dp', 'rep')), may hold values from 0 to 1, as said below
- mixing: bfloat16 [2, 768, 2304], P('section', 'dp'), may hold values from -0.21875 to 0.21875
- merging: bfloat16 [2, 768, 768], P('section', 'dp'), may hold values from -0.875 to 0.875
- crossing: bfloat16 [2, 768, 1536], P('section', 'dp'), may hold values from -0.21875 to 0.21875
- widening: bfloat16 [2, 768, 3072], P('section', 'dp'), may hold values from -0.21875 to 0.21875
- narrowing: bfloat16 [2, 3072, 768], P('section', 'dp'), may hold values from -0.109375 to 0.109375
- scales: bfloat16 [2, 3, 768], P('section', None, 'dp'), may hold values from 0.5 to 1.5
- cotangent: bfloat16 [64, 128, 768], P(('dp', 'rep'), None, 'section'), may hold values from -6 to 6
Outputs:
- decoded: bfloat16 [64, 128, 768], P(('dp', 'rep'), None, 'section')
- caption_grad: bfloat16 [64, 128, 768], P(('dp', 'rep'), None, 'section')
- patch_grad: bfloat16 [64, 196, 768], P(('dp', 'rep'), None, 'section')
- mixing_grad: float32 [2, 768, 2304], P('section', 'dp')
- merging_grad: float32 [2, 768, 768], P('section', 'dp')
- crossing_grad: float32 [2, 768, 1536], P('section', 'dp')
- widening_grad: float32 [2, 768, 3072], P('section', 'dp')
- narrowing_grad: float32 [2, 3072, 768], P('section', 'dp')
- scales_grad: float32 [2, 3, 768], P('section', None, 'dp')
Inputs may be any that keep to these rules, and one draw needn't show every extreme that they name: `tissue_keep`: every image keeps between 24 and 196 patches, in any places; some image keeps exactly 24, some all. `caption_mask`: each caption's mask is 1 on a prefix of 8 to 128 positions and 0 after it; both ends are reached.
All inputs are finite; a program needn't handle non-finite values.
Results may differ from a plain program's by a relative error of at most 0.019.
Values may be sent and summed in bfloat16 or wider, within the bound.
A program may use at most 320 MiB of HBM per device.

v0:
```python
import jax
import jax.numpy as jnp
from jax import lax
from jax.sharding import PartitionSpec as P

HEADS = 12
MICRO = 2


def partner(value, axis, distance):
    mask = 2**distance
    pairs = [(source, source ^ mask) for source in range(lax.axis_size(axis))]
    return lax.ppermute(value, axis, pairs)


def as_sent(value):
    return jax.tree.map(lambda a: a.astype(jnp.bfloat16) if a.dtype == jnp.float32 else a, value)


def to_low(values):
    return values.astype(jnp.bfloat16)


def layer_norm(values, gain):
    centered = values - jnp.mean(values, axis=-1, keepdims=True)
    return (
        centered * lax.rsqrt(jnp.mean(centered * centered, axis=-1, keepdims=True) + 1e-05) * gain
    )


def gelu_exact(values):
    return jax.nn.gelu(values, approximate=False)


def project(acts, weight):
    return jnp.einsum("bsd,de->bse", acts, weight, preferred_element_type=jnp.float32)


def back_project(grads, weight):
    return jnp.einsum("bse,de->bsd", grads, weight, preferred_element_type=jnp.float32)


def weight_grad(acts, grads):
    return jnp.einsum("bsd,bse->de", acts, grads, preferred_element_type=jnp.float32)


def split_heads(values):
    return values.reshape(values.shape[0], values.shape[1], HEADS, values.shape[2] // HEADS)


def attend_forward(queries, keys, values, mask):
    scale = queries.shape[-1] ** (-0.5)
    scores = (
        jnp.einsum("bqhe,bkhe->bhqk", queries, keys, preferred_element_type=jnp.float32) * scale
    )
    scores = jnp.where(mask[:, None], scores, -1000000000.0)
    peak = jnp.max(scores, axis=-1, keepdims=True)
    expo = jnp.exp(scores - peak)
    softmaxed = expo / jnp.sum(expo, axis=-1, keepdims=True)
    mixed = jnp.einsum(
        "bhqk,bkhe->bqhe", to_low(softmaxed), values, preferred_element_type=jnp.float32
    )
    return (to_low(mixed), softmaxed)


def attend_backward(grad_mixed, softmaxed, queries, keys, values, mask):
    scale = queries.shape[-1] ** (-0.5)
    grad_soft = jnp.einsum(
        "bqhe,bkhe->bhqk", grad_mixed, values, preferred_element_type=jnp.float32
    )
    grad_value = jnp.einsum(
        "bhqk,bqhe->bkhe", to_low(softmaxed), grad_mixed, preferred_element_type=jnp.float32
    )
    grad_scores = softmaxed * (grad_soft - jnp.sum(softmaxed * grad_soft, axis=-1, keepdims=True))
    grad_scores = to_low(jnp.where(mask[:, None], grad_scores, 0.0))
    grad_query = (
        jnp.einsum("bhqk,bkhe->bqhe", grad_scores, keys, preferred_element_type=jnp.float32) * scale
    )
    grad_key = (
        jnp.einsum("bhqk,bqhe->bkhe", grad_scores, queries, preferred_element_type=jnp.float32)
        * scale
    )
    return (grad_query, grad_key, grad_value)


def attention_forward(states, gain, w_in, w_out, mask):
    width = states.shape[2]
    first = to_low(layer_norm(states, gain))
    united = to_low(project(first, w_in))
    queries = split_heads(united[..., :width])
    keys = split_heads(united[..., width : 2 * width])
    values = split_heads(united[..., 2 * width :])
    mixed, softmaxed = attend_forward(queries, keys, values, mask)
    joined = mixed.reshape(states.shape)
    hidden = states + project(joined, w_out)
    return (first, queries, keys, values, softmaxed, joined, hidden)


def feedforward_forward(states, gain, w_up, w_down):
    second = to_low(layer_norm(states, gain))
    widened = project(second, w_up)
    active = to_low(gelu_exact(widened))
    after = states + project(active, w_down)
    return (second, widened, active, after)


def attention_back(
    grad_after, states, gain, first, queries, keys, values, softmaxed, joined, mask, w_in, w_out
):
    branch = to_low(grad_after)
    g_out = weight_grad(joined, branch)
    grad_joined = to_low(back_project(branch, w_out))
    grad_query, grad_key, grad_value = attend_backward(
        split_heads(grad_joined), softmaxed, queries, keys, values, mask
    )
    shape = states.shape
    grad_united = to_low(
        jnp.concatenate(
            [grad_query.reshape(shape), grad_key.reshape(shape), grad_value.reshape(shape)], axis=-1
        )
    )
    g_in = weight_grad(first, grad_united)
    _, pull = jax.vjp(layer_norm, states, gain)
    grad_norm, g_gain = pull(back_project(grad_united, w_in))
    return (grad_after + grad_norm, g_in, g_out, g_gain)


def feedforward_back(grad_after, states, gain, second, widened, active, w_up, w_down):
    branch = to_low(grad_after)
    g_down = weight_grad(active, branch)
    _, pull = jax.vjp(gelu_exact, widened)
    grad_wide = to_low(pull(back_project(branch, w_down))[0])
    g_up = weight_grad(second, grad_wide)
    _, pull = jax.vjp(layer_norm, states, gain)
    grad_norm, g_gain = pull(back_project(grad_wide, w_up))
    return (grad_after + grad_norm, g_up, g_down, g_gain)


def encoder_pass(states, keep, weights):
    w_in, w_out, w_pair, w_up, w_down, gains = weights
    gains = gains.astype(jnp.float32)
    batch, count, width = states.shape
    mask = jnp.broadcast_to(keep[:, None, :] > 0, (batch, count, count))
    first, queries, keys, values, softmaxed, joined, hidden = attention_forward(
        states, gains[0], w_in, w_out, mask
    )
    second, widened, active, after = feedforward_forward(hidden, gains[1], w_up, w_down)
    final = to_low(layer_norm(after, gains[2]))
    memory = to_low(project(final, w_pair))
    saved = (
        mask,
        first,
        queries,
        keys,
        values,
        softmaxed,
        joined,
        hidden,
        second,
        widened,
        active,
        after,
        final,
    )
    return (memory, saved)


def encoder_backward(states, keep, weights, grad_memory):
    w_in, w_out, w_pair, w_up, w_down, gains = weights
    gains = gains.astype(jnp.float32)
    _, saved = encoder_pass(states, keep, weights)
    (
        mask,
        first,
        queries,
        keys,
        values,
        softmaxed,
        joined,
        hidden,
        second,
        widened,
        active,
        after,
        final,
    ) = saved
    g_pair = weight_grad(final, grad_memory)
    _, pull = jax.vjp(layer_norm, after, gains[2])
    grad_after, g_final = pull(back_project(grad_memory, w_pair))
    grad_hidden, g_up, g_down, g_second = feedforward_back(
        grad_after, hidden, gains[1], second, widened, active, w_up, w_down
    )
    grad_states, g_in, g_out, g_first = attention_back(
        grad_hidden,
        states,
        gains[0],
        first,
        queries,
        keys,
        values,
        softmaxed,
        joined,
        mask,
        w_in,
        w_out,
    )
    return (
        grad_states,
        (g_in, g_out, g_pair, g_up, g_down, jnp.stack([g_first, g_second, g_final])),
    )


def decoder_step(text, text_keep, memory, keep, weights, cotan):
    w_in, w_out, w_pair, w_up, w_down, gains = weights
    gains = gains.astype(jnp.float32)
    batch, length, width = text.shape
    query_pos = lax.broadcasted_iota(jnp.int32, (length, length), 0)
    key_pos = lax.broadcasted_iota(jnp.int32, (length, length), 1)
    self_mask = (key_pos <= query_pos)[None] & (text_keep[:, None, :] > 0)
    cross_mask = jnp.broadcast_to(keep[:, None, :] > 0, (batch, length, keep.shape[1]))
    first, queries, keys, values, softmaxed, joined, hidden = attention_forward(
        text, gains[0], w_in, w_out, self_mask
    )
    second = to_low(layer_norm(hidden, gains[1]))
    cross_query = to_low(project(second, w_pair[:, :width]))
    memory_keys = split_heads(memory[..., :width])
    memory_vals = split_heads(memory[..., width:])
    cross_mixed, cross_soft = attend_forward(
        split_heads(cross_query), memory_keys, memory_vals, cross_mask
    )
    cross_joined = cross_mixed.reshape(text.shape)
    crossed = hidden + project(cross_joined, w_pair[:, width:])
    third, widened, active, output = feedforward_forward(crossed, gains[2], w_up, w_down)
    grad_crossed, g_up, g_down, g_third = feedforward_back(
        cotan, crossed, gains[2], third, widened, active, w_up, w_down
    )
    branch = to_low(grad_crossed)
    g_cross_out = weight_grad(cross_joined, branch)
    grad_cross_joined = to_low(back_project(branch, w_pair[:, width:]))
    grad_query, grad_key, grad_value = attend_backward(
        split_heads(grad_cross_joined),
        cross_soft,
        split_heads(cross_query),
        memory_keys,
        memory_vals,
        cross_mask,
    )
    grad_cross_query = to_low(grad_query.reshape(text.shape))
    mem_shape = (batch, memory.shape[1], width)
    grad_memory = to_low(
        jnp.concatenate([grad_key.reshape(mem_shape), grad_value.reshape(mem_shape)], axis=-1)
    )
    g_cross_query = weight_grad(second, grad_cross_query)
    _, pull = jax.vjp(layer_norm, hidden, gains[1])
    grad_norm, g_second = pull(back_project(grad_cross_query, w_pair[:, :width]))
    grad_hidden = grad_crossed + grad_norm
    grad_text, g_in, g_out, g_first = attention_back(
        grad_hidden,
        text,
        gains[0],
        first,
        queries,
        keys,
        values,
        softmaxed,
        joined,
        self_mask,
        w_in,
        w_out,
    )
    g_pair = jnp.concatenate([g_cross_query, g_cross_out], axis=1)
    return (
        output,
        grad_text,
        grad_memory,
        (g_in, g_out, g_pair, g_up, g_down, jnp.stack([g_first, g_second, g_third])),
    )


def local(
    patches,
    captions,
    tissue_keep,
    caption_mask,
    mixing,
    merging,
    crossing,
    widening,
    narrowing,
    scales,
    cotangent,
):
    section = lax.axis_index("section")
    on_encoder = section == 0
    images, count, half = patches.shape
    length = captions.shape[1]
    width = 2 * half
    spare = 2 * length - count
    text_pair = jnp.concatenate([captions, cotangent], axis=1)
    padded = jnp.pad(patches, ((0, 0), (0, spare), (0, 0)))
    incoming = partner(jnp.where(on_encoder, text_pair, padded), "section", 0)
    full_patches = jnp.concatenate([patches, incoming[:, :count]], axis=2).astype(jnp.float32)
    full_text = jnp.concatenate([incoming[:, :length], captions], axis=2).astype(jnp.float32)
    full_cotan = jnp.concatenate([incoming[:, length:], cotangent], axis=2).astype(jnp.float32)
    gathered = (
        lax.all_gather(mixing, "dp", axis=1, tiled=True),
        lax.all_gather(merging, "dp", axis=1, tiled=True),
        lax.all_gather(crossing, "dp", axis=1, tiled=True),
        lax.all_gather(widening, "dp", axis=1, tiled=True),
        lax.all_gather(narrowing, "dp", axis=1, tiled=True),
        lax.all_gather(scales, "dp", axis=2, tiled=True),
    )
    weights = tuple((piece[0] for piece in gathered))
    per_micro = images // MICRO
    zero_grads = tuple((jnp.zeros(piece.shape, jnp.float32) for piece in weights))
    zero_send = jnp.zeros((per_micro, count, 2 * width), jnp.bfloat16)
    zero_patch = jnp.zeros((per_micro, count, width), jnp.float32)
    zero_text = jnp.zeros((per_micro, length, width), jnp.float32)
    totals = zero_grads
    patch_grads = jnp.zeros((images, count, width), jnp.float32)
    decoded_all = jnp.zeros((images, length, width), jnp.float32)
    caption_all = jnp.zeros((images, length, width), jnp.float32)
    received = zero_send
    for tick in range(MICRO + 2):

        def encoder_branch(tick=tick, received=received):
            send, grads, patch_part = (zero_send, zero_grads, zero_patch)
            if tick >= 2:
                start = (tick - 2) * per_micro
                patch_part, grads = encoder_backward(
                    full_patches[start : start + per_micro],
                    tissue_keep[start : start + per_micro],
                    weights,
                    received,
                )
            if tick < MICRO:
                start = tick * per_micro
                send = encoder_pass(
                    full_patches[start : start + per_micro],
                    tissue_keep[start : start + per_micro],
                    weights,
                )[0]
            return (send, grads, patch_part, zero_text, zero_text)

        def decoder_branch(tick=tick, received=received):
            if 1 <= tick <= MICRO:
                start = (tick - 1) * per_micro
                stop = start + per_micro
                output, grad_text, grad_memory, grads = decoder_step(
                    full_text[start:stop],
                    caption_mask[start:stop],
                    received,
                    tissue_keep[start:stop],
                    weights,
                    full_cotan[start:stop],
                )
                return (grad_memory, grads, zero_patch, output, grad_text)
            return (zero_send, zero_grads, zero_patch, zero_text, zero_text)

        send, grads, patch_part, out_part, text_part = lax.cond(
            on_encoder, encoder_branch, decoder_branch
        )
        totals = tuple((total + grad for total, grad in zip(totals, grads)))
        if tick >= 2:
            start = (tick - 2) * per_micro
            patch_grads = patch_grads.at[start : start + per_micro].add(patch_part)
        if 1 <= tick <= MICRO:
            start = (tick - 1) * per_micro
            decoded_all = decoded_all.at[start : start + per_micro].add(out_part)
            caption_all = caption_all.at[start : start + per_micro].add(text_part)
        if tick <= MICRO:
            received = partner(send, "section", 0)
    terms = tuple((total[None] for total in totals))
    shares = (
        lax.psum_scatter(
            terms[0].astype(jnp.bfloat16), "dp", scatter_dimension=1, tiled=True
        ).astype(jnp.float32),
        lax.psum_scatter(
            terms[1].astype(jnp.bfloat16), "dp", scatter_dimension=1, tiled=True
        ).astype(jnp.float32),
        lax.psum_scatter(
            terms[2].astype(jnp.bfloat16), "dp", scatter_dimension=1, tiled=True
        ).astype(jnp.float32),
        lax.psum_scatter(
            terms[3].astype(jnp.bfloat16), "dp", scatter_dimension=1, tiled=True
        ).astype(jnp.float32),
        lax.psum_scatter(
            terms[4].astype(jnp.bfloat16), "dp", scatter_dimension=1, tiled=True
        ).astype(jnp.float32),
        lax.psum_scatter(
            terms[5].astype(jnp.bfloat16), "dp", scatter_dimension=2, tiled=True
        ).astype(jnp.float32),
    )
    summed = jax.tree.map(lambda part: part.astype(jnp.float32), lax.psum(as_sent(shares), "rep"))
    low_patch = to_low(patch_grads)
    low_decoded = to_low(decoded_all)
    low_caption = to_low(caption_all)
    encoder_send = jnp.pad(low_patch[:, :, half:], ((0, 0), (0, spare), (0, 0)))
    decoder_send = jnp.concatenate([low_decoded[:, :, :half], low_caption[:, :, :half]], axis=1)
    returned = partner(jnp.where(on_encoder, encoder_send, decoder_send), "section", 0)
    patch_out = jnp.where(on_encoder, low_patch[:, :, :half], returned[:, :count])
    decoded = jnp.where(on_encoder, returned[:, :length], low_decoded[:, :, half:])
    caption_out = jnp.where(on_encoder, returned[:, length:], low_caption[:, :, half:])
    return (
        decoded,
        caption_out,
        patch_out,
        summed[0],
        summed[1],
        summed[2],
        summed[3],
        summed[4],
        summed[5],
    )


def solution(mesh):
    in_specs = (
        P(("dp", "rep"), None, "section"),
        P(("dp", "rep"), None, "section"),
        P(("dp", "rep"), None),
        P(("dp", "rep"), None),
        P("section", "dp", None),
        P("section", "dp", None),
        P("section", "dp", None),
        P("section", "dp", None),
        P("section", "dp", None),
        P("section", None, "dp"),
        P(("dp", "rep"), None, "section"),
    )
    out_specs = (
        P(("dp", "rep"), None, "section"),
        P(("dp", "rep"), None, "section"),
        P(("dp", "rep"), None, "section"),
        P("section", "dp", None),
        P("section", "dp", None),
        P("section", "dp", None),
        P("section", "dp", None),
        P("section", "dp", None),
        P("section", None, "dp"),
    )
    return jax.shard_map(local, mesh=mesh, in_specs=in_specs, out_specs=out_specs, check_vma=False)
```

profile of v0, /device:TPU:0, one launch (start us, length us, event | category | flops | bytes accessed | tf_op | source)
XLA Modules:
  0.0 1447.4 jit_solution(4908993791743038168)
XLA Ops:
  14.5 33.4 %all_gather.18 = bf16[1,3,768]{1,0,2:T(2,128)(2,1)S(1)} all-gather(bf16[1,3,96]{1,0,2:T(2,128)(2,1)S(1)} %copy.568), channel_id=1, replica_groups=mesh['section'=2,'dp'=8,'rep'=2] {'dp'}, dimensions={2}, use_global_device_ids=true | all-gather | bytes 5184 | tf_op jit(solution)/shard_map/all_gather | solution.py:311
  55.8 52.7 %all-gather.10.cloned.1.call-done = bf16[1,768,1536]{2,1,0:T(8,128)(2,1)} async-done(((bf16[1,96,1536]{2,1,0:T(8,128)(2,1)}), bf16[1,768,1536]{2,1,0:T(8,128)(2,1)}) %all-gather.10.cloned.1.call-update) | async-done | bytes 2359312 | tf_op jit(solution)/shard_map/all_gather | solution.py:308
  108.5 65.4 %all-gather.6.cloned.1.call-done = bf16[1,768,2304]{2,1,0:T(8,128)(2,1)} async-done(((bf16[1,96,2304]{2,1,0:T(8,128)(2,1)}), bf16[1,768,2304]{2,1,0:T(8,128)(2,1)}) %all-gather.6.cloned.1.call-update) | async-done | bytes 3538960 | tf_op jit(solution)/shard_map/all_gather | solution.py:306
  173.9 80.1 %all-gather.12.cloned.1.call-done = bf16[1,768,3072]{2,1,0:T(8,128)(2,1)} async-done(((bf16[1,96,3072]{2,1,0:T(8,128)(2,1)}), bf16[1,768,3072]{2,1,0:T(8,128)(2,1)}) %all-gather.12.cloned.1.call-update) | async-done | bytes 4718608 | tf_op jit(solution)/shard_map/all_gather | solution.py:309
  254.0 79.7 %all-gather.14.cloned.1.call-done = bf16[1,3072,768]{2,1,0:T(8,128)(2,1)} async-done(((bf16[1,384,768]{2,1,0:T(8,128)(2,1)}), bf16[1,3072,768]{2,1,0:T(8,128)(2,1)}) %all-gather.14.cloned.1.call-update) | async-done | bytes 4718608 | tf_op jit(solution)/shard_map/all_gather | solution.py:310
  333.8 44.8 %conditional.5 = (bf16[2,196,1536]{2,1,0:T(8,128)(2,1)}) conditional(s32[]{:T(128)} %convert_element_type.390, () %tuple.65, (f32[4,196,768]{2,0,1:T(4,128)}, bf16[3,768]{1,0:T(4,128)(2,1)S(1)}, bf16[768,2304]{1,0:T(8,128)(2,1)}, s32[4,196]{1,0:T(4,128)S(1)}, bf16[768,768]{1,0:T(8,128)(2,1)}, /*index=5*/bf16[768,3072]{1,0:T(8,128)(2,1)}, ...), branch_computations={%region_0.1_spmd, %region_1.10_spmd} | conditional | flops 6823852544 | bytes 109860824 | solution.py:360
  362.6 13.3 fusion.618
  384.8 67.9 %conditional.6 = (bf16[2,196,1536]{1,2,0:T(8,128)(2,1)}, f32[768,2304]{1,0:T(8,128)}, f32[768,768]{1,0:T(8,128)}, f32[768,3072]{1,0:T(8,128)}, f32[3072,768]{1,0...) conditional(s32[]{:T(128)} %convert_element_type.390, ...), branch_computations={%region_10.32_spmd, %region_32.41_spmd} | conditional | flops 13580513280 | bytes 375091264
  417.7 13.3 fusion.622
  457.7 96.3 %collective-permute-start.2 = (bf16[2,196,1536]{2,0,1:T(2,128)(2,1)}, bf16[2,196,1536]{2,0,1:T(2,128)(2,1)S(1)}, u32[]{:S(2)}, u32[]{:S(2)}) collective-permute-start(bf16[2,196,1536]{2,0,1:T(2,128)(2,1)} %copy.577), channel_id=1, source_target_pairs={{0,16},{16,0},{1,17},{17,1},{2,18},{18,2},{3,19},{19,3},{4,20},{20... | collective-permute-start | bytes 3612680 | tf_op jit(solution)/shard_map/ppermute | solution.py:13
  556.7 160.2 %conditional.7 = (bf16[2,196,1536]{1,2,0:T(8,128)(2,1)}, f32[768,2304]{1,0:T(8,128)}, f32[768,768]{1,0:T(8,128)}, f32[768,3072]{1,0:T(8,128)}, f32[3072,768]{1,0...) conditional(s32[]{:T(128)} %convert_element_type.390, ...), branch_computations={%region_41.63_spmd, %region_63.82_spmd} | conditional | flops 19373477888 | bytes 433556480 | solution.py:360
  571.2 9.8 copy.534
  580.9 12.4 fusion.636
  610.6 11.5 multiply_convert_fusion.33
  646.8 9.6 copy.540
  656.4 12.2 select_convert_fusion.4
  725.8 158.4 %conditional.8 = (f32[768,2304]{1,0:T(8,128)}, f32[768,768]{1,0:T(8,128)}, f32[768,1536]{1,0:T(8,128)}, f32[768,3072]{1,0:T(8,128)}, f32[3072,768]{1,0:T(8,128)}...) conditional(s32[]{:T(128)} %convert_element_type.390, () %tuple.70, (f32[4,196,768]{2,0,1:T(4,128)}, ...), branch_computations={%region_82.83_spmd, %region_83.102_spmd} | conditional | flops 19373477888 | bytes 417747072 | solution.py:360
  743.0 9.8 copy.551
  752.9 12.4 fusion.640
  784.0 11.8 multiply_convert_fusion.44
  821.8 9.6 copy.557
  831.4 11.8 select_convert_fusion.5
  896.5 10.1 fusion.595
  906.7 12.2 fusion.594
  918.9 12.3 fusion.593
  935.1 16.7 %reduce-scatter.11.cloned.1.call-done = bf16[1,96,768]{2,1,0:T(8,128)(2,1)} async-done(((bf16[1,768,768]{2,1,0:T(8,128)(2,1)}), bf16[1,96,768]{2,1,0:T(8,128)(2,1)}) %reduce-scatter.11.cloned.1.call-update) | async-done | bytes 147472 | tf_op jit(solution)/shard_map/reduce_scatter | solution.py:378
  951.8 72.1 %reduce-scatter.13.cloned.1.call-done = bf16[1,96,1536]{2,1,0:T(8,128)(2,1)} async-done(((bf16[1,768,1536]{2,1,0:T(8,128)(2,1)}), bf16[1,96,1536]{2,1,0:T(8,128)(2,1)}) %reduce-scatter.13.cloned.1.call-update) | async-done | bytes 294928 | tf_op jit(solution)/shard_map/reduce_scatter | solution.py:381
  1023.9 82.4 %reduce-scatter.9.cloned.1.call-done = bf16[1,96,2304]{2,1,0:T(8,128)(2,1)} async-done(((bf16[1,768,2304]{2,1,0:T(8,128)(2,1)}), bf16[1,96,2304]{2,1,0:T(8,128)(2,1)}) %reduce-scatter.9.cloned.1.call-update) | async-done | bytes 442384 | tf_op jit(solution)/shard_map/reduce_scatter | solution.py:375
  1106.3 99.0 %reduce-scatter.17.cloned.1.call-done = bf16[1,384,768]{2,1,0:T(8,128)(2,1)} async-done(((bf16[1,3072,768]{2,1,0:T(8,128)(2,1)}), bf16[1,384,768]{2,1,0:T(8,128)(2,1)}) %reduce-scatter.17.cloned.1.call-update) | async-done | bytes 589840 | tf_op jit(solution)/shard_map/reduce_scatter | solution.py:387
  1205.2 98.9 %reduce-scatter.15.cloned.1.call-done = bf16[1,96,3072]{2,1,0:T(8,128)(2,1)} async-done(((bf16[1,768,3072]{2,1,0:T(8,128)(2,1)}), bf16[1,96,3072]{2,1,0:T(8,128)(2,1)}) %reduce-scatter.15.cloned.1.call-update) | async-done | bytes 589840 | tf_op jit(solution)/shard_map/reduce_scatter | solution.py:384
  1309.4 60.1 %reduce-scatter.19.cloned.1.call-done = bf16[96,3]{1,0:T(8,128)(2,1)} async-done(((bf16[768,3]{1,0:T(8,128)(2,1)}), bf16[96,3]{1,0:T(8,128)(2,1)}) %reduce-scatter.19.cloned.1.call-update) | async-done | bytes 592
  1382.7 50.7 %all-reduce.5.cloned.1.call-done = (bf16[1,96,2304]{2,1,0:T(8,128)(2,1)}, bf16[1,96,768]{2,1,0:T(8,128)(2,1)}, bf16[1,96,1536]{2,1,0:T(8,128)(2,1)}, bf16[1,96,3072]{2,1,0:T(8,128)(2,1)}, bf16[1,384,768]{2,1,0:T(8,128)(2,1)}) async-done(((bf16[1,96,2304]{2,1,0:T(8,128)(2,1)}, bf16[1,96,768]{2,1,0:T(8,128)(2,1)}, bf16[1,96,1536]{2,1,0:T(8,128)(2,1)}, bf16[1,96,3072]{2,1,0:T(8,128)(2,1)}, ...) | async-done | bytes 2064400 | tf_op jit(solution)/shard_map/psum | solution.py:394
  (469 shorter events, 356.4 us)
Async XLA Ops:
  7.2 48.6 %all-gather.8.cloned.1.call-start = ((), (), s32[]{:S(2)}) async-start(), calls=%async_computation.7 | async-start | bytes 1327104 | tf_op jit(solution)/shard_map/all_gather | solution.py:307
  7.9 100.6 %all-gather.10.cloned.1.call-start = ((), (), s32[]{:S(2)}) async-start(), calls=%async_computation.8 | async-start | bytes 2654208 | tf_op jit(solution)/shard_map/all_gather | solution.py:308
  8.7 165.2 %all-gather.6.cloned.1.call-start = ((), (), s32[]{:S(2)}) async-start(), calls=%async_computation.6 | async-start | bytes 3981312 | tf_op jit(solution)/shard_map/all_gather | solution.py:306
  9.4 244.6 %all-gather.12.cloned.1.call-start = ((), (), s32[]{:S(2)}) async-start(), calls=%async_computation.9 | async-start | bytes 5308416 | tf_op jit(solution)/shard_map/all_gather | solution.py:309
  10.0 323.8 %all-gather.14.cloned.1.call-start = ((), (), s32[]{:S(2)}) async-start(), calls=%async_computation.10 | async-start | bytes 5308416 | tf_op jit(solution)/shard_map/all_gather | solution.py:310
  10.6 941.2 %reduce-scatter.11.cloned.1.call-start = ((), (), s32[]{:S(2)}) async-start(), calls=%async_computation.12 | async-start | bytes 1327104 | tf_op jit(solution)/shard_map/reduce_scatter | solution.py:378
  13.9 34.3 %collective-permute-start = (bf16[4,256,384]{2,0,1:T(4,128)(2,1)}, bf16[4,256,384]{2,0,1:T(4,128)(2,1)S(1)}, u32[]{:S(2)}, u32[]{:S(2)}) collective-permute-start(bf16[4,256,384]{2,0,1:T(4,128)(2,1)} %maximum_select_fusion), channel_id=1, source_target_pairs={{0,16},{16,0},{1,17},{17,1},{2,18},{18,2},{3,19},{19,3},{4,20},{20... | collective-permute-start | bytes 2359304 | tf_op jit(solution)/shard_map/ppermute | solution.py:13
  48.2 285.5 %copy-start.129 = (s32[4,196]{1,0:T(4,128)S(1)}, s32[4,196]{1,0:T(4,128)}, u32[]{:S(2)}) copy-start(s32[4,196]{1,0:T(4,128)} %param.33) | copy-start | bytes 9412
  48.3 285.5 %copy-start.84 = (bf16[4,256,384]{2,0,1:T(4,128)(2,1)}, bf16[4,256,384]{2,0,1:T(4,128)(2,1)S(1)}, u32[]{:S(2)}) copy-start(bf16[4,256,384]{2,0,1:T(4,128)(2,1)S(1)} %collective-permute-done) | copy-start | bytes 2359300
  362.6 13.6 copy-start.33
  380.9 2.9 collective-permute-start.1
  417.7 13.6 copy-start.36
  452.7 104.1 %copy-start.66 = (bf16[2,128,768]{2,0,1:T(2,128)(2,1)}, bf16[2,128,768]{2,0,1:T(2,128)(2,1)S(1)}, u32[]{:S(2)}) copy-start(bf16[2,128,768]{2,0,1:T(2,128)(2,1)S(1)} %get-tuple-element.741) | copy-start | bytes 1179652
  457.7 99.0 %collective-permute-start.2 = (bf16[2,196,1536]{2,0,1:T(2,128)(2,1)}, bf16[2,196,1536]{2,0,1:T(2,128)(2,1)S(1)}, u32[]{:S(2)}, u32[]{:S(2)}) collective-permute-start(bf16[2,196,1536]{2,0,1:T(2,128)(2,1)} %copy.577), channel_id=1, source_target_pairs={{0,16},{16,0},{1,17},{17,1},{2,18},{18,2},{3,19},{19,3},{4,20},{20... | collective-permute-start | bytes 3612680 | tf_op jit(solution)/shard_map/ppermute | solution.py:13
  603.1 19.0 %slice-start.18 = ((s8[4718592]{0:T(1024)(128)(4,1)}), s8[4194304]{0:T(1024)(128)(4,1)S(1)}, s32[]{:S(2)}) async-start(s8[4718592]{0:T(1024)(128)(4,1)} %bitcast.630), calls=%async_computation.36 | async-start | bytes 8388608 | tf_op jit(solution)/shard_map/cond
  604.2 17.9 %slice-start.19 = ((s8[4718592]{0:T(1024)(128)(4,1)}), s8[524288]{0:T(1024)(128)(4,1)S(1)}, s32[]{:S(2)}) async-start(s8[4718592]{0:T(1024)(128)(4,1)} %bitcast.630), calls=%async_computation.37 | async-start | bytes 1048576 | tf_op jit(solution)/shard_map/cond
  722.0 3.8 collective-permute-start.3
  752.9 12.4 copy-start.195
  776.1 19.8 %slice-start.20 = ((s8[4718592]{0:T(1024)(128)(4,1)}), s8[4194304]{0:T(1024)(128)(4,1)S(1)}, s32[]{:S(2)}) async-start(s8[4718592]{0:T(1024)(128)(4,1)} %bitcast.632), calls=%async_computation.38 | async-start | bytes 8388608 | tf_op jit(solution)/shard_map/cond
  776.9 36.6 %copy-start.22 = (f32[2,196,768]{2,1,0:T(8,128)}, f32[2,196,768]{2,1,0:T(8,128)S(1)}, u32[]{:S(2)}) copy-start(f32[2,196,768]{2,1,0:T(8,128)S(1)} %get-tuple-element.909) | copy-start | bytes 3612676 | tf_op jit(solution)/shard_map/cond
  776.9 36.5 %copy-start.153 = (f32[2,196]{1,0:T(2,128)}, f32[2,196]{1,0:T(2,128)S(1)}, u32[]{:S(2)}) copy-start(f32[2,196]{1,0:T(2,128)S(1)} %broadcast_multiply_fusion.16) | copy-start | bytes 4708 | tf_op jit(solution)/shard_map/cond
  777.2 36.2 %copy-start.187 = (f32[2,196]{1,0:T(2,128)}, f32[2,196]{1,0:T(2,128)S(1)}, u32[]{:S(2)}) copy-start(f32[2,196]{1,0:T(2,128)S(1)} %fusion.587) | copy-start | bytes 4708 | tf_op jit(solution)/shard_map/cond
  777.2 18.7 %slice-start.21 = ((s8[4718592]{0:T(1024)(128)(4,1)}), s8[524288]{0:T(1024)(128)(4,1)S(1)}, s32[]{:S(2)}) async-start(s8[4718592]{0:T(1024)(128)(4,1)} %bitcast.632), calls=%async_computation.39 | async-start | bytes 1048576 | tf_op jit(solution)/shard_map/cond
  801.0 13.0 copy-start.26
  888.6 135.3 %reduce-scatter.13.cloned.1.call-start = ((), (), s32[]{:S(2)}) async-start(), calls=%async_computation.13 | async-start | bytes 2654208 | tf_op jit(solution)/shard_map/reduce_scatter | solution.py:381
  896.5 209.8 %reduce-scatter.9.cloned.1.call-start = ((), (), s32[]{:S(2)}) async-start(), calls=%async_computation.11 | async-start | bytes 3981312 | tf_op jit(solution)/shard_map/reduce_scatter | solution.py:375
  906.6 298.6 %reduce-scatter.17.cloned.1.call-start = ((), (), s32[]{:S(2)}) async-start(), calls=%async_computation.15 | async-start | bytes 5308416 | tf_op jit(solution)/shard_map/reduce_scatter | solution.py:387
  918.9 385.2 %reduce-scatter.15.cloned.1.call-start = ((), (), s32[]{:S(2)}) async-start(), calls=%async_computation.14 | async-start | bytes 5308416 | tf_op jit(solution)/shard_map/reduce_scatter | solution.py:384
  931.3 372.9 %copy-start.67 = (bf16[2,128,768]{2,0,1:T(2,128)(2,1)S(1)}, bf16[2,128,768]{2,0,1:T(2,128)(2,1)}, u32[]{:S(2)}) copy-start(bf16[2,128,768]{2,0,1:T(2,128)(2,1)} %copy-done.66) | copy-start | bytes 1179652
  931.3 438.3 %reduce-scatter.19.cloned.1.call-start = ((), (), s32[]{:S(2)}) async-start(), calls=%async_computation.16 | async-start | bytes 221184
  935.0 498.3 %all-reduce.5.cloned.1.call-start = ((), (), s32[]{:S(2)}) async-start(), calls=%async_computation.17 | async-start | bytes 4128768 | tf_op jit(solution)/shard_map/psum | solution.py:394
  1309.4 66.7 %collective-permute-start.4 = (bf16[4,256,384]{2,0,1:T(4,128)(2,1)S(1)}, bf16[4,256,384]{2,0,1:T(4,128)(2,1)S(1)}, u32[]{:S(2)}, u32[]{:S(2)}) collective-permute-start(bf16[4,256,384]{2,0,1:T(4,128)(2,1)S(1)} %maximum_select_fusion.1), channel_id=1, source_target_pairs={{0,16},{16,0},{1,17},{17,1},{2,18},{18,2},{3,19},{19,3},{4,20},{20... | collective-permute-start | bytes 2359304 | tf_op jit(solution)/shard_map/ppermute | solution.py:13
  (94 other events, 361.3 us)
Sparse Core Ops, SparseCore 0:
  10.2 45.6 all-gather.7
  58.0 50.4 all-gather.9
  110.7 63.1 all-gather.5
  175.9 78.0 all-gather.11
  256.1 77.6 all-gather.13
  888.7 63.0 reduce-scatter.10
  955.3 68.5 reduce-scatter.12
  1027.5 78.6 reduce-scatter.8
  1109.9 95.2 reduce-scatter.16
  1208.7 95.3 reduce-scatter.14
  1307.9 61.6 reduce-scatter.18
  1372.0 61.2 all-reduce.4
where the time goes:
time: 1450 us
  waiting for transfers between devices  772 us (53%)
  matrix products  205 us (14%)
  other arithmetic  165 us (11%)
  local copies, waits for them, and re-layouts  138 us (10%)
  starting transfers between devices  98.5 us (7%)
  blocking collectives  38.4 us (3%)
  loops' own time  16.7 us (1%)
  between operations  14.7 us (1%)
    reduce_scatter x1, waiting for transfers between devices, local(): lax.psum_scatter(terms[4].astype(jnp.bfloat16), 'dp', scatter_dimension=1...  99 us
    reduce_scatter x1, waiting for transfers between devices, local(): lax.psum_scatter(terms[3].astype(jnp.bfloat16), 'dp', scatter_dimension=1...  98.9 us
    ppermute x5, starting transfers between devices, partner(): return lax.ppermute(value, axis, pairs)  98 us
    reduce_scatter x1, waiting for transfers between devices, local(): lax.psum_scatter(terms[0].astype(jnp.bfloat16), 'dp', scatter_dimension=1...  82.4 us
    all_gather x1, waiting for transfers between devices, local(): lax.all_gather(widening, 'dp', axis=1, tiled=True)  80.1 us
    all_gather x1, waiting for transfers between devices, local(): lax.all_gather(narrowing, 'dp', axis=1, tiled=True)  79.7 us
    reduce_scatter x1, waiting for transfers between devices, local(): lax.psum_scatter(terms[2].astype(jnp.bfloat16), 'dp', scatter_dimension=1...  72.1 us
    dot_general x18, matrix products, project(): jnp.einsum('bsd,de->bse', acts, weight, preferred_element_type=jnp.float32)  71.6 us
  transfers between devices with their start and end apart: 17, of which 15 were waited for; matrix products, arithmetic and copies ran while one was open for 5% of the time, Pallas kernels for 0%

commit v1 on v0

--- a/solution.py
+++ b/solution.py
@@ -4,17 +4,12 @@
 from jax.sharding import PartitionSpec as P
 
 HEADS = 12
-MICRO = 2
 
 
 def partner(value, axis, distance):
     mask = 2**distance
     pairs = [(source, source ^ mask) for source in range(lax.axis_size(axis))]
     return lax.ppermute(value, axis, pairs)
-
-
-def as_sent(value):
-    return jax.tree.map(lambda a: a.astype(jnp.bfloat16) if a.dtype == jnp.float32 else a, value)
 
 
 def to_low(values):
@@ -165,10 +160,9 @@
     return (memory, saved)
 
 
-def encoder_backward(states, keep, weights, grad_memory):
+def encoder_backward(states, saved, weights, grad_memory):
     w_in, w_out, w_pair, w_up, w_down, gains = weights
     gains = gains.astype(jnp.float32)
-    _, saved = encoder_pass(states, keep, weights)
     (
         mask,
         first,
@@ -277,6 +271,45 @@
     )
 
 
+def to_whole_images(values, section):
+    half = values.shape[0] // 2
+    low_part, high_part = values[:half], values[half:]
+    incoming = partner(jnp.where(section == 0, high_part, low_part), "section", 0)
+    kept = jnp.where(section == 0, low_part, high_part)
+    left = jnp.where(section == 0, kept, incoming)
+    right = jnp.where(section == 0, incoming, kept)
+    return jnp.concatenate([left, right], axis=-1)
+
+
+def to_half_features(values, section):
+    half = values.shape[-1] // 2
+    left, right = values[..., :half], values[..., half:]
+    incoming = partner(jnp.where(section == 0, right, left), "section", 0)
+    kept = jnp.where(section == 0, left, right)
+    low_part = jnp.where(section == 0, kept, incoming)
+    high_part = jnp.where(section == 0, incoming, kept)
+    return jnp.concatenate([low_part, high_part], axis=0)
+
+
+def gather_blocks(piece, dimension):
+    sections = lax.axis_size("section")
+    shards = lax.axis_size("dp")
+    whole = lax.all_gather(piece[0], ("section", "dp"), axis=0, tiled=False)
+    if dimension == 0:
+        return whole.reshape(sections, shards * piece.shape[1], piece.shape[2])
+    whole = whole.reshape(sections, shards, piece.shape[1], piece.shape[2])
+    return whole.transpose(0, 2, 1, 3).reshape(sections, piece.shape[1], -1)
+
+
+def reduce_blocks(first, second, section, dimension):
+    first, second = to_low(first), to_low(second)
+    incoming = partner(jnp.where(section == 0, second, first), "section", 0)
+    kept = jnp.where(section == 0, first, second)
+    total = to_low(kept.astype(jnp.float32) + incoming.astype(jnp.float32))
+    share = lax.psum_scatter(total, "dp", scatter_dimension=dimension, tiled=True)
+    return lax.psum(share, "rep").astype(jnp.float32)[None]
+
+
 def local(
     patches,
     captions,
@@ -291,127 +324,47 @@
     cotangent,
 ):
     section = lax.axis_index("section")
-    on_encoder = section == 0
-    images, count, half = patches.shape
+    count = patches.shape[1]
     length = captions.shape[1]
-    width = 2 * half
-    spare = 2 * length - count
-    text_pair = jnp.concatenate([captions, cotangent], axis=1)
-    padded = jnp.pad(patches, ((0, 0), (0, spare), (0, 0)))
-    incoming = partner(jnp.where(on_encoder, text_pair, padded), "section", 0)
-    full_patches = jnp.concatenate([patches, incoming[:, :count]], axis=2).astype(jnp.float32)
-    full_text = jnp.concatenate([incoming[:, :length], captions], axis=2).astype(jnp.float32)
-    full_cotan = jnp.concatenate([incoming[:, length:], cotangent], axis=2).astype(jnp.float32)
-    gathered = (
-        lax.all_gather(mixing, "dp", axis=1, tiled=True),
-        lax.all_gather(merging, "dp", axis=1, tiled=True),
-        lax.all_gather(crossing, "dp", axis=1, tiled=True),
-        lax.all_gather(widening, "dp", axis=1, tiled=True),
-        lax.all_gather(narrowing, "dp", axis=1, tiled=True),
-        lax.all_gather(scales, "dp", axis=2, tiled=True),
-    )
-    weights = tuple((piece[0] for piece in gathered))
-    per_micro = images // MICRO
-    zero_grads = tuple((jnp.zeros(piece.shape, jnp.float32) for piece in weights))
-    zero_send = jnp.zeros((per_micro, count, 2 * width), jnp.bfloat16)
-    zero_patch = jnp.zeros((per_micro, count, width), jnp.float32)
-    zero_text = jnp.zeros((per_micro, length, width), jnp.float32)
-    totals = zero_grads
-    patch_grads = jnp.zeros((images, count, width), jnp.float32)
-    decoded_all = jnp.zeros((images, length, width), jnp.float32)
-    caption_all = jnp.zeros((images, length, width), jnp.float32)
-    received = zero_send
-    for tick in range(MICRO + 2):
-
-        def encoder_branch(tick=tick, received=received):
-            send, grads, patch_part = (zero_send, zero_grads, zero_patch)
-            if tick >= 2:
-                start = (tick - 2) * per_micro
-                patch_part, grads = encoder_backward(
-                    full_patches[start : start + per_micro],
-                    tissue_keep[start : start + per_micro],
-                    weights,
-                    received,
-                )
-            if tick < MICRO:
-                start = tick * per_micro
-                send = encoder_pass(
-                    full_patches[start : start + per_micro],
-                    tissue_keep[start : start + per_micro],
-                    weights,
-                )[0]
-            return (send, grads, patch_part, zero_text, zero_text)
-
-        def decoder_branch(tick=tick, received=received):
-            if 1 <= tick <= MICRO:
-                start = (tick - 1) * per_micro
-                stop = start + per_micro
-                output, grad_text, grad_memory, grads = decoder_step(
-                    full_text[start:stop],
-                    caption_mask[start:stop],
-                    received,
-                    tissue_keep[start:stop],
-                    weights,
-                    full_cotan[start:stop],
-                )
-                return (grad_memory, grads, zero_patch, output, grad_text)
-            return (zero_send, zero_grads, zero_patch, zero_text, zero_text)
-
-        send, grads, patch_part, out_part, text_part = lax.cond(
-            on_encoder, encoder_branch, decoder_branch
+    gathered = tuple(
+        gather_blocks(piece, dimension)
+        for piece, dimension in (
+            (mixing, 0),
+            (merging, 0),
+            (crossing, 0),
+            (widening, 0),
+            (narrowing, 0),
+            (scales, 1),
         )
-        totals = tuple((total + grad for total, grad in zip(totals, grads)))
-        if tick >= 2:
-            start = (tick - 2) * per_micro
-            patch_grads = patch_grads.at[start : start + per_micro].add(patch_part)
-        if 1 <= tick <= MICRO:
-            start = (tick - 1) * per_micro
-            decoded_all = decoded_all.at[start : start + per_micro].add(out_part)
-            caption_all = caption_all.at[start : start + per_micro].add(text_part)
-        if tick <= MICRO:
-            received = partner(send, "section", 0)
-    terms = tuple((total[None] for total in totals))
-    shares = (
-        lax.psum_scatter(
-            terms[0].astype(jnp.bfloat16), "dp", scatter_dimension=1, tiled=True
-        ).astype(jnp.float32),
-        lax.psum_scatter(
-            terms[1].astype(jnp.bfloat16), "dp", scatter_dimension=1, tiled=True
-        ).astype(jnp.float32),
-        lax.psum_scatter(
-            terms[2].astype(jnp.bfloat16), "dp", scatter_dimension=1, tiled=True
-        ).astype(jnp.float32),
-        lax.psum_scatter(
-            terms[3].astype(jnp.bfloat16), "dp", scatter_dimension=1, tiled=True
-        ).astype(jnp.float32),
-        lax.psum_scatter(
-            terms[4].astype(jnp.bfloat16), "dp", scatter_dimension=1, tiled=True
-        ).astype(jnp.float32),
-        lax.psum_scatter(
-            terms[5].astype(jnp.bfloat16), "dp", scatter_dimension=2, tiled=True
-        ).astype(jnp.float32),
-    )
-    summed = jax.tree.map(lambda part: part.astype(jnp.float32), lax.psum(as_sent(shares), "rep"))
-    low_patch = to_low(patch_grads)
-    low_decoded = to_low(decoded_all)
-    low_caption = to_low(caption_all)
-    encoder_send = jnp.pad(low_patch[:, :, half:], ((0, 0), (0, spare), (0, 0)))
-    decoder_send = jnp.concatenate([low_decoded[:, :, :half], low_caption[:, :, :half]], axis=1)
-    returned = partner(jnp.where(on_encoder, encoder_send, decoder_send), "section", 0)
-    patch_out = jnp.where(on_encoder, low_patch[:, :, :half], returned[:, :count])
-    decoded = jnp.where(on_encoder, returned[:, :length], low_decoded[:, :, half:])
-    caption_out = jnp.where(on_encoder, returned[:, length:], low_caption[:, :, half:])
+    )
+    enc_weights = tuple(piece[0] for piece in gathered)
+    dec_weights = tuple(piece[1] for piece in gathered)
+    states = to_whole_images(jnp.concatenate([patches, captions, cotangent], axis=1), section)
+    states = states.astype(jnp.float32)
+    own_patches = states[:, :count]
+    own_text = states[:, count : count + length]
+    own_cotan = states[:, count + length :]
+    own = own_patches.shape[0]
+    keep = lax.dynamic_slice_in_dim(tissue_keep, section * own, own, 0)
+    text_keep = lax.dynamic_slice_in_dim(caption_mask, section * own, own, 0)
+    memory, saved = encoder_pass(own_patches, keep, enc_weights)
+    output, grad_text, grad_memory, dec_grads = decoder_step(
+        own_text, text_keep, memory, keep, dec_weights, own_cotan
+    )
+    grad_patches, enc_grads = encoder_backward(own_patches, saved, enc_weights, grad_memory)
+    results = to_half_features(
+        jnp.concatenate([to_low(grad_patches), to_low(output), to_low(grad_text)], axis=1),
+        section,
+    )
+    summed = tuple(
+        reduce_blocks(first, second, section, dimension)
+        for first, second, dimension in zip(enc_grads, dec_grads, (0, 0, 0, 0, 0, 1))
+    )
     return (
-        decoded,
-        caption_out,
-        patch_out,
-        summed[0],
-        summed[1],
-        summed[2],
-        summed[3],
-        summed[4],
-        summed[5],
-    )
+        results[:, count : count + length],
+        results[:, count + length :],
+        results[:, :count],
+    ) + summed
 
 
 def solution(mesh):

time: 1450 us -> 1050 us (0.72)
  waiting for transfers between devices: 772 us -> 648 us
  starting transfers between devices: 98.5 us -> 7.57 us
  other arithmetic: 165 us -> 97 us
  matrix products: 205 us -> 140 us
  local copies, waits for them, and re-layouts: 138 us -> 97.1 us
  loops' own time: 16.7 us -> 0 us
    ppermute x5 -> x8, starting transfers between devices: 98 us -> 6.3 us  [partner(): return lax.ppermute(value, axis, pairs)]
    all_gather x5, waiting for transfers between devices: 283 us -> 198 us  [gather_blocks(): whole = lax.all_gather(piece[0], ('section', 'dp'), axis=0, tiled=False)]
    reduce_scatter x5, waiting for transfers between devices: 369 us -> 309 us  [reduce_blocks(): lax.psum_scatter(total, 'dp', scatter_dimension=dimension, tiled=True)]
    convert_element_type x14 -> x0, other arithmetic: 59.3 us -> none  [the longest x1 12.3 us: local(): terms[3].astype(jnp.bfloat16)]
    dot_general x18 -> x11, matrix products: 71.6 us -> 24.1 us  [project(): jnp.einsum('bsd,de->bse', acts, weight, preferred_element_type=jnp.float32)]
    slice x6 -> x9, local copies, waits for them, and re-layouts: 1.2 us -> 34.1 us  [the longest x3 15.2 us: local(): enc_weights = tuple((piece[0] for piece in gathered))]
    broadcast_in_dim x11 -> x0, local copies, waits for them, and re-layouts: 21.6 us -> none  [the longest x6 17.3 us: local(): jnp.zeros(piece.shape, jnp.float32)]
    convert_element_type x6 -> x13, other arithmetic: 34.8 us -> 54.8 us  [to_low(): return values.astype(jnp.bfloat16)]
  transfers between devices with their start and end apart: 17 -> 20, of which waited for: 15 -> 14; matrix products, arithmetic and copies ran while one was open for 5% -> 19% of each run, Pallas kernels for 0% -> 0%
where the time goes in v1:
time: 1050 us; the launch traced here: 1040 us
  waiting for transfers between devices  648 us (62%)
  matrix products  140 us (13%)
  local copies, waits for them, and re-layouts  97.1 us (9%)
  other arithmetic  97 us (9%)
  blocking collectives  39.3 us (4%)
  between operations  16.3 us (2%)
    reduce_scatter x5, waiting for transfers between devices, reduce_blocks(): lax.psum_scatter(total, 'dp', scatter_dimension=dimension, tiled=True)  309 us
    all_gather x5, waiting for transfers between devices, gather_blocks(): whole = lax.all_gather(piece[0], ('section', 'dp'), axis=0, tiled=False)  198 us
    unnamed x13, waiting for transfers between devices  65.2 us
    psum x1, waiting for transfers between devices, reduce_blocks(): return lax.psum(share, 'rep').astype(jnp.float32)[None]  55.1 us
    convert_element_type x13, other arithmetic, to_low(): return values.astype(jnp.bfloat16)  54.8 us
    all_gather x1, blocking collectives, gather_blocks(): whole = lax.all_gather(piece[0], ('section', 'dp'), axis=0, tiled=False)  34.4 us
    dot_general x11, matrix products, back_project(): jnp.einsum('bse,de->bsd', grads, weight, preferred_element_type=jnp.float32)  31.4 us
    dot_general x11, matrix products, weight_grad(): jnp.einsum('bsd,bse->de', acts, grads, preferred_element_type=jnp.float32)  31 us
  transfers between devices with their start and end apart: 20, of which 14 were waited for; matrix products, arithmetic and copies ran while one was open for 19% of the time, Pallas kernels for 0%

profile of v1, /device:TPU:0, one launch (start us, length us, event | category | flops | bytes accessed | tf_op | source)
XLA Modules:
  0.0 1044.9 jit_solution(11736521416284548077)
XLA Ops:
  12.8 34.4 %all_gather.18 = bf16[16,3,96]{2,1,0:T(4,128)(2,1)S(1)} all-gather(bf16[1,3,96]{2,1,0:T(4,128)(2,1)S(1)} %copy-done.129), channel_id=1, replica_groups=mesh['section'=2,'dp'=8,'rep'=2] {'section','dp'}, dimensions={0}, use_global_device_ids=true | all-gather | bytes 9792 | tf_op jit(solution)/shard_map/all_gather | solution.py:297
  50.3 5.1 all-gather.8.cloned.1.call-done
  58.1 51.3 %all-gather.10.cloned.1.call-done = bf16[16,96,1536]{2,1,0:T(8,128)(2,1)} async-done(((bf16[1,96,1536]{2,1,0:T(8,128)(2,1)}), bf16[16,96,1536]{2,1,0:T(8,128)(2,1)}) %all-gather.10.cloned.1.call-update) | async-done | bytes 4718608 | tf_op jit(solution)/shard_map/all_gather | solution.py:297
  114.4 61.9 %all-gather.6.cloned.1.call-done = bf16[16,96,2304]{2,1,0:T(8,128)(2,1)} async-done(((bf16[1,96,2304]{2,1,0:T(8,128)(2,1)}), bf16[16,96,2304]{2,1,0:T(8,128)(2,1)}) %all-gather.6.cloned.1.call-update) | async-done | bytes 7077904 | tf_op jit(solution)/shard_map/all_gather | solution.py:297
  176.3 5.4 fusion.173
  203.9 9.8 copy.178
  213.7 12.4 %fusion.180 = (f32[2,12,196]{0,2,1:T(8,128)S(1)}, f32[2,12,196,196]{3,0,2,1:T(2,128)S(1)}) fusion(f32[2,12,196,196]{3,0,2,1:T(2,128)} %copy.178, pred[2,196]{1,0:T(4,128)(4,1)S(1)} %dynamic-slice_compare_fusion), kind=kOutput, calls=%fused_computation.316 | output fusion | flops 3688131 | bytes 7395080 | tf_op jit(solution)/shard_map/sub | solution.py:53
  226.1 5.1 fusion.170
  234.8 23.3 %all-gather.12.cloned.1.call-done = bf16[16,96,3072]{2,1,0:T(8,128)(2,1)} async-done(((bf16[1,96,3072]{2,1,0:T(8,128)(2,1)}), bf16[16,96,3072]{2,1,0:T(8,128)(2,1)}) %all-gather.12.cloned.1.call-update) | async-done | bytes 9437200 | tf_op jit(solution)/shard_map/all_gather | solution.py:297
  258.1 7.0 fusion.172
  270.6 12.4 %multiply_convert_fusion = (bf16[2,196,3072]{2,1,0:T(8,128)(2,1)}, f32[2,196,3072]{2,1,0:T(8,128)}) fusion(f32[2,196,3072]{2,1,0:T(8,128)S(1)} %get-tuple-element.120, u8[196,3072]{1,0:T(8,128)(4,1)S(1)} %get-tuple-element.46, u8[196,3072]{1,0:T(8,128)(4,1)S(1)} %get-tuple-element.45), kind=kLoop, calls=%fused_computation.23 | loop fusion | flops 84295680 | bytes 13246464 | tf_op jit(solution)/shard_map/convert_element_type | solution.py:16
  283.1 56.4 %all-gather.14.cloned.1.call-done = bf16[16,384,768]{2,1,0:T(8,128)(2,1)} async-done(((bf16[1,384,768]{2,1,0:T(8,128)(2,1)}), bf16[16,384,768]{2,1,0:T(8,128)(2,1)}) %all-gather.14.cloned.1.call-update) | async-done | bytes 9437200 | tf_op jit(solution)/shard_map/all_gather | solution.py:297
  339.5 8.3 fusion.171
  367.2 5.1 fusion.118
  372.3 8.3 multiply_convert_fusion.1
  396.0 5.9 fusion.81
  401.9 5.8 multiply_convert_fusion.4
  421.8 8.6 add_convert_fusion.3
  458.1 9.6 copy.189
  467.8 12.9 %select_convert_fusion = bf16[2,12,196,196]{3,0,2,1:T(2,128)(2,1)} fusion(f32[2,12,196,196]{3,0,2,1:T(2,128)} %get-tuple-element.83, f32[2,12,196,196]{3,0,2,1:T(2,128)} %copy.189, pred[2,196]{1,0:T(4,128)(4,1)S(1)} %dynamic-slice_compare_fusion), kind=kOutput, calls=%fused_computation.36 | output fusion | flops 4614819 | bytes 9220232 | tf_op jit(solution)/shard_map/sub | solution.py:69
  504.6 5.4 bitcast_convert_fusion.5
  518.8 5.8 collective-permute-done.2
  536.2 7.5 collective-permute-done.5
  545.9 7.7 add_convert_fusion.1
  561.3 7.5 collective-permute-done.6
  571.1 6.7 add_convert_fusion
  592.2 28.5 %reduce-scatter.13.cloned.1.call-done = bf16[96,1536]{1,0:T(8,128)(2,1)} async-done(((bf16[768,1536]{1,0:T(8,128)(2,1)}), bf16[96,1536]{1,0:T(8,128)(2,1)}) %reduce-scatter.13.cloned.1.call-update) | async-done | bytes 294928 | tf_op jit(solution)/shard_map/reduce_scatter | solution.py:309
  620.7 82.3 %reduce-scatter.9.cloned.1.call-done = bf16[96,2304]{1,0:T(8,128)(2,1)} async-done(((bf16[768,2304]{1,0:T(8,128)(2,1)}), bf16[96,2304]{1,0:T(8,128)(2,1)}) %reduce-scatter.9.cloned.1.call-update) | async-done | bytes 442384 | tf_op jit(solution)/shard_map/reduce_scatter | solution.py:309
  703.0 99.0 %reduce-scatter.15.cloned.1.call-done = bf16[96,3072]{1,0:T(8,128)(2,1)} async-done(((bf16[768,3072]{1,0:T(8,128)(2,1)}), bf16[96,3072]{1,0:T(8,128)(2,1)}) %reduce-scatter.15.cloned.1.call-update) | async-done | bytes 589840 | tf_op jit(solution)/shard_map/reduce_scatter | solution.py:309
  802.0 98.8 %reduce-scatter.17.cloned.1.call-done = bf16[384,768]{1,0:T(8,128)(2,1)} async-done(((bf16[3072,768]{1,0:T(8,128)(2,1)}), bf16[384,768]{1,0:T(8,128)(2,1)}) %reduce-scatter.17.cloned.1.call-update) | async-done | bytes 589840 | tf_op jit(solution)/shard_map/reduce_scatter | solution.py:309
  903.8 62.5 %reduce-scatter.19.cloned.1.call-done = bf16[96,3]{1,0:T(8,128)(2,1)} async-done(((bf16[768,3]{1,0:T(8,128)(2,1)}), bf16[96,3]{1,0:T(8,128)(2,1)}) %reduce-scatter.19.cloned.1.call-update) | async-done | bytes 592
  975.0 55.1 %all-reduce.3.cloned.1.call-done = (bf16[1,96,2304]{2,1,0:T(8,128)(2,1)}, bf16[1,96,768]{2,1,0:T(8,128)(2,1)}, bf16[1,96,1536]{2,1,0:T(8,128)(2,1)}, bf16[1,96,3072]{2,1,0:T(8,128)(2,1)}, bf16[1,384,768]{2,1,0:T(8,128)(2,1)}) async-done(((bf16[1,96,2304]{2,1,0:T(8,128)(2,1)}, bf16[1,96,768]{2,1,0:T(8,128)(2,1)}, bf16[1,96,1536]{2,1,0:T(8,128)(2,1)}, bf16[1,96,3072]{2,1,0:T(8,128)(2,1)}, ...) | async-done | bytes 2064400 | tf_op jit(solution)/shard_map/psum | solution.py:310
  (491 shorter events, 212.7 us)
Async XLA Ops:
  7.2 48.1 %all-gather.8.cloned.1.call-start = ((), (), s32[]{:S(2)}) async-start(), calls=%async_computation.7 | async-start | bytes 2506752 | tf_op jit(solution)/shard_map/all_gather | solution.py:297
  7.9 101.5 %all-gather.10.cloned.1.call-start = ((), (), s32[]{:S(2)}) async-start(), calls=%async_computation.8 | async-start | bytes 5013504 | tf_op jit(solution)/shard_map/all_gather | solution.py:297
  8.7 167.6 %all-gather.6.cloned.1.call-start = ((), (), s32[]{:S(2)}) async-start(), calls=%async_computation.6 | async-start | bytes 7520256 | tf_op jit(solution)/shard_map/all_gather | solution.py:297
  9.4 248.6 %all-gather.12.cloned.1.call-start = ((), (), s32[]{:S(2)}) async-start(), calls=%async_computation.9 | async-start | bytes 10027008 | tf_op jit(solution)/shard_map/all_gather | solution.py:297
  10.0 329.5 %all-gather.14.cloned.1.call-start = ((), (), s32[]{:S(2)}) async-start(), calls=%async_computation.10 | async-start | bytes 10027008 | tf_op jit(solution)/shard_map/all_gather | solution.py:297
  12.1 35.8 %collective-permute-start = (bf16[2,452,384]{2,0,1:T(2,128)(2,1)S(1)}, bf16[2,452,384]{2,0,1:T(2,128)(2,1)S(1)}, u32[]{:S(2)}, u32[]{:S(2)}) collective-permute-start(bf16[2,452,384]{2,0,1:T(2,128)(2,1)S(1)} %copy.166), channel_id=1, source_target_pairs={{0,16},{16,0},{1,17},{17,1},{2,18},{18,2},{3,19},{19,3},{4,20},{20... | collective-permute-start | bytes 2082824 | tf_op jit(solution)/shard_map/ppermute | solution.py:12
  12.7 579.5 %reduce-scatter.11.cloned.1.call-start = ((), (), s32[]{:S(2)}) async-start(), calls=%async_computation.12 | async-start | bytes 1327104 | tf_op jit(solution)/shard_map/reduce_scatter | solution.py:309
  47.5 134.2 %copy-start.96 = (f32[768]{0:T(1024)}, f32[768]{0:T(1024)S(1)}, u32[]{:S(2)}) copy-start(f32[768]{0:T(1024)S(1)} %mul.501) | copy-start | bytes 9220
  47.6 385.7 %copy-start.112 = (f32[768]{0:T(1024)}, f32[768]{0:T(1024)S(1)}, u32[]{:S(2)}) copy-start(f32[768]{0:T(1024)S(1)} %mul.524) | copy-start | bytes 9220
  47.9 137.1 %copy-start.98 = (pred[2,128,128]{1,2,0:T(8,128)(4,1)}, pred[2,128,128]{1,2,0:T(8,128)(4,1)S(1)}, u32[]{:S(2)}) copy-start(pred[2,128,128]{1,2,0:T(8,128)(4,1)S(1)} %broadcast_and_fusion) | copy-start | bytes 98308
  49.2 140.7 %copy-start.17 = (bf16[2,128,768]{2,1,0:T(8,128)(2,1)}, bf16[2,128,768]{2,1,0:T(8,128)(2,1)S(1)}, u32[]{:S(2)}) copy-start(bf16[2,128,768]{2,1,0:T(8,128)(2,1)S(1)} %get-tuple-element.87) | copy-start | bytes 1179652
  49.3 143.7 %copy-start.12 = (bf16[2,196,768]{2,1,0:T(8,128)(2,1)}, bf16[2,196,768]{2,1,0:T(8,128)(2,1)S(1)}, u32[]{:S(2)}) copy-start(bf16[2,196,768]{2,1,0:T(8,128)(2,1)S(1)} %get-tuple-element.85) | copy-start | bytes 1806340
  50.2 142.8 %copy-start.102 = (f32[2,196]{1,0:T(2,128)}, f32[2,196]{1,0:T(2,128)S(1)}, u32[]{:S(2)}) copy-start(f32[2,196]{1,0:T(2,128)S(1)} %fusion.142) | copy-start | bytes 4708
  233.5 199.9 %copy-start.104 = (f32[2,196]{1,0:T(2,128)}, f32[2,196]{1,0:T(2,128)S(1)}, u32[]{:S(2)}) copy-start(f32[2,196]{1,0:T(2,128)S(1)} %broadcast_multiply_fusion.1) | copy-start | bytes 4708
  234.8 198.5 %copy-start.123 = (f32[2,196]{1,0:T(2,128)}, f32[2,196]{1,0:T(2,128)S(1)}, u32[]{:S(2)}) copy-start(f32[2,196]{1,0:T(2,128)S(1)} %fusion.143) | copy-start | bytes 4708
  451.6 29.7 %collective-permute-start.3 = (bf16[768,768]{1,0:T(8,128)(2,1)}, bf16[768,768]{1,0:T(8,128)(2,1)S(1)}, u32[]{:S(2)}, u32[]{:S(2)}) collective-permute-start(bf16[768,768]{1,0:T(8,128)(2,1)} %get-tuple-element.141), channel_id=1, source_target_pairs={{0,16},{16,0},{1,17},{17,1},{2,18},{18,2},{3,19},{19,3},{4,20},{20... | collective-permute-start | bytes 3538952 | tf_op jit(solution)/shard_map/ppermute | solution.py:12
  458.1 51.9 %collective-permute-start.4 = (bf16[768,1536]{1,0:T(8,128)(2,1)}, bf16[768,1536]{1,0:T(8,128)(2,1)}, u32[]{:S(2)}, u32[]{:S(2)}) collective-permute-start(bf16[768,1536]{1,0:T(8,128)(2,1)} %get-tuple-element.143), channel_id=1, source_target_pairs={{0,16},{16,0},{1,17},{17,1},{2,18},{18,2},{3,19},{19,3},{4,20},{20... | collective-permute-start | bytes 7077896 | tf_op jit(solution)/shard_map/ppermute | solution.py:12
  485.3 135.5 %reduce-scatter.13.cloned.1.call-start = ((), (), s32[]{:S(2)}) async-start(), calls=%async_computation.13 | async-start | bytes 2654208 | tf_op jit(solution)/shard_map/reduce_scatter | solution.py:309
  514.2 188.8 %reduce-scatter.9.cloned.1.call-start = ((), (), s32[]{:S(2)}) async-start(), calls=%async_computation.11 | async-start | bytes 3981312 | tf_op jit(solution)/shard_map/reduce_scatter | solution.py:309
  516.0 8.6 collective-permute-start.2
  527.9 274.1 %reduce-scatter.15.cloned.1.call-start = ((), (), s32[]{:S(2)}) async-start(), calls=%async_computation.14 | async-start | bytes 5308416 | tf_op jit(solution)/shard_map/reduce_scatter | solution.py:309
  535.7 8.0 collective-permute-start.5
  553.6 347.2 %reduce-scatter.17.cloned.1.call-start = ((), (), s32[]{:S(2)}) async-start(), calls=%async_computation.15 | async-start | bytes 5308416 | tf_op jit(solution)/shard_map/reduce_scatter | solution.py:309
  560.9 8.0 collective-permute-start.6
  577.8 388.4 %reduce-scatter.19.cloned.1.call-start = ((), (), s32[]{:S(2)}) async-start(), calls=%async_computation.16 | async-start | bytes 221184
  586.1 2.6 collective-permute-start.7
  588.6 312.2 %copy-start.7 = (f32[2,196,768]{2,1,0:T(8,128)S(1)}, f32[2,196,768]{2,1,0:T(8,128)}, u32[]{:S(2)}) copy-start(f32[2,196,768]{2,1,0:T(8,128)} %copy-done.5) | copy-start | bytes 3612676
  588.6 312.2 %copy-start.9 = (f32[2,196,768]{2,1,0:T(8,128)S(1)}, f32[2,196,768]{2,1,0:T(8,128)}, u32[]{:S(2)}) copy-start(f32[2,196,768]{2,1,0:T(8,128)} %copy-done.8) | copy-start | bytes 3612676
  588.6 312.2 %copy-start.101 = (f32[2,196]{1,0:T(2,128)S(1)}, f32[2,196]{1,0:T(2,128)}, u32[]{:S(2)}) copy-start(f32[2,196]{1,0:T(2,128)} %copy-done.100) | copy-start | bytes 4708
  589.6 440.5 %all-reduce.3.cloned.1.call-start = ((), (), s32[]{:S(2)}) async-start(), calls=%async_computation.17 | async-start | bytes 4128768 | tf_op jit(solution)/shard_map/psum | solution.py:310
  592.2 308.7 %copy-start.16 = (bf16[2,196,768]{2,1,0:T(8,128)(2,1)S(1)}, bf16[2,196,768]{2,1,0:T(8,128)(2,1)}, u32[]{:S(2)}) copy-start(bf16[2,196,768]{2,1,0:T(8,128)(2,1)} %copy-done.12) | copy-start | bytes 1806340
  903.7 68.9 %collective-permute-start.1 = (bf16[2,452,384]{2,0,1:T(2,128)(2,1)S(1)}, bf16[2,452,384]{2,0,1:T(2,128)(2,1)S(1)}, u32[]{:S(2)}, u32[]{:S(2)}) collective-permute-start(bf16[2,452,384]{2,0,1:T(2,128)(2,1)S(1)} %copy.204), channel_id=1, source_target_pairs={{0,16},{16,0},{1,17},{17,1},{2,18},{18,2},{3,19},{19,3},{4,20},{20... | collective-permute-start | bytes 2082824 | tf_op jit(solution)/shard_map/ppermute | solution.py:12
  (133 other events, 1086.5 us)
Sparse Core Ops, SparseCore 0:
  10.2 45.0 all-gather.7
  57.5 51.8 all-gather.9
  111.6 64.5 all-gather.5
  178.3 79.6 all-gather.11
  260.1 79.3 all-gather.13
  485.4 63.1 reduce-scatter.10
  552.1 68.5 reduce-scatter.12
  624.4 78.5 reduce-scatter.8
  706.7 95.2 reduce-scatter.14
  805.5 95.2 reduce-scatter.16
  904.6 61.6 reduce-scatter.18
  968.7 61.3 all-reduce.2

commit v2 on v1

--- a/solution.py
+++ b/solution.py
@@ -1,9 +1,14 @@
+import functools
+
 import jax
 import jax.numpy as jnp
 from jax import lax
+from jax.experimental import pallas as pl
+from jax.experimental.pallas import tpu as pltpu
 from jax.sharding import PartitionSpec as P
 
 HEADS = 12
+MESH_IDS = pl.DeviceIdType.MESH
 
 
 def partner(value, axis, distance):
@@ -301,13 +306,146 @@
     return whole.transpose(0, 2, 1, 3).reshape(sections, piece.shape[1], -1)
 
 
-def reduce_blocks(first, second, section, dimension):
+def ring_place(shard, size):
+    column = shard % 2
+    row = shard // 2
+    return row * (1 - column) + (size - 1 - row) * column
+
+
+def ring_shard(place, size):
+    column = place // (size // 2)
+    row = place * (1 - column) + (size - 1 - place) * column
+    return 2 * row + column
+
+
+def reduce_kernel(size, reps, kinds, *refs):
+    grads, outs = refs[:kinds], refs[kinds : 2 * kinds]
+    slots, sides = refs[2 * kinds : 3 * kinds], refs[3 * kinds : 4 * kinds]
+    send, recv, side_send, side_recv = refs[4 * kinds :]
+    place = ring_place(lax.axis_index("dp"), size)
+    replica = lax.axis_index("rep")
+    targets = (
+        ring_shard((place + 1) % size, size),
+        ring_shard((place + size - 1) % size, size),
+    )
+    signs = (-1, 1)
+
+    barrier = pltpu.get_barrier_semaphore()
+    for target in targets:
+        pl.semaphore_signal(barrier, inc=1, device_id={"dp": target}, device_id_type=MESH_IDS)
+    for other in range(1, reps):
+        pl.semaphore_signal(
+            barrier,
+            inc=1,
+            device_id={"rep": (replica + other) % reps},
+            device_id_type=MESH_IDS,
+        )
+    pl.semaphore_wait(barrier, 1 + reps)
+
+    def own(kind, way, step):
+        chunk = (place + signs[way] * (step + 1) + 2 * size) % size
+        return grads[kind].at[ring_shard(chunk, size), way]
+
+    def hop(kind, way, step, source):
+        return pltpu.make_async_remote_copy(
+            src_ref=source,
+            dst_ref=slots[kind].at[step, way],
+            send_sem=send.at[kind, way, step],
+            recv_sem=recv.at[kind, way, step],
+            device_id={"dp": targets[way]},
+            device_id_type=MESH_IDS,
+        )
+
+    def side(kind, other):
+        return pltpu.make_async_remote_copy(
+            src_ref=slots[kind].at[size - 2],
+            dst_ref=sides[kind].at[other - 1],
+            send_sem=side_send.at[kind, other - 1],
+            recv_sem=side_recv.at[kind, other - 1],
+            device_id={"rep": (replica + other) % reps},
+            device_id_type=MESH_IDS,
+        )
+
+    def add(kind, way, step):
+        slot = slots[kind].at[step, way]
+        mine = own(kind, way, step + 1)
+        slot[...] = (slot[...].astype(jnp.float32) + mine[...].astype(jnp.float32)).astype(
+            jnp.bfloat16
+        )
+
+    for kind in range(kinds):
+        for way in range(2):
+            hop(kind, way, 0, own(kind, way, 0)).start()
+
+    def walk(step, carry):
+        for kind in range(kinds):
+            for way in range(2):
+                hop(kind, way, step, slots[kind].at[step, way]).wait_recv()
+                add(kind, way, step)
+                hop(kind, way, step + 1, slots[kind].at[step, way]).start()
+        return carry
+
+    lax.fori_loop(0, size - 2, walk, 0)
+    for kind in range(kinds):
+        for way in range(2):
+            hop(kind, way, size - 2, slots[kind].at[size - 2, way]).wait_recv()
+            add(kind, way, size - 2)
+        for other in range(1, reps):
+            side(kind, other).start()
+    for kind in range(kinds):
+        total = slots[kind][size - 2].astype(jnp.float32)
+        for other in range(1, reps):
+            side(kind, other).wait_recv()
+            total += sides[kind][other - 1].astype(jnp.float32)
+        outs[kind][...] = total
+
+    def drain(step, carry):
+        for kind in range(kinds):
+            for way in range(2):
+                hop(kind, way, step, slots[kind].at[step, way]).wait_send()
+        return carry
+
+    lax.fori_loop(0, size - 1, drain, 0)
+    for kind in range(kinds):
+        for other in range(1, reps):
+            side(kind, other).wait_send()
+
+
+def reduce_all(grads):
+    size, reps = lax.axis_size("dp"), lax.axis_size("rep")
+    kinds = len(grads)
+    pieces = [g.shape[1:] for g in grads]
+    scratch = [pltpu.VMEM((size - 1,) + p, jnp.bfloat16) for p in pieces]
+    scratch += [pltpu.VMEM((max(reps - 1, 1),) + p, jnp.bfloat16) for p in pieces]
+    scratch += [pltpu.SemaphoreType.DMA((kinds, 2, size - 1))] * 2
+    scratch += [pltpu.SemaphoreType.DMA((kinds, max(reps - 1, 1)))] * 2
+    return pl.pallas_call(
+        functools.partial(reduce_kernel, size, reps, kinds),
+        out_shape=[jax.ShapeDtypeStruct(p, jnp.float32) for p in pieces],
+        in_specs=[pl.BlockSpec(memory_space=pltpu.VMEM)] * kinds,
+        out_specs=[pl.BlockSpec(memory_space=pltpu.VMEM)] * kinds,
+        scratch_shapes=scratch,
+        compiler_params=pltpu.CompilerParams(
+            collective_id=0, has_side_effects=True, vmem_limit_bytes=60 * 1024 * 1024
+        ),
+    )(*grads)
+
+
+def by_shard(total, dimension):
+    size = lax.axis_size("dp")
+    if dimension == 0:
+        return total.reshape(size, 2, total.shape[0] // (2 * size), total.shape[1])
+    rows, width = total.shape
+    part = total.reshape(rows, size, width // size).transpose(1, 0, 2)[:, None]
+    return jnp.pad(part, ((0, 0), (0, 1), (0, 16 - rows), (0, 128 - width // size)))
+
+
+def swap_blocks(first, second, section, dimension):
     first, second = to_low(first), to_low(second)
     incoming = partner(jnp.where(section == 0, second, first), "section", 0)
     kept = jnp.where(section == 0, first, second)
     total = to_low(kept.astype(jnp.float32) + incoming.astype(jnp.float32))
-    share = lax.psum_scatter(total, "dp", scatter_dimension=dimension, tiled=True)
-    return lax.psum(share, "rep").astype(jnp.float32)[None]
+    return by_shard(total, dimension)
 
 
 def local(
@@ -356,10 +494,14 @@
         jnp.concatenate([to_low(grad_patches), to_low(output), to_low(grad_text)], axis=1),
         section,
     )
-    summed = tuple(
-        reduce_blocks(first, second, section, dimension)
-        for first, second, dimension in zip(enc_grads, dec_grads, (0, 0, 0, 0, 0, 1))
-    )
+    reduced = reduce_all(
+        [
+            swap_blocks(first, second, section, dimension)
+            for first, second, dimension in zip(enc_grads, dec_grads, (0, 0, 0, 0, 0, 1))
+        ]
+    )
+    summed = tuple(part.reshape(1, -1, part.shape[-1]) for part in reduced[:-1])
+    summed += (reduced[-1][:1, : scales.shape[1], : scales.shape[2]],)
     return (
         results[:, count : count + length],
         results[:, count + length :],

time: 1050 us -> 802 us (0.76)
  waiting for transfers between devices: 648 us -> 204 us
  Pallas kernels: 0 us -> 197 us
  matrix products: 140 us -> 152 us
    reduce_scatter x5 -> x0, waiting for transfers between devices: 309 us -> none  [reduce_blocks(): lax.psum_scatter(total, 'dp', scatter_dimension=dimension, tiled=True)]
    pallas_call x0 -> x1, Pallas kernels: none -> 197 us  [reduce_all(): pl.pallas_call(functools.partial(reduce_kernel, size, reps, kinds), out_s...]
    unnamed x13 -> x5, waiting for transfers between devices: 65.2 us -> 2.6 us
    psum x1 -> x0, waiting for transfers between devices: 55.1 us -> none  [reduce_blocks(): return lax.psum(share, 'rep').astype(jnp.float32)[None]]
    ppermute x8, waiting for transfers between devices: 21 us -> 3.52 us  [partner(): return lax.ppermute(value, axis, pairs)]
    unnamed x295 -> x238, local copies, waits for them, and re-layouts: 21.5 us -> 21.1 us
  transfers between devices with their start and end apart: 20 -> 13, of which waited for: 14 -> 6; matrix products, arithmetic and copies ran while one was open for 19% -> 17% of each run, Pallas kernels for 0% -> 0%
where the time goes in v2:
time: 802 us; the launch traced here: 793 us
  waiting for transfers between devices  204 us (25%)
  Pallas kernels  197 us (25%)
  matrix products  152 us (19%)
  local copies, waits for them, and re-layouts  98.2 us (12%)
  other arithmetic  89.3 us (11%)
  blocking collectives  34.4 us (4%)
  between operations  15.8 us (2%)
    all_gather x5, waiting for transfers between devices, gather_blocks(): whole = lax.all_gather(piece[0], ('section', 'dp'), axis=0, tiled=False)  198 us
    pallas_call x1, Pallas kernels, reduce_all(): pl.pallas_call(functools.partial(reduce_kernel, size, reps, kinds), out_s...  197 us
    convert_element_type x13, other arithmetic, to_low(): return values.astype(jnp.bfloat16)  55.1 us
    dot_general x11, matrix products, weight_grad(): jnp.einsum('bsd,bse->de', acts, grads, preferred_element_type=jnp.float32)  38.5 us
    all_gather x1, blocking collectives, gather_blocks(): whole = lax.all_gather(piece[0], ('section', 'dp'), axis=0, tiled=False)  34.4 us
    dot_general x11, matrix products, back_project(): jnp.einsum('bse,de->bsd', grads, weight, preferred_element_type=jnp.float32)  32.2 us
    dot_general x11, matrix products, project(): jnp.einsum('bsd,de->bse', acts, weight, preferred_element_type=jnp.float32)  27.4 us
    unnamed x238, local copies, waits for them, and re-layouts  21.1 us
  transfers between devices with their start and end apart: 13, of which 6 were waited for; matrix products, arithmetic and copies ran while one was open for 17% of the time, Pallas kernels for 0%

profile of v2, /device:TPU:0, one launch (start us, length us, event | category | flops | bytes accessed | tf_op | source)
XLA Modules:
  0.0 792.6 jit_solution(903336834102201748)
XLA Ops:
  12.7 34.4 %all_gather.18 = bf16[16,3,96]{2,1,0:T(4,128)(2,1)S(1)} all-gather(bf16[1,3,96]{2,1,0:T(4,128)(2,1)S(1)} %copy-done.98), channel_id=1, replica_groups=mesh['section'=2,'dp'=8,'rep'=2] {'section','dp'}, dimensions={0}, use_global_device_ids=true | all-gather | bytes 9792 | tf_op jit(solution)/shard_map/all_gather | solution.py:302
  50.2 5.2 all-gather.8.cloned.1.call-done
  58.1 51.3 %all-gather.10.cloned.1.call-done = bf16[16,96,1536]{2,1,0:T(8,128)(2,1)} async-done(((bf16[1,96,1536]{2,1,0:T(8,128)(2,1)}), bf16[16,96,1536]{2,1,0:T(8,128)(2,1)}) %all-gather.10.cloned.1.call-update) | async-done | bytes 4718608 | tf_op jit(solution)/shard_map/all_gather | solution.py:302
  109.4 4.9 fusion.174
  114.4 61.9 %all-gather.6.cloned.1.call-done = bf16[16,96,2304]{2,1,0:T(8,128)(2,1)} async-done(((bf16[1,96,2304]{2,1,0:T(8,128)(2,1)}), bf16[16,96,2304]{2,1,0:T(8,128)(2,1)}) %all-gather.6.cloned.1.call-update) | async-done | bytes 7077904 | tf_op jit(solution)/shard_map/all_gather | solution.py:302
  176.3 5.3 fusion.173
  203.7 9.8 %copy.182 = f32[2,12,196,196]{3,0,2,1:T(2,128)} copy(f32[2,12,196,196]{2,3,1,0:T(8,128)} %fusion.186) | data formatting | bytes 7375872 | tf_op jit(solution)/shard_map/bqhe,bkhe->bhqk/dot_general | solution.py:54
  213.5 12.4 %fusion.180 = (f32[2,12,196]{0,2,1:T(8,128)S(1)}, f32[2,12,196,196]{3,0,2,1:T(2,128)S(1)}) fusion(f32[2,12,196,196]{3,0,2,1:T(2,128)} %copy.182, pred[2,196]{1,0:T(4,128)(4,1)S(1)} %dynamic-slice_compare_fusion), kind=kOutput, calls=%fused_computation.317 | output fusion | flops 3688131 | bytes 7395080 | tf_op jit(solution)/shard_map/sub | solution.py:58
  226.0 5.0 fusion.170
  234.6 23.4 %all-gather.12.cloned.1.call-done = bf16[16,96,3072]{2,1,0:T(8,128)(2,1)} async-done(((bf16[1,96,3072]{2,1,0:T(8,128)(2,1)}), bf16[16,96,3072]{2,1,0:T(8,128)(2,1)}) %all-gather.12.cloned.1.call-update) | async-done | bytes 9437200 | tf_op jit(solution)/shard_map/all_gather | solution.py:302
  258.1 7.1 fusion.172
  270.8 12.7 %multiply_convert_fusion = (bf16[2,196,3072]{2,1,0:T(8,128)(2,1)}, f32[2,196,3072]{2,1,0:T(8,128)}) fusion(f32[2,196,3072]{2,1,0:T(8,128)S(1)} %get-tuple-element.127, u8[196,3072]{1,0:T(8,128)(4,1)S(1)} %get-tuple-element.58, u8[196,3072]{1,0:T(8,128)(4,1)S(1)} %get-tuple-element.57), kind=kLoop, calls=%fused_computation.23 | loop fusion | flops 84295680 | bytes 13246464 | tf_op jit(solution)/shard_map/convert_element_type | solution.py:21
  283.4 56.1 %all-gather.14.cloned.1.call-done = bf16[16,384,768]{2,1,0:T(8,128)(2,1)} async-done(((bf16[1,384,768]{2,1,0:T(8,128)(2,1)}), bf16[16,384,768]{2,1,0:T(8,128)(2,1)}) %all-gather.14.cloned.1.call-update) | async-done | bytes 9437200 | tf_op jit(solution)/shard_map/all_gather | solution.py:302
  339.5 6.8 fusion.171
  346.3 5.7 fusion.182
  366.6 5.1 fusion.118
  371.8 8.0 %multiply_convert_fusion.1 = (bf16[2,128,3072]{2,1,0:T(8,128)(2,1)}, f32[2,128,3072]{2,1,0:T(8,128)S(1)}) fusion(f32[2,128,3072]{2,1,0:T(8,128)S(1)} %get-tuple-element.136, u8[128,3072]{1,0:T(8,128)(4,1)S(1)} %get-tuple-element.60, u8[128,3072]{1,0:T(8,128)(4,1)S(1)} %get-tuple-element.59), kind=kLoop, calls=%fused_computation.55 | loop fusion | flops 55050240 | bytes 8650752 | tf_op jit(solution)/shard_map/convert_element_type | solution.py:21
  394.9 5.9 fusion.81
  400.8 5.9 multiply_convert_fusion.4
  433.2 8.3 %add_convert_fusion.3 = bf16[2,196,3072]{2,1,0:T(8,128)(2,1)S(1)} fusion(f32[2,196,3072]{2,1,0:T(8,128)} %get-tuple-element.88, f32[2,196,3072]{2,1,0:T(8,128)} %copy-done.28, bf16[3072,768,1]{1,0,2:T(8,128)(2,1)} %bitcast.224, f32[2,196,768]{2,1,0:T(8,128)S(1)} %get-tuple-element.82, f32[2,196]{1,0:T(2,128)S(1)} %negate_multiply_fusion.4), kind=kOutput, calls=%fused_computation.22 | convolution fusion | flops 1867149312 | bytes 17966624 | tf_op jit(solution)/shard_map/bse,de->bsd/dot_general | solution.py:40
  444.0 4.6 bitcast_convert_fusion.3
  465.1 9.6 %copy.193 = f32[2,12,196,196]{3,0,2,1:T(2,128)} copy(f32[2,12,196,196]{2,3,1,0:T(8,128)} %fusion.188) | data formatting | bytes 7375872 | tf_op jit(solution)/shard_map/bqhe,bkhe->bhqk/dot_general | solution.py:68
  474.7 12.0 %select_convert_fusion = bf16[2,12,196,196]{3,0,2,1:T(2,128)(2,1)S(1)} fusion(f32[2,12,196,196]{3,0,2,1:T(2,128)} %get-tuple-element.90, f32[2,12,196,196]{3,0,2,1:T(2,128)} %copy.193, pred[2,196]{1,0:T(4,128)(4,1)S(1)} %dynamic-slice_compare_fusion), kind=kOutput, calls=%fused_computation.36 | output fusion | flops 4614819 | bytes 9220232 | tf_op jit(solution)/shard_map/sub | solution.py:74
  492.3 5.0 fusion.93
  497.3 5.1 bitcast_convert_fusion.5
  502.5 4.6 fusion.80
  529.5 5.3 broadcast_select_fusion.1
  536.3 5.1 broadcast_select_fusion
  559.5 5.2 add_convert_fusion.2
  564.8 9.5 %add_convert_fusion.1 = bf16[768,3072]{1,0:T(8,128)(2,1)} fusion(bf16[768,3072]{1,0:T(8,128)(2,1)} %collective-permute-done.5, bf16[768,3072]{1,0:T(8,128)(2,1)} %bitcast_convert_fusion.3, bf16[768,3072]{1,0:T(8,128)(2,1)} %get-tuple-element.153, pred[]{:T(512)S(6)} %eq.2), kind=kLoop, calls=%fused_computation.11 | loop fusion | flops 11796480 | bytes 18874368 | tf_op jit(solution)/shard_map/convert_element_type | solution.py:21
  574.3 6.5 add_convert_fusion
  580.8 196.7 %shard_map.178 = (f32[2,48,2304]{2,1,0:T(8,128)}, f32[2,48,768]{2,1,0:T(8,128)}, f32[2,48,1536]{2,1,0:T(8,128)}, f32[2,48,3072]{2,1,0:T(8,128)}, f32[2,192,768]{2,1,0:T(8,128)}, /*index=5*/f32[2,16,128]{2,1,0:T(8,128)}) custom-call(bf16[8,2,48,2304]{3,2,1,0:T(8,128)(2,1)} %bitcast.200, bf16[8,2,48,768]{3,2,1,0:T(8,128)(2,1)} %bitcast.214, ...), custom_call_target="tpu_custom_call" | custom-call | tf_op jit(solution)/shard_map/pallas_call | solution.py:422
  (415 shorter events, 172.2 us)
Async XLA Ops:
  7.2 48.1 %all-gather.8.cloned.1.call-start = ((), (), s32[]{:S(2)}) async-start(), calls=%async_computation.1 | async-start | bytes 2506752 | tf_op jit(solution)/shard_map/all_gather | solution.py:302
  7.9 101.5 %all-gather.10.cloned.1.call-start = ((), (), s32[]{:S(2)}) async-start(), calls=%async_computation.2 | async-start | bytes 5013504 | tf_op jit(solution)/shard_map/all_gather | solution.py:302
  8.7 167.6 %all-gather.6.cloned.1.call-start = ((), (), s32[]{:S(2)}) async-start(), calls=%async_computation | async-start | bytes 7520256 | tf_op jit(solution)/shard_map/all_gather | solution.py:302
  9.4 248.6 %all-gather.12.cloned.1.call-start = ((), (), s32[]{:S(2)}) async-start(), calls=%async_computation.3 | async-start | bytes 10027008 | tf_op jit(solution)/shard_map/all_gather | solution.py:302
  10.0 329.5 %all-gather.14.cloned.1.call-start = ((), (), s32[]{:S(2)}) async-start(), calls=%async_computation.4 | async-start | bytes 10027008 | tf_op jit(solution)/shard_map/all_gather | solution.py:302
  11.5 36.2 %copy-start.100 = (s32[4,128]{1,0:T(4,128)S(1)}, s32[4,128]{1,0:T(4,128)}, u32[]{:S(2)}) copy-start(s32[4,128]{1,0:T(4,128)} %param.14) | copy-start | bytes 6148
  11.5 36.2 %copy-start.99 = (s32[4,196]{1,0:T(4,128)S(1)}, s32[4,196]{1,0:T(4,128)}, u32[]{:S(2)}) copy-start(s32[4,196]{1,0:T(4,128)} %param.13) | copy-start | bytes 9412
  12.1 35.7 %collective-permute-start = (bf16[2,452,384]{2,0,1:T(2,128)(2,1)S(1)}, bf16[2,452,384]{2,0,1:T(2,128)(2,1)S(1)}, u32[]{:S(2)}, u32[]{:S(2)}) collective-permute-start(bf16[2,452,384]{2,0,1:T(2,128)(2,1)S(1)} %copy.170), channel_id=1, source_target_pairs={{0,16},{16,0},{1,17},{17,1},{2,18},{18,2},{3,19},{19,3},{4,20},{20... | collective-permute-start | bytes 2082824 | tf_op jit(solution)/shard_map/ppermute | solution.py:17
  47.5 134.1 %copy-start.88 = (f32[768]{0:T(1024)}, f32[768]{0:T(1024)S(1)}, u32[]{:S(2)}) copy-start(f32[768]{0:T(1024)S(1)} %mul.501) | copy-start | bytes 9220
  49.1 140.5 %copy-start.13 = (bf16[2,128,768]{2,1,0:T(8,128)(2,1)}, bf16[2,128,768]{2,1,0:T(8,128)(2,1)S(1)}, u32[]{:S(2)}) copy-start(bf16[2,128,768]{2,1,0:T(8,128)(2,1)S(1)} %get-tuple-element.94) | copy-start | bytes 1179652
  49.3 143.5 %copy-start.10 = (bf16[2,196,768]{2,1,0:T(8,128)(2,1)}, bf16[2,196,768]{2,1,0:T(8,128)(2,1)S(1)}, u32[]{:S(2)}) copy-start(bf16[2,196,768]{2,1,0:T(8,128)(2,1)S(1)} %get-tuple-element.92) | copy-start | bytes 1806340
  49.3 132.2 %copy-start.92 = (f32[2,128]{1,0:T(2,128)}, f32[2,128]{1,0:T(2,128)S(1)}, u32[]{:S(2)}) copy-start(f32[2,128]{1,0:T(2,128)S(1)} %broadcast_multiply_fusion.5) | copy-start | bytes 3076
  50.1 64.2 %copy-start.90 = (f32[2,196]{1,0:T(2,128)}, f32[2,196]{1,0:T(2,128)S(1)}, u32[]{:S(2)}) copy-start(f32[2,196]{1,0:T(2,128)S(1)} %fusion.92) | copy-start | bytes 4708
  50.1 131.4 %copy-start.94 = (f32[2,128]{1,0:T(2,128)}, f32[2,128]{1,0:T(2,128)S(1)}, u32[]{:S(2)}) copy-start(f32[2,128]{1,0:T(2,128)S(1)} %fusion.149) | copy-start | bytes 3076
  58.1 131.5 %copy-start.8 = (bf16[8,96,768]{2,1,0:T(8,128)(2,1)}, bf16[8,96,768]{2,1,0:T(8,128)(2,1)S(1)}, u32[]{:S(2)}) copy-start(bf16[8,96,768]{2,1,0:T(8,128)(2,1)S(1)} %get-tuple-element.104) | copy-start | bytes 3538948
  366.4 17.2 %copy-start = (f32[2,128,768]{2,1,0:T(8,128)}, f32[2,128,768]{2,1,0:T(8,128)S(1)}, u32[]{:S(2)}) copy-start(f32[2,128,768]{2,1,0:T(8,128)S(1)} %get-tuple-element.135) | copy-start | bytes 2359300
  366.4 13.5 %slice-start.8 = ((s8[4718592]{0:T(1024)(128)(4,1)}), s8[4194304]{0:T(1024)(128)(4,1)S(1)}, s32[]{:S(2)}) async-start(s8[4718592]{0:T(1024)(128)(4,1)} %bitcast.216), calls=%async_computation.13 | async-start | bytes 8388608
  366.6 13.2 %slice-start.9 = ((s8[4718592]{0:T(1024)(128)(4,1)}), s8[524288]{0:T(1024)(128)(4,1)S(1)}, s32[]{:S(2)}) async-start(s8[4718592]{0:T(1024)(128)(4,1)} %bitcast.216), calls=%async_computation.14 | async-start | bytes 1048576
  371.8 10.2 %slice-start.12 = ((s8[4718592]{0:T(1024)(128)(4,1)}), s8[4194304]{0:T(1024)(128)(4,1)S(1)}, s32[]{:S(2)}) async-start(s8[4718592]{0:T(1024)(128)(4,1)} %bitcast.226), calls=%async_computation.17 | async-start | bytes 8388608
  433.2 20.4 %copy-start.4 = (f32[2,196,768]{2,1,0:T(8,128)}, f32[2,196,768]{2,1,0:T(8,128)S(1)}, u32[]{:S(2)}) copy-start(f32[2,196,768]{2,1,0:T(8,128)S(1)} %get-tuple-element.82) | copy-start | bytes 3612676
  474.7 12.0 %copy-start.49 = (bf16[2,196,768]{1,2,0:T(8,128)(2,1)S(1)}, bf16[2,196,768]{1,2,0:T(8,128)(2,1)}, u32[]{:S(2)}) copy-start(bf16[2,196,768]{1,2,0:T(8,128)(2,1)} %copy-done.48) | copy-start | bytes 1806340
  502.5 10.4 %copy-start.14 = (bf16[2,128,768]{2,1,0:T(8,128)(2,1)S(1)}, bf16[2,128,768]{2,1,0:T(8,128)(2,1)}, u32[]{:S(2)}) copy-start(bf16[2,128,768]{2,1,0:T(8,128)(2,1)} %copy-done.13) | copy-start | bytes 1179652
  502.5 10.4 %copy-start.89 = (f32[768]{0:T(1024)S(1)}, f32[768]{0:T(1024)}, u32[]{:S(2)}) copy-start(f32[768]{0:T(1024)} %copy-done.88) | copy-start | bytes 9220
  502.5 10.4 %copy-start.93 = (f32[2,128]{1,0:T(2,128)S(1)}, f32[2,128]{1,0:T(2,128)}, u32[]{:S(2)}) copy-start(f32[2,128]{1,0:T(2,128)} %copy-done.92) | copy-start | bytes 3076
  522.2 33.2 %collective-permute-start.4 = (bf16[768,1536]{1,0:T(8,128)(2,1)}, bf16[768,1536]{1,0:T(8,128)(2,1)}, u32[]{:S(2)}, u32[]{:S(2)}) collective-permute-start(bf16[768,1536]{1,0:T(8,128)(2,1)} %get-tuple-element.150), channel_id=1, source_target_pairs={{0,16},{16,0},{1,17},{17,1},{2,18},{18,2},{3,19},{19,3},{4,20},{20... | collective-permute-start | bytes 7077896 | tf_op jit(solution)/shard_map/ppermute | solution.py:17
  524.1 18.1 %collective-permute-start.7 = (bf16[3,768]{1,0:T(4,128)(2,1)S(1)}, bf16[3,768]{1,0:T(4,128)(2,1)S(1)}, u32[]{:S(2)}, u32[]{:S(2)}) collective-permute-start(bf16[3,768]{1,0:T(4,128)(2,1)S(1)} %broadcast_select_fusion.13), channel_id=1, source_target_pairs={{0,16},{16,0},{1,17},{17,1},{2,18},{18,2},{3,19},{19,3},{4,20},{20... | collective-permute-start | bytes 13832 | tf_op jit(solution)/shard_map/ppermute | solution.py:17
  529.3 30.2 %collective-permute-start.2 = (bf16[768,2304]{1,0:T(8,128)(2,1)}, bf16[768,2304]{1,0:T(8,128)(2,1)}, u32[]{:S(2)}, u32[]{:S(2)}) collective-permute-start(bf16[768,2304]{1,0:T(8,128)(2,1)} %get-tuple-element.146), channel_id=1, source_target_pairs={{0,16},{16,0},{1,17},{17,1},{2,18},{18,2},{3,19},{19,3},{4,20},{20... | collective-permute-start | bytes 10616840 | tf_op jit(solution)/shard_map/ppermute | solution.py:17
  534.9 29.9 %collective-permute-start.5 = (bf16[768,3072]{1,0:T(8,128)(2,1)}, bf16[768,3072]{1,0:T(8,128)(2,1)}, u32[]{:S(2)}, u32[]{:S(2)}) collective-permute-start(bf16[768,3072]{1,0:T(8,128)(2,1)} %get-tuple-element.152), channel_id=1, source_target_pairs={{0,16},{16,0},{1,17},{17,1},{2,18},{18,2},{3,19},{19,3},{4,20},{20... | collective-permute-start | bytes 14155784 | tf_op jit(solution)/shard_map/ppermute | solution.py:17
  536.0 8.5 %collective-permute-start.1 = (bf16[2,452,384]{2,0,1:T(2,128)(2,1)S(1)}, bf16[2,452,384]{2,0,1:T(2,128)(2,1)}, u32[]{:S(2)}, u32[]{:S(2)}) collective-permute-start(bf16[2,452,384]{2,0,1:T(2,128)(2,1)S(1)} %copy.208), channel_id=1, source_target_pairs={{0,16},{16,0},{1,17},{17,1},{2,18},{18,2},{3,19},{19,3},{4,20},{20... | collective-permute-start | bytes 2082824 | tf_op jit(solution)/shard_map/ppermute | solution.py:17
  542.3 32.0 %collective-permute-start.6 = (bf16[3072,768]{1,0:T(8,128)(2,1)}, bf16[3072,768]{1,0:T(8,128)(2,1)}, u32[]{:S(2)}, u32[]{:S(2)}) collective-permute-start(bf16[3072,768]{1,0:T(8,128)(2,1)} %get-tuple-element.154), channel_id=1, source_target_pairs={{0,16},{16,0},{1,17},{17,1},{2,18},{18,2},{3,19},{19,3},{4,20},{20... | collective-permute-start | bytes 14155784 | tf_op jit(solution)/shard_map/ppermute | solution.py:17
  544.5 8.1 %collective-permute-start.3 = (bf16[768,768]{1,0:T(8,128)(2,1)}, bf16[768,768]{1,0:T(8,128)(2,1)}, u32[]{:S(2)}, u32[]{:S(2)}) collective-permute-start(bf16[768,768]{1,0:T(8,128)(2,1)} %get-tuple-element.148), channel_id=1, source_target_pairs={{0,16},{16,0},{1,17},{17,1},{2,18},{18,2},{3,19},{19,3},{4,20},{20... | collective-permute-start | bytes 3538952 | tf_op jit(solution)/shard_map/ppermute | solution.py:17
  564.7 9.5 %slice-start.5 = ((s8[4718592]{0:T(1024)(128)(4,1)}), s8[524288]{0:T(1024)(128)(4,1)S(1)}, s32[]{:S(2)}) async-start(s8[4718592]{0:T(1024)(128)(4,1)} %bitcast.194), calls=%async_computation.10 | async-start | bytes 1048576
  (96 other events, 376.8 us)
Sparse Core Ops, SparseCore 0:
  10.2 45.0 all-gather.7
  57.5 51.8 all-gather.9
  111.6 64.5 all-gather.5
  178.3 79.6 all-gather.11
  260.1 79.3 all-gather.13

commit v3 on v2

--- a/solution.py
+++ b/solution.py
@@ -296,16 +296,6 @@
     return jnp.concatenate([low_part, high_part], axis=0)
 
 
-def gather_blocks(piece, dimension):
-    sections = lax.axis_size("section")
-    shards = lax.axis_size("dp")
-    whole = lax.all_gather(piece[0], ("section", "dp"), axis=0, tiled=False)
-    if dimension == 0:
-        return whole.reshape(sections, shards * piece.shape[1], piece.shape[2])
-    whole = whole.reshape(sections, shards, piece.shape[1], piece.shape[2])
-    return whole.transpose(0, 2, 1, 3).reshape(sections, piece.shape[1], -1)
-
-
 def ring_place(shard, size):
     column = shard % 2
     row = shard // 2
@@ -440,6 +430,189 @@
     return jnp.pad(part, ((0, 0), (0, 1), (0, 16 - rows), (0, 128 - width // size)))
 
 
+def gather_kernel(size, reps, kinds, cuts, *refs):
+    pieces, firsts, seconds = refs[:kinds], refs[kinds : 2 * kinds], refs[2 * kinds : 3 * kinds]
+    send, recv, side_send, side_recv, pair_send, pair_recv, keep = refs[3 * kinds :]
+    me = lax.axis_index("dp")
+    place = ring_place(me, size)
+    replica, section = lax.axis_index("rep"), lax.axis_index("section")
+    targets = (
+        ring_shard((place + 1) % size, size),
+        ring_shard((place + size - 1) % size, size),
+    )
+    signs = (-1, 1)
+    helped = [kind for kind in range(kinds) if cuts[kind] > 1]
+
+    barrier = pltpu.get_barrier_semaphore()
+    for target in targets:
+        pl.semaphore_signal(barrier, inc=1, device_id={"dp": target}, device_id_type=MESH_IDS)
+    pl.semaphore_signal(
+        barrier, inc=1, device_id={"section": 1 - section}, device_id_type=MESH_IDS
+    )
+    if helped:
+        pl.semaphore_signal(
+            barrier, inc=1, device_id={"rep": 1 - replica}, device_id_type=MESH_IDS
+        )
+    pl.semaphore_wait(barrier, 4 if helped else 3)
+
+    def carry(mine, theirs):
+        def holder(way, step):
+            return ring_shard((place + signs[way] * step + size) % size, size)
+
+        def ring_rows(kind):
+            return pl.ds(replica, 2) if cuts[kind] > 1 else pl.ds(0, 1)
+
+        def hop(kind, way, step, first=False):
+            at = holder(way, step)
+            source = pieces[kind] if first else mine[kind].at[at]
+            return pltpu.make_async_remote_copy(
+                src_ref=source.at[way, ring_rows(kind)],
+                dst_ref=mine[kind].at[at, way, ring_rows(kind)],
+                send_sem=send.at[kind, way, step],
+                recv_sem=recv.at[kind, way, step],
+                device_id={"dp": targets[way]},
+                device_id_type=MESH_IDS,
+            )
+
+        def arrived(kind, way, step):
+            at = holder(way, step + 1)
+            return pltpu.make_async_remote_copy(
+                src_ref=mine[kind].at[at, way, ring_rows(kind)],
+                dst_ref=mine[kind].at[at, way, ring_rows(kind)],
+                send_sem=send.at[kind, way, step],
+                recv_sem=recv.at[kind, way, step],
+                device_id={"dp": targets[way]},
+                device_id_type=MESH_IDS,
+            )
+
+        def side(kind, way, step, part):
+            region = mine[kind].at[holder(way, step), way, pl.ds(part, 1)]
+            return pltpu.make_async_remote_copy(
+                src_ref=region,
+                dst_ref=region,
+                send_sem=side_send.at[kind],
+                recv_sem=side_recv.at[kind, way, step - 1],
+                device_id={"rep": 1 - replica},
+                device_id_type=MESH_IDS,
+            )
+
+        def pair(kind, source, target):
+            return pltpu.make_async_remote_copy(
+                src_ref=source,
+                dst_ref=target,
+                send_sem=pair_send.at[kind],
+                recv_sem=pair_recv.at[kind],
+                device_id={"section": 1 - section},
+                device_id_type=MESH_IDS,
+            )
+
+        def forward(kind, way, step, rows):
+            region = mine[kind].at[holder(way, step), way, rows]
+            pair(kind, region, region).start()
+
+        def take_side(kind, way, step):
+            part = 2 * (1 - replica)
+            side(kind, way, step, part).wait_recv()
+
+        for kind in range(kinds):
+            for way in range(2):
+                hop(kind, way, 0, first=True).start()
+        for kind in range(kinds):
+            pair(kind, pieces[kind], mine[kind].at[me]).start()
+            pltpu.make_async_copy(pieces[kind], mine[kind].at[me], keep.at[kind]).start()
+
+        def settle(step, last=False, sides=True):
+            for kind in range(kinds):
+                for way in range(2):
+                    arrived(kind, way, step).wait_recv()
+                    if not last:
+                        hop(kind, way, step + 1).start()
+                    if cuts[kind] > 1:
+                        side(kind, way, step + 1, 2 * replica).start()
+                    forward(kind, way, step + 1, ring_rows(kind))
+            for kind in helped if sides else []:
+                for way in range(2):
+                    take_side(kind, way, step)
+
+        def settle_sides(step):
+            for kind in helped:
+                for way in range(2):
+                    forward(kind, way, step, pl.ds(2 * (1 - replica), 1))
+
+        settle(0, sides=False)
+
+        def walk(step, nothing):
+            settle(step)
+            settle_sides(step)
+            return nothing
+
+        lax.fori_loop(1, size - 2, walk, 0)
+        settle(size - 2, last=True)
+        settle_sides(size - 2)
+        for kind in helped:
+            for way in range(2):
+                take_side(kind, way, size - 1)
+        settle_sides(size - 1)
+
+        for kind in range(kinds):
+            pltpu.make_async_copy(pieces[kind], mine[kind].at[me], keep.at[kind]).wait()
+
+        def drain(step, nothing):
+            for kind in range(kinds):
+                for way in range(2):
+                    arrived(kind, way, step).wait_send()
+            return nothing
+
+        lax.fori_loop(0, size - 1, drain, 0)
+        for kind in range(kinds):
+            if cuts[kind] > 1:
+                sent = mine[kind].at[pl.ds(0, size - 1), :, pl.ds(2 * replica, 1)]
+                pltpu.make_async_copy(sent, sent, side_send.at[kind]).wait()
+            pltpu.make_async_copy(mine[kind], mine[kind], pair_send.at[kind]).wait()
+            pltpu.make_async_copy(theirs[kind], theirs[kind], pair_recv.at[kind]).wait()
+
+    @pl.when(section == 0)
+    def _():
+        carry(firsts, seconds)
+
+    @pl.when(section == 1)
+    def _():
+        carry(seconds, firsts)
+
+
+def cut_of(rows, reps):
+    return 3 if reps == 2 and rows % 48 == 0 else 1
+
+
+def gather_all(pieces):
+    size, reps = lax.axis_size("dp"), lax.axis_size("rep")
+    kinds = len(pieces)
+    cuts = [cut_of(piece.shape[0], reps) for piece in pieces]
+    shaped = [
+        piece.reshape(2, cut, piece.shape[0] // (2 * cut), piece.shape[1])
+        for piece, cut in zip(pieces, cuts)
+    ]
+    wholes = [jax.ShapeDtypeStruct((size,) + piece.shape, piece.dtype) for piece in shaped]
+    scratch = [pltpu.SemaphoreType.DMA((kinds, 2, size - 1))] * 2
+    scratch += [pltpu.SemaphoreType.DMA((kinds,)), pltpu.SemaphoreType.DMA((kinds, 2, size - 1))]
+    scratch += [pltpu.SemaphoreType.DMA((kinds,))] * 3
+    outs = pl.pallas_call(
+        functools.partial(gather_kernel, size, reps, kinds, cuts),
+        out_shape=wholes * 2,
+        in_specs=[pl.BlockSpec(memory_space=pltpu.VMEM)] * kinds,
+        out_specs=[pl.BlockSpec(memory_space=pl.ANY)] * (2 * kinds),
+        scratch_shapes=scratch,
+        compiler_params=pltpu.CompilerParams(collective_id=1, has_side_effects=True),
+    )(*shaped)
+    return outs[:kinds], outs[kinds:]
+
+
+def as_weights(outs, rows, width):
+    weights = [part.reshape(-1, part.shape[-1]) for part in outs[:-1]]
+    gains = outs[-1].reshape(outs[-1].shape[0], -1, outs[-1].shape[-1])[:, :rows, :width]
+    return tuple(weights) + (gains.transpose(1, 0, 2).reshape(rows, -1),)
+
+
 def swap_blocks(first, second, section, dimension):
     first, second = to_low(first), to_low(second)
     incoming = partner(jnp.where(section == 0, second, first), "section", 0)
@@ -464,19 +637,13 @@
     section = lax.axis_index("section")
     count = patches.shape[1]
     length = captions.shape[1]
-    gathered = tuple(
-        gather_blocks(piece, dimension)
-        for piece, dimension in (
-            (mixing, 0),
-            (merging, 0),
-            (crossing, 0),
-            (widening, 0),
-            (narrowing, 0),
-            (scales, 1),
-        )
-    )
-    enc_weights = tuple(piece[0] for piece in gathered)
-    dec_weights = tuple(piece[1] for piece in gathered)
+    rows, width = scales.shape[1:]
+    gains = jnp.pad(scales[0], ((0, 48 - rows), (0, 128 - width)))
+    firsts, seconds = gather_all(
+        [mixing[0], merging[0], crossing[0], widening[0], narrowing[0], gains]
+    )
+    enc_weights = as_weights(firsts, rows, width)
+    dec_weights = as_weights(seconds, rows, width)
     states = to_whole_images(jnp.concatenate([patches, captions, cotangent], axis=1), section)
     states = states.astype(jnp.float32)
     own_patches = states[:, :count]
@@ -501,7 +668,7 @@
         ]
     )
     summed = tuple(part.reshape(1, -1, part.shape[-1]) for part in reduced[:-1])
-    summed += (reduced[-1][:1, : scales.shape[1], : scales.shape[2]],)
+    summed += (reduced[-1][:1, :rows, :width],)
     return (
         results[:, count : count + length],
         results[:, count + length :],

time: 802 us -> 644 us (0.80)
  waiting for transfers between devices: 204 us -> 3.63 us
  Pallas kernels: 197 us -> 319 us
  blocking collectives: 34.4 us -> 0 us
  local copies, waits for them, and re-layouts: 98.2 us -> 69 us
  between operations: 15.8 us -> 2.42 us
    all_gather x5 -> x0, waiting for transfers between devices: 198 us -> none  [gather_blocks(): whole = lax.all_gather(piece[0], ('section', 'dp'), axis=0, tiled=False)]
    pallas_call x0 -> x1, Pallas kernels: none -> 122 us  [gather_all(): pl.pallas_call(functools.partial(gather_kernel, size, reps, kinds, cuts),...]
    all_gather x1 -> x0, blocking collectives: 34.4 us -> none  [gather_blocks(): whole = lax.all_gather(piece[0], ('section', 'dp'), axis=0, tiled=False)]
    slice x6 -> x1, local copies, waits for them, and re-layouts: 27.7 us -> 0.79 us  [local(): summed += (reduced[-1][:1, :rows, :width],)]
    unnamed x238 -> x226, local copies, waits for them, and re-layouts: 21.1 us -> 19.1 us
  transfers between devices with their start and end apart: 13 -> 8, of which waited for: 6 -> 1; matrix products, arithmetic and copies ran while one was open for 17% -> 8% of each run, Pallas kernels for 0% -> 19%
where the time goes in v3:
time: 644 us; the launch traced here: 639 us
  Pallas kernels  319 us (50%)
  matrix products  150 us (23%)
  other arithmetic  91.9 us (14%)
  local copies, waits for them, and re-layouts  69 us (11%)
    pallas_call x1, Pallas kernels, reduce_all(): pl.pallas_call(functools.partial(reduce_kernel, size, reps, kinds), out_s...  197 us
    pallas_call x1, Pallas kernels, gather_all(): pl.pallas_call(functools.partial(gather_kernel, size, reps, kinds, cuts),...  122 us
    convert_element_type x13, other arithmetic, to_low(): return values.astype(jnp.bfloat16)  55.1 us
    dot_general x11, matrix products, weight_grad(): jnp.einsum('bsd,bse->de', acts, grads, preferred_element_type=jnp.float32)  38.5 us
    dot_general x11, matrix products, back_project(): jnp.einsum('bse,de->bsd', grads, weight, preferred_element_type=jnp.float32)  32 us
    dot_general x11, matrix products, project(): jnp.einsum('bsd,de->bse', acts, weight, preferred_element_type=jnp.float32)  27.4 us
    unnamed x226, local copies, waits for them, and re-layouts  19.1 us
  transfers between devices with their start and end apart: 8, of which 1 were waited for; matrix products, arithmetic and copies ran while one was open for 8% of the time, Pallas kernels for 19%

profile of v3, /device:TPU:0, one launch (start us, length us, event | category | flops | bytes accessed | tf_op | source)
XLA Modules:
  0.0 638.7 jit_solution(7895399143254405888)
XLA Ops:
  5.0 121.9 %shard_map.178 = (bf16[8,2,3,16,2304]{4,3,2,1,0:T(8,128)(2,1)}, bf16[8,2,3,16,768]{4,3,2,1,0:T(8,128)(2,1)}, bf16[8,2,3,16,1536]{4,3,2,1,0:T(8,128)(2,1)}, bf16[...) custom-call(bf16[2,3,16,2304]{3,2,1,0:T(8,128)(2,1)} %bitcast.256, ...), custom_call_target="tpu_custom_call" | custom-call | tf_op jit(solution)/shard_map/pallas_call | solution.py:599
  152.4 9.8 %copy.182 = f32[2,12,196,196]{3,0,2,1:T(2,128)} copy(f32[2,12,196,196]{2,3,1,0:T(8,128)} %fusion.181) | data formatting | bytes 7375872 | tf_op jit(solution)/shard_map/bqhe,bkhe->bhqk/dot_general | solution.py:54
  162.2 12.4 %fusion.175 = (f32[2,12,196]{0,2,1:T(8,128)S(1)}, f32[2,12,196,196]{3,0,2,1:T(2,128)S(1)}) fusion(f32[2,12,196,196]{3,0,2,1:T(2,128)} %copy.182, pred[2,196]{1,0:T(4,128)(4,1)S(1)} %dynamic-slice_compare_fusion), kind=kOutput, calls=%fused_computation.312 | output fusion | flops 3688131 | bytes 7395080 | tf_op jit(solution)/shard_map/sub | solution.py:58
  174.6 5.0 fusion.170
  182.2 6.5 %fusion.99 = (u8[196,3072]{1,0:T(8,128)(4,1)S(1)}, u8[196,3072]{1,0:T(8,128)(4,1)S(1)}, f32[2,196,3072]{2,1,0:T(8,128)S(1)}) fusion(bf16[768,3072,1]{1,0,2:T(8,128)(2,1)} %bitcast.278, f32[2,196,768]{2,1,0:T(8,128)S(1)} %get-tuple-element.138, f32[768]{0:T(1024)S(1)} %mul.524, f32[2,196]{1,0:T(2,128)S(1)} %fusion.143, ...), kind=kOutput, calls=%fused_computation.165 | convolution fusion | flops 1865342976 | bytes 11950144 | tf_op jit(solution)/shard_map/bsd,de->bse/dot_general | solution.py:36
  188.7 12.5 %multiply_convert_fusion = (bf16[2,196,3072]{2,1,0:T(8,128)(2,1)S(1)}, f32[2,196,3072]{2,1,0:T(8,128)}) fusion(f32[2,196,3072]{2,1,0:T(8,128)S(1)} %get-tuple-element.139, u8[196,3072]{1,0:T(8,128)(4,1)S(1)} %get-tuple-element.82, u8[196,3072]{1,0:T(8,128)(4,1)S(1)} %get-tuple-element.81), kind=kLoop, calls=%fused_computation.23 | loop fusion | flops 84295680 | bytes 13246464 | tf_op jit(solution)/shard_map/convert_element_type | solution.py:21
  210.7 3.9 fusion.179
  218.1 5.4 fusion.118
  223.6 8.0 %multiply_convert_fusion.1 = (bf16[2,128,3072]{2,1,0:T(8,128)(2,1)}, f32[2,128,3072]{2,1,0:T(8,128)S(1)}) fusion(f32[2,128,3072]{2,1,0:T(8,128)S(1)} %get-tuple-element.148, u8[128,3072]{1,0:T(8,128)(4,1)S(1)} %get-tuple-element.84, u8[128,3072]{1,0:T(8,128)(4,1)S(1)} %get-tuple-element.83), kind=kLoop, calls=%fused_computation.55 | loop fusion | flops 55050240 | bytes 8650752 | tf_op jit(solution)/shard_map/convert_element_type | solution.py:21
  247.4 5.9 fusion.81
  253.3 5.9 multiply_convert_fusion.4
  269.9 4.3 fusion.87
  274.2 4.6 fusion.84
  281.7 3.8 multiply_reduce_fusion.3
  286.1 8.1 %add_convert_fusion.3 = bf16[2,196,3072]{2,1,0:T(8,128)(2,1)S(1)} fusion(f32[2,196,3072]{2,1,0:T(8,128)} %get-tuple-element.112, f32[2,196,3072]{2,1,0:T(8,128)} %copy-done.24, bf16[3072,768,1]{1,0,2:T(8,128)(2,1)} %bitcast.282, f32[2,196,768]{2,1,0:T(8,128)S(1)} %get-tuple-element.106, f32[2,196]{1,0:T(2,128)S(1)} %negate_multiply_fusion.4), kind=kOutput, calls=%fused_computation.22 | convolution fusion | flops 1867149312 | bytes 17966624 | tf_op jit(solution)/shard_map/bse,de->bsd/dot_general | solution.py:40
  296.6 4.7 bitcast_convert_fusion.3
  301.3 4.5 bitcast_convert_fusion.1
  317.7 9.6 %copy.193 = f32[2,12,196,196]{3,0,2,1:T(2,128)} copy(f32[2,12,196,196]{2,3,1,0:T(8,128)} %fusion.183) | data formatting | bytes 7375872 | tf_op jit(solution)/shard_map/bqhe,bkhe->bhqk/dot_general | solution.py:68
  327.3 12.1 %select_convert_fusion = bf16[2,12,196,196]{3,0,2,1:T(2,128)(2,1)S(1)} fusion(f32[2,12,196,196]{3,0,2,1:T(2,128)} %get-tuple-element.114, f32[2,12,196,196]{3,0,2,1:T(2,128)} %copy.193, pred[2,196]{1,0:T(4,128)(4,1)S(1)} %dynamic-slice_compare_fusion), kind=kOutput, calls=%fused_computation.36 | output fusion | flops 4614819 | bytes 9220232 | tf_op jit(solution)/shard_map/sub | solution.py:74
  345.0 5.0 fusion.93
  350.0 5.2 bitcast_convert_fusion.5
  355.2 4.6 fusion.80
  365.6 3.7 fusion.114
  371.2 3.7 broadcast_select_fusion.3
  377.7 4.5 broadcast_select_fusion.2
  382.4 5.1 broadcast_select_fusion.1
  389.1 5.0 broadcast_select_fusion
  408.1 4.1 add_convert_fusion.4
  412.2 5.2 add_convert_fusion.2
  417.5 9.5 %add_convert_fusion.1 = bf16[768,3072]{1,0:T(8,128)(2,1)} fusion(bf16[768,3072]{1,0:T(8,128)(2,1)} %collective-permute-done.5, bf16[768,3072]{1,0:T(8,128)(2,1)} %bitcast_convert_fusion.3, bf16[768,3072]{1,0:T(8,128)(2,1)} %get-tuple-element.165, pred[]{:T(512)S(6)} %eq.2), kind=kLoop, calls=%fused_computation.11 | loop fusion | flops 11796480 | bytes 18874368 | tf_op jit(solution)/shard_map/convert_element_type | solution.py:21
  427.1 6.6 %add_convert_fusion = bf16[3072,768]{1,0:T(8,128)(2,1)} fusion(bf16[3072,768]{1,0:T(8,128)(2,1)} %collective-permute-done.6, bf16[3072,768]{1,0:T(8,128)(2,1)S(1)} %bitcast.203, bf16[3072,768]{1,0:T(8,128)(2,1)S(1)} %bitcast.205, pred[]{:T(512)S(6)} %eq.2), kind=kLoop, calls=%fused_computation.10 | loop fusion | flops 11796480 | bytes 18874368 | tf_op jit(solution)/shard_map/convert_element_type | solution.py:21
  433.6 196.6 %shard_map.179 = (f32[2,48,2304]{2,1,0:T(8,128)}, f32[2,48,768]{2,1,0:T(8,128)}, f32[2,48,1536]{2,1,0:T(8,128)}, f32[2,48,3072]{2,1,0:T(8,128)}, f32[2,192,768]{2,1,0:T(8,128)}, /*index=5*/f32[2,16,128]{2,1,0:T(8,128)}) custom-call(bf16[8,2,48,2304]{3,2,1,0:T(8,128)(2,1)} %bitcast.210, bf16[8,2,48,768]{3,2,1,0:T(8,128)(2,1)} %bitcast.218, ...), custom_call_target="tpu_custom_call" | custom-call | tf_op jit(solution)/shard_map/pallas_call | solution.py:412
  (386 shorter events, 128.6 us)
Async XLA Ops:
  3.2 125.7 %copy-start.88 = (s32[4,128]{1,0:T(4,128)S(1)}, s32[4,128]{1,0:T(4,128)}, u32[]{:S(2)}) copy-start(s32[4,128]{1,0:T(4,128)} %param.14) | copy-start | bytes 6148
  3.2 125.7 %copy-start.87 = (s32[4,196]{1,0:T(4,128)S(1)}, s32[4,196]{1,0:T(4,128)}, u32[]{:S(2)}) copy-start(s32[4,196]{1,0:T(4,128)} %param.13) | copy-start | bytes 9412
  3.8 125.2 %collective-permute-start = (bf16[2,452,384]{2,0,1:T(2,128)(2,1)S(1)}, bf16[2,452,384]{2,0,1:T(2,128)(2,1)S(1)}, u32[]{:S(2)}, u32[]{:S(2)}) collective-permute-start(bf16[2,452,384]{2,0,1:T(2,128)(2,1)S(1)} %copy.170), channel_id=1, source_target_pairs={{0,16},{16,0},{1,17},{17,1},{2,18},{18,2},{3,19},{19,3},{4,20},{20... | collective-permute-start | bytes 2082824 | tf_op jit(solution)/shard_map/ppermute | solution.py:17
  130.3 7.9 %copy-start.11 = (bf16[2,128,768]{2,1,0:T(8,128)(2,1)}, bf16[2,128,768]{2,1,0:T(8,128)(2,1)S(1)}, u32[]{:S(2)}) copy-start(bf16[2,128,768]{2,1,0:T(8,128)(2,1)S(1)} %get-tuple-element.118) | copy-start | bytes 1179652
  130.5 10.9 %copy-start.8 = (bf16[2,196,768]{2,1,0:T(8,128)(2,1)}, bf16[2,196,768]{2,1,0:T(8,128)(2,1)S(1)}, u32[]{:S(2)}) copy-start(bf16[2,196,768]{2,1,0:T(8,128)(2,1)S(1)} %get-tuple-element.116) | copy-start | bytes 1806340
  181.1 20.2 %slice-start.12 = ((s8[4718592]{0:T(1024)(128)(4,1)}), s8[4194304]{0:T(1024)(128)(4,1)S(1)}, s32[]{:S(2)}) async-start(s8[4718592]{0:T(1024)(128)(4,1)} %bitcast.283), calls=%async_computation.12 | async-start | bytes 8388608
  181.9 19.4 %copy-start.28 = (f32[2,196,768]{2,1,0:T(8,128)}, f32[2,196,768]{2,1,0:T(8,128)S(1)}, u32[]{:S(2)}) copy-start(f32[2,196,768]{2,1,0:T(8,128)S(1)} %get-tuple-element.138) | copy-start | bytes 3612676
  182.2 19.1 %slice-start.13 = ((s8[4718592]{0:T(1024)(128)(4,1)}), s8[524288]{0:T(1024)(128)(4,1)S(1)}, s32[]{:S(2)}) async-start(s8[4718592]{0:T(1024)(128)(4,1)} %bitcast.283), calls=%async_computation.13 | async-start | bytes 1048576
  188.7 12.5 %copy-start.24 = (f32[2,196,3072]{2,1,0:T(8,128)}, f32[2,196,3072]{2,1,0:T(8,128)S(1)}, u32[]{:S(2)}) copy-start(f32[2,196,3072]{2,1,0:T(8,128)S(1)} %get-tuple-element.139) | copy-start | bytes 14450692
  217.3 14.3 %slice-start.8 = ((s8[4718592]{0:T(1024)(128)(4,1)}), s8[4194304]{0:T(1024)(128)(4,1)S(1)}, s32[]{:S(2)}) async-start(s8[4718592]{0:T(1024)(128)(4,1)} %bitcast.275), calls=%async_computation.8 | async-start | bytes 8388608
  217.9 17.5 %copy-start = (f32[2,128,768]{2,1,0:T(8,128)}, f32[2,128,768]{2,1,0:T(8,128)S(1)}, u32[]{:S(2)}) copy-start(f32[2,128,768]{2,1,0:T(8,128)S(1)} %get-tuple-element.147) | copy-start | bytes 2359300
  218.1 13.5 %slice-start.9 = ((s8[4718592]{0:T(1024)(128)(4,1)}), s8[524288]{0:T(1024)(128)(4,1)S(1)}, s32[]{:S(2)}) async-start(s8[4718592]{0:T(1024)(128)(4,1)} %bitcast.275), calls=%async_computation.9 | async-start | bytes 1048576
  223.6 8.1 %copy-start.21 = (bf16[2,128,768]{2,1,0:T(8,128)(2,1)S(1)}, bf16[2,128,768]{2,1,0:T(8,128)(2,1)}, u32[]{:S(2)}) copy-start(bf16[2,128,768]{2,1,0:T(8,128)(2,1)} %pad_maximum_fusion.16) | copy-start | bytes 1179652
  223.6 10.1 %slice-start.14 = ((s8[4718592]{0:T(1024)(128)(4,1)}), s8[4194304]{0:T(1024)(128)(4,1)S(1)}, s32[]{:S(2)}) async-start(s8[4718592]{0:T(1024)(128)(4,1)} %bitcast.287), calls=%async_computation.14 | async-start | bytes 8388608
  281.7 12.5 %slice-start.10 = ((s8[4718592]{0:T(1024)(128)(4,1)}), s8[4194304]{0:T(1024)(128)(4,1)S(1)}, s32[]{:S(2)}) async-start(s8[4718592]{0:T(1024)(128)(4,1)} %bitcast.279), calls=%async_computation.10 | async-start | bytes 8388608
  286.0 20.2 %copy-start.4 = (f32[2,196,768]{2,1,0:T(8,128)}, f32[2,196,768]{2,1,0:T(8,128)S(1)}, u32[]{:S(2)}) copy-start(f32[2,196,768]{2,1,0:T(8,128)S(1)} %get-tuple-element.106) | copy-start | bytes 3612676
  286.1 8.1 %copy-start.29 = (f32[2,196,768]{2,1,0:T(8,128)S(1)}, f32[2,196,768]{2,1,0:T(8,128)}, u32[]{:S(2)}) copy-start(f32[2,196,768]{2,1,0:T(8,128)} %copy-done.28) | copy-start | bytes 3612676
  286.1 8.1 %slice-start.11 = ((s8[4718592]{0:T(1024)(128)(4,1)}), s8[524288]{0:T(1024)(128)(4,1)S(1)}, s32[]{:S(2)}) async-start(s8[4718592]{0:T(1024)(128)(4,1)} %bitcast.279), calls=%async_computation.11 | async-start | bytes 1048576
  327.3 12.1 %copy-start.42 = (bf16[2,196,768]{1,2,0:T(8,128)(2,1)S(1)}, bf16[2,196,768]{1,2,0:T(8,128)(2,1)}, u32[]{:S(2)}) copy-start(bf16[2,196,768]{1,2,0:T(8,128)(2,1)} %copy-done.41) | copy-start | bytes 1806340
  355.2 10.4 %copy-start.12 = (bf16[2,128,768]{2,1,0:T(8,128)(2,1)S(1)}, bf16[2,128,768]{2,1,0:T(8,128)(2,1)}, u32[]{:S(2)}) copy-start(bf16[2,128,768]{2,1,0:T(8,128)(2,1)} %copy-done.11) | copy-start | bytes 1179652
  374.9 33.2 %collective-permute-start.4 = (bf16[768,1536]{1,0:T(8,128)(2,1)}, bf16[768,1536]{1,0:T(8,128)(2,1)}, u32[]{:S(2)}, u32[]{:S(2)}) collective-permute-start(bf16[768,1536]{1,0:T(8,128)(2,1)} %get-tuple-element.162), channel_id=1, source_target_pairs={{0,16},{16,0},{1,17},{17,1},{2,18},{18,2},{3,19},{19,3},{4,20},{20... | collective-permute-start | bytes 7077896 | tf_op jit(solution)/shard_map/ppermute | solution.py:17
  376.9 18.0 %collective-permute-start.7 = (bf16[3,768]{1,0:T(4,128)(2,1)S(1)}, bf16[3,768]{1,0:T(4,128)(2,1)S(1)}, u32[]{:S(2)}, u32[]{:S(2)}) collective-permute-start(bf16[3,768]{1,0:T(4,128)(2,1)S(1)} %broadcast_select_fusion.13), channel_id=1, source_target_pairs={{0,16},{16,0},{1,17},{17,1},{2,18},{18,2},{3,19},{19,3},{4,20},{20... | collective-permute-start | bytes 13832 | tf_op jit(solution)/shard_map/ppermute | solution.py:17
  382.1 6.9 %slice-start = ((s8[4718592]{0:T(1024)(128)(4,1)}), s8[4194304]{0:T(1024)(128)(4,1)S(1)}, s32[]{:S(2)}) async-start(s8[4718592]{0:T(1024)(128)(4,1)} %bitcast.200), calls=%async_computation | async-start | bytes 8388608
  382.1 30.1 %collective-permute-start.2 = (bf16[768,2304]{1,0:T(8,128)(2,1)}, bf16[768,2304]{1,0:T(8,128)(2,1)}, u32[]{:S(2)}, u32[]{:S(2)}) collective-permute-start(bf16[768,2304]{1,0:T(8,128)(2,1)} %get-tuple-element.158), channel_id=1, source_target_pairs={{0,16},{16,0},{1,17},{17,1},{2,18},{18,2},{3,19},{19,3},{4,20},{20... | collective-permute-start | bytes 10616840 | tf_op jit(solution)/shard_map/ppermute | solution.py:17
  387.6 29.9 %collective-permute-start.5 = (bf16[768,3072]{1,0:T(8,128)(2,1)}, bf16[768,3072]{1,0:T(8,128)(2,1)}, u32[]{:S(2)}, u32[]{:S(2)}) collective-permute-start(bf16[768,3072]{1,0:T(8,128)(2,1)} %get-tuple-element.164), channel_id=1, source_target_pairs={{0,16},{16,0},{1,17},{17,1},{2,18},{18,2},{3,19},{19,3},{4,20},{20... | collective-permute-start | bytes 14155784 | tf_op jit(solution)/shard_map/ppermute | solution.py:17
  388.7 8.4 %collective-permute-start.1 = (bf16[2,452,384]{2,0,1:T(2,128)(2,1)S(1)}, bf16[2,452,384]{2,0,1:T(2,128)(2,1)}, u32[]{:S(2)}, u32[]{:S(2)}) collective-permute-start(bf16[2,452,384]{2,0,1:T(2,128)(2,1)S(1)} %copy.208), channel_id=1, source_target_pairs={{0,16},{16,0},{1,17},{17,1},{2,18},{18,2},{3,19},{19,3},{4,20},{20... | collective-permute-start | bytes 2082824 | tf_op jit(solution)/shard_map/ppermute | solution.py:17
  394.9 32.1 %collective-permute-start.6 = (bf16[3072,768]{1,0:T(8,128)(2,1)}, bf16[3072,768]{1,0:T(8,128)(2,1)}, u32[]{:S(2)}, u32[]{:S(2)}) collective-permute-start(bf16[3072,768]{1,0:T(8,128)(2,1)} %get-tuple-element.166), channel_id=1, source_target_pairs={{0,16},{16,0},{1,17},{17,1},{2,18},{18,2},{3,19},{19,3},{4,20},{20... | collective-permute-start | bytes 14155784 | tf_op jit(solution)/shard_map/ppermute | solution.py:17
  397.0 8.2 %collective-permute-start.3 = (bf16[768,768]{1,0:T(8,128)(2,1)}, bf16[768,768]{1,0:T(8,128)(2,1)}, u32[]{:S(2)}, u32[]{:S(2)}) collective-permute-start(bf16[768,768]{1,0:T(8,128)(2,1)} %get-tuple-element.160), channel_id=1, source_target_pairs={{0,16},{16,0},{1,17},{17,1},{2,18},{18,2},{3,19},{19,3},{4,20},{20... | collective-permute-start | bytes 3538952 | tf_op jit(solution)/shard_map/ppermute | solution.py:17
  417.5 9.5 %slice-start.2 = ((s8[4718592]{0:T(1024)(128)(4,1)}), s8[4194304]{0:T(1024)(128)(4,1)S(1)}, s32[]{:S(2)}) async-start(s8[4718592]{0:T(1024)(128)(4,1)} %bitcast.202), calls=%async_computation.2 | async-start | bytes 8388608
  417.5 9.5 %slice-start.4 = ((s8[4718592]{0:T(1024)(128)(4,1)}), s8[4194304]{0:T(1024)(128)(4,1)S(1)}, s32[]{:S(2)}) async-start(s8[4718592]{0:T(1024)(128)(4,1)} %bitcast.204), calls=%async_computation.4 | async-start | bytes 8388608
  417.5 9.5 %slice-start.3 = ((s8[4718592]{0:T(1024)(128)(4,1)}), s8[524288]{0:T(1024)(128)(4,1)S(1)}, s32[]{:S(2)}) async-start(s8[4718592]{0:T(1024)(128)(4,1)} %bitcast.202), calls=%async_computation.3 | async-start | bytes 1048576
  417.5 9.6 %slice-start.5 = ((s8[4718592]{0:T(1024)(128)(4,1)}), s8[524288]{0:T(1024)(128)(4,1)S(1)}, s32[]{:S(2)}) async-start(s8[4718592]{0:T(1024)(128)(4,1)} %bitcast.204), calls=%async_computation.5 | async-start | bytes 1048576
  (85 other events, 279.9 us)

commit v4 on v3

--- a/solution.py
+++ b/solution.py
@@ -44,56 +44,141 @@
     return jnp.einsum("bsd,bse->de", acts, grads, preferred_element_type=jnp.float32)
 
 
-def split_heads(values):
-    return values.reshape(values.shape[0], values.shape[1], HEADS, values.shape[2] // HEADS)
-
-
-def attend_forward(queries, keys, values, mask):
-    scale = queries.shape[-1] ** (-0.5)
-    scores = (
-        jnp.einsum("bqhe,bkhe->bhqk", queries, keys, preferred_element_type=jnp.float32) * scale
-    )
-    scores = jnp.where(mask[:, None], scores, -1000000000.0)
-    peak = jnp.max(scores, axis=-1, keepdims=True)
-    expo = jnp.exp(scores - peak)
-    softmaxed = expo / jnp.sum(expo, axis=-1, keepdims=True)
-    mixed = jnp.einsum(
-        "bhqk,bkhe->bqhe", to_low(softmaxed), values, preferred_element_type=jnp.float32
-    )
-    return (to_low(mixed), softmaxed)
-
-
-def attend_backward(grad_mixed, softmaxed, queries, keys, values, mask):
-    scale = queries.shape[-1] ** (-0.5)
-    grad_soft = jnp.einsum(
-        "bqhe,bkhe->bhqk", grad_mixed, values, preferred_element_type=jnp.float32
-    )
-    grad_value = jnp.einsum(
-        "bhqk,bqhe->bkhe", to_low(softmaxed), grad_mixed, preferred_element_type=jnp.float32
-    )
-    grad_scores = softmaxed * (grad_soft - jnp.sum(softmaxed * grad_soft, axis=-1, keepdims=True))
-    grad_scores = to_low(jnp.where(mask[:, None], grad_scores, 0.0))
-    grad_query = (
-        jnp.einsum("bhqk,bkhe->bqhe", grad_scores, keys, preferred_element_type=jnp.float32) * scale
-    )
-    grad_key = (
-        jnp.einsum("bhqk,bqhe->bkhe", grad_scores, queries, preferred_element_type=jnp.float32)
-        * scale
-    )
-    return (grad_query, grad_key, grad_value)
-
-
-def attention_forward(states, gain, w_in, w_out, mask):
-    width = states.shape[2]
+def across(left, right):
+    return lax.dot_general(left, right, (((1,), (1,)), ((), ())), preferred_element_type=jnp.float32)
+
+
+def along(left, right):
+    return lax.dot_general(left, right, (((0,), (0,)), ((), ())), preferred_element_type=jnp.float32)
+
+
+def plain(left, right):
+    return lax.dot_general(left, right, (((1,), (0,)), ((), ())), preferred_element_type=jnp.float32)
+
+
+def seen_keys(keep, keys, queries, causal):
+    seen = jnp.broadcast_to(keep > 0, (keys, queries))
+    if causal:
+        key_at = lax.broadcasted_iota(jnp.int32, (keys, queries), 0)
+        query_at = lax.broadcasted_iota(jnp.int32, (keys, queries), 1)
+        seen = seen & (key_at <= query_at)
+    return seen
+
+
+def soft_keys(keys, queries, seen, scale):
+    scores = jnp.where(seen, across(keys, queries) * scale, -1000000000.0)
+    expo = jnp.exp(scores - jnp.max(scores, axis=0, keepdims=True))
+    return expo * (1.0 / jnp.sum(expo, axis=0, keepdims=True))
+
+
+def halves_of(values):
+    lane = lax.broadcasted_iota(jnp.int32, values.shape, 1)
+    in_first = lane < values.shape[1] // 2
+    zero = jnp.zeros_like(values)
+    return (jnp.where(in_first, values, zero), jnp.where(in_first, zero, values))
+
+
+def join_halves(first, second):
+    lane = lax.broadcasted_iota(jnp.int32, first.shape, 1)
+    return jnp.where(lane < first.shape[1] // 2, first, second)
+
+
+def attend_kernel(causal, width, joint, scale, *refs):
+    if joint:
+        q_ref, keep_ref, out_ref = refs
+        k_ref, key_at, value_at = q_ref, width, 2 * width
+    else:
+        q_ref, k_ref, keep_ref, out_ref = refs
+        key_at, value_at = 0, width
+    count, length = k_ref.shape[1], q_ref.shape[1]
+    seen = seen_keys(keep_ref[0], count, length, causal)
+    pair = 2 * width // HEADS
+    for at in range(0, width, pair):
+        queries = q_ref[0, :, at : at + pair]
+        values = k_ref[0, :, value_at + at : value_at + at + pair]
+        mixed = [
+            along(to_low(soft_keys(keys, queries, seen, scale)), values)
+            for keys in halves_of(k_ref[0, :, key_at + at : key_at + at + pair])
+        ]
+        out_ref[0, :, at : at + pair] = to_low(join_halves(*mixed))
+
+
+def attend_back_kernel(causal, width, joint, scale, *refs):
+    if joint:
+        q_ref, keep_ref, g_ref, dq_ref = refs
+        k_ref, dk_ref, key_at, value_at = q_ref, dq_ref, width, 2 * width
+    else:
+        q_ref, k_ref, keep_ref, g_ref, dq_ref, dk_ref = refs
+        key_at, value_at = 0, width
+    count, length = k_ref.shape[1], q_ref.shape[1]
+    seen = seen_keys(keep_ref[0], count, length, causal)
+    pair = 2 * width // HEADS
+    for at in range(0, width, pair):
+        queries = q_ref[0, :, at : at + pair]
+        grads = g_ref[0, :, at : at + pair]
+        all_keys = k_ref[0, :, key_at + at : key_at + at + pair]
+        all_values = k_ref[0, :, value_at + at : value_at + at + pair]
+        parts = []
+        for keys, values in zip(halves_of(all_keys), halves_of(all_values)):
+            soft = soft_keys(keys, queries, seen, scale)
+            grad_soft = across(values, grads)
+            inner = jnp.sum(soft * grad_soft, axis=0, keepdims=True)
+            grad_scores = to_low(jnp.where(seen, soft * (grad_soft - inner), 0.0))
+            parts.append(
+                (
+                    along(grad_scores, all_keys) * scale,
+                    plain(grad_scores, queries) * scale,
+                    plain(to_low(soft), grads),
+                )
+            )
+        grad_query, grad_key, grad_value = (join_halves(*both) for both in zip(*parts))
+        dq_ref[0, :, at : at + pair] = to_low(grad_query)
+        dk_ref[0, :, key_at + at : key_at + at + pair] = to_low(grad_key)
+        dk_ref[0, :, value_at + at : value_at + at + pair] = to_low(grad_value)
+
+
+def per_image(value):
+    return pl.BlockSpec((1,) + value.shape[1:], lambda image: (image, 0, 0))
+
+
+def attend(queries, memory, keep, causal):
+    joint = memory is None
+    width = queries.shape[2] // 3 if joint else queries.shape[2]
+    operands = [queries] if joint else [queries, memory]
+    operands.append(keep[:, :, None])
+    out = jax.ShapeDtypeStruct(queries.shape[:2] + (width,), jnp.bfloat16)
+    scale = (width // HEADS) ** (-0.5)
+    return pl.pallas_call(
+        functools.partial(attend_kernel, causal, width, joint, scale),
+        grid=(queries.shape[0],),
+        out_shape=out,
+        in_specs=[per_image(value) for value in operands],
+        out_specs=per_image(out),
+    )(*operands)
+
+
+def attend_back(grad_mixed, queries, memory, keep, causal):
+    joint = memory is None
+    width = grad_mixed.shape[2]
+    operands = [queries] if joint else [queries, memory]
+    outs = [jax.ShapeDtypeStruct(value.shape, jnp.bfloat16) for value in operands]
+    operands += [keep[:, :, None], grad_mixed]
+    scale = (width // HEADS) ** (-0.5)
+    return pl.pallas_call(
+        functools.partial(attend_back_kernel, causal, width, joint, scale),
+        grid=(queries.shape[0],),
+        out_shape=outs,
+        in_specs=[per_image(value) for value in operands],
+        out_specs=[per_image(value) for value in outs],
+    )(*operands)
+
+
+def attention_forward(states, gain, w_in, w_out, keep, causal):
     first = to_low(layer_norm(states, gain))
     united = to_low(project(first, w_in))
-    queries = split_heads(united[..., :width])
-    keys = split_heads(united[..., width : 2 * width])
-    values = split_heads(united[..., 2 * width :])
-    mixed, softmaxed = attend_forward(queries, keys, values, mask)
-    joined = mixed.reshape(states.shape)
+    joined = attend(united, None, keep, causal)
     hidden = states + project(joined, w_out)
-    return (first, queries, keys, values, softmaxed, joined, hidden)
+    return (first, united, joined, hidden)
 
 
 def feedforward_forward(states, gain, w_up, w_down):
@@ -104,21 +189,11 @@
     return (second, widened, active, after)
 
 
-def attention_back(
-    grad_after, states, gain, first, queries, keys, values, softmaxed, joined, mask, w_in, w_out
-):
+def attention_back(grad_after, states, gain, first, united, joined, keep, causal, w_in, w_out):
     branch = to_low(grad_after)
     g_out = weight_grad(joined, branch)
     grad_joined = to_low(back_project(branch, w_out))
-    grad_query, grad_key, grad_value = attend_backward(
-        split_heads(grad_joined), softmaxed, queries, keys, values, mask
-    )
-    shape = states.shape
-    grad_united = to_low(
-        jnp.concatenate(
-            [grad_query.reshape(shape), grad_key.reshape(shape), grad_value.reshape(shape)], axis=-1
-        )
-    )
+    (grad_united,) = attend_back(grad_joined, united, None, keep, causal)
     g_in = weight_grad(first, grad_united)
     _, pull = jax.vjp(layer_norm, states, gain)
     grad_norm, g_gain = pull(back_project(grad_united, w_in))
@@ -139,50 +214,19 @@
 def encoder_pass(states, keep, weights):
     w_in, w_out, w_pair, w_up, w_down, gains = weights
     gains = gains.astype(jnp.float32)
-    batch, count, width = states.shape
-    mask = jnp.broadcast_to(keep[:, None, :] > 0, (batch, count, count))
-    first, queries, keys, values, softmaxed, joined, hidden = attention_forward(
-        states, gains[0], w_in, w_out, mask
+    first, united, joined, hidden = attention_forward(
+        states, gains[0], w_in, w_out, keep, False
     )
     second, widened, active, after = feedforward_forward(hidden, gains[1], w_up, w_down)
     final = to_low(layer_norm(after, gains[2]))
     memory = to_low(project(final, w_pair))
-    saved = (
-        mask,
-        first,
-        queries,
-        keys,
-        values,
-        softmaxed,
-        joined,
-        hidden,
-        second,
-        widened,
-        active,
-        after,
-        final,
-    )
-    return (memory, saved)
-
-
-def encoder_backward(states, saved, weights, grad_memory):
+    return (memory, (first, united, joined, hidden, second, widened, active, after, final))
+
+
+def encoder_backward(states, keep, saved, weights, grad_memory):
     w_in, w_out, w_pair, w_up, w_down, gains = weights
     gains = gains.astype(jnp.float32)
-    (
-        mask,
-        first,
-        queries,
-        keys,
-        values,
-        softmaxed,
-        joined,
-        hidden,
-        second,
-        widened,
-        active,
-        after,
-        final,
-    ) = saved
+    first, united, joined, hidden, second, widened, active, after, final = saved
     g_pair = weight_grad(final, grad_memory)
     _, pull = jax.vjp(layer_norm, after, gains[2])
     grad_after, g_final = pull(back_project(grad_memory, w_pair))
@@ -190,18 +234,7 @@
         grad_after, hidden, gains[1], second, widened, active, w_up, w_down
     )
     grad_states, g_in, g_out, g_first = attention_back(
-        grad_hidden,
-        states,
-        gains[0],
-        first,
-        queries,
-        keys,
-        values,
-        softmaxed,
-        joined,
-        mask,
-        w_in,
-        w_out,
+        grad_hidden, states, gains[0], first, united, joined, keep, False, w_in, w_out
     )
     return (
         grad_states,
@@ -212,22 +245,13 @@
 def decoder_step(text, text_keep, memory, keep, weights, cotan):
     w_in, w_out, w_pair, w_up, w_down, gains = weights
     gains = gains.astype(jnp.float32)
-    batch, length, width = text.shape
-    query_pos = lax.broadcasted_iota(jnp.int32, (length, length), 0)
-    key_pos = lax.broadcasted_iota(jnp.int32, (length, length), 1)
-    self_mask = (key_pos <= query_pos)[None] & (text_keep[:, None, :] > 0)
-    cross_mask = jnp.broadcast_to(keep[:, None, :] > 0, (batch, length, keep.shape[1]))
-    first, queries, keys, values, softmaxed, joined, hidden = attention_forward(
-        text, gains[0], w_in, w_out, self_mask
+    width = text.shape[2]
+    first, united, joined, hidden = attention_forward(
+        text, gains[0], w_in, w_out, text_keep, True
     )
     second = to_low(layer_norm(hidden, gains[1]))
     cross_query = to_low(project(second, w_pair[:, :width]))
-    memory_keys = split_heads(memory[..., :width])
-    memory_vals = split_heads(memory[..., width:])
-    cross_mixed, cross_soft = attend_forward(
-        split_heads(cross_query), memory_keys, memory_vals, cross_mask
-    )
-    cross_joined = cross_mixed.reshape(text.shape)
+    cross_joined = attend(cross_query, memory, keep, False)
     crossed = hidden + project(cross_joined, w_pair[:, width:])
     third, widened, active, output = feedforward_forward(crossed, gains[2], w_up, w_down)
     grad_crossed, g_up, g_down, g_third = feedforward_back(
@@ -236,36 +260,15 @@
     branch = to_low(grad_crossed)
     g_cross_out = weight_grad(cross_joined, branch)
     grad_cross_joined = to_low(back_project(branch, w_pair[:, width:]))
-    grad_query, grad_key, grad_value = attend_backward(
-        split_heads(grad_cross_joined),
-        cross_soft,
-        split_heads(cross_query),
-        memory_keys,
-        memory_vals,
-        cross_mask,
-    )
-    grad_cross_query = to_low(grad_query.reshape(text.shape))
-    mem_shape = (batch, memory.shape[1], width)
-    grad_memory = to_low(
-        jnp.concatenate([grad_key.reshape(mem_shape), grad_value.reshape(mem_shape)], axis=-1)
+    grad_cross_query, grad_memory = attend_back(
+        grad_cross_joined, cross_query, memory, keep, False
     )
     g_cross_query = weight_grad(second, grad_cross_query)
     _, pull = jax.vjp(layer_norm, hidden, gains[1])
     grad_norm, g_second = pull(back_project(grad_cross_query, w_pair[:, :width]))
     grad_hidden = grad_crossed + grad_norm
     grad_text, g_in, g_out, g_first = attention_back(
-        grad_hidden,
-        text,
-        gains[0],
-        first,
-        queries,
-        keys,
-        values,
-        softmaxed,
-        joined,
-        self_mask,
-        w_in,
-        w_out,
+        grad_hidden, text, gains[0], first, united, joined, text_keep, True, w_in, w_out
     )
     g_pair = jnp.concatenate([g_cross_query, g_cross_out], axis=1)
     return (
@@ -656,7 +659,9 @@
     output, grad_text, grad_memory, dec_grads = decoder_step(
         own_text, text_keep, memory, keep, dec_weights, own_cotan
     )
-    grad_patches, enc_grads = encoder_backward(own_patches, saved, enc_weights, grad_memory)
+    grad_patches, enc_grads = encoder_backward(
+        own_patches, keep, saved, enc_weights, grad_memory
+    )
     results = to_half_features(
         jnp.concatenate([to_low(grad_patches), to_low(output), to_low(grad_text)], axis=1),
         section,

time: 644 us -> 569 us (0.88)
  Pallas kernels: 319 us -> 373 us
  matrix products: 150 us -> 98.1 us
  local copies, waits for them, and re-layouts: 69 us -> 22.7 us
  other arithmetic: 91.9 us -> 61.7 us
    pallas_call x0 -> x6, Pallas kernels: none -> 54.5 us  [the longest x3 31 us: attend_back(): pl.pallas_call(functools.partial(attend_back_kernel, causal, width, joint...]
    dot_general x16 -> x0, matrix products: 47 us -> none  [the longest x3 11.1 us: attend_backward(): jnp.einsum('bhqk,bkhe->bqhe', grad_scores, keys, preferred_element_type=j...]
    sub x2 -> x0, other arithmetic: 24.5 us -> none  [the longest x1 12.4 us: attend_forward(): expo = jnp.exp(scores - peak)]
    dot_general x2 -> x0, local copies, waits for them, and re-layouts: 19.4 us -> none  [the longest x1 9.81 us: attend_forward(): jnp.einsum('bqhe,bkhe->bhqk', queries, keys, preferred_element_type=jnp.f...]
    reshape x8 -> x0, local copies, waits for them, and re-layouts: 11 us -> none  [the longest x2 3 us: attention_back(): grad_value.reshape(shape)]
    slice x11 -> x0, local copies, waits for them, and re-layouts: 10.3 us -> none  [the longest x2 3.34 us: decoder_step(): memory_keys = split_heads(memory[..., :width])]
    convert_element_type x13 -> x12, other arithmetic: 55.1 us -> 49 us  [to_low(): return values.astype(jnp.bfloat16)]
    unnamed x226 -> x166, local copies, waits for them, and re-layouts: 19.1 us -> 17.3 us
  transfers between devices with their start and end apart: 8 -> 8, of which waited for: 1 -> 1; matrix products, arithmetic and copies ran while one was open for 8% -> 9% of each run, Pallas kernels for 19% -> 22%
where the time goes in v4:
time: 569 us; the launch traced here: 563 us
  Pallas kernels  373 us (66%)
  matrix products  98.1 us (17%)
  other arithmetic  61.7 us (11%)
  local copies, waits for them, and re-layouts  22.7 us (4%)
    pallas_call x1, Pallas kernels, reduce_all(): pl.pallas_call(functools.partial(reduce_kernel, size, reps, kinds), out_s...  197 us
    pallas_call x1, Pallas kernels, gather_all(): pl.pallas_call(functools.partial(gather_kernel, size, reps, kinds, cuts),...  122 us
    convert_element_type x12, other arithmetic, to_low(): return values.astype(jnp.bfloat16)  49 us
    dot_general x11, matrix products, weight_grad(): jnp.einsum('bsd,bse->de', acts, grads, preferred_element_type=jnp.float32)  37 us
    pallas_call x3, Pallas kernels, attend_back(): pl.pallas_call(functools.partial(attend_back_kernel, causal, width, joint...  31 us
    dot_general x11, matrix products, project(): jnp.einsum('bsd,de->bse', acts, weight, preferred_element_type=jnp.float32)  31 us
    dot_general x11, matrix products, back_project(): jnp.einsum('bse,de->bsd', grads, weight, preferred_element_type=jnp.float32)  30.1 us
    pallas_call x3, Pallas kernels, attend(): pl.pallas_call(functools.partial(attend_kernel, causal, width, joint, sca...  23.5 us
  transfers between devices with their start and end apart: 8, of which 1 were waited for; matrix products, arithmetic and copies ran while one was open for 9% of the time, Pallas kernels for 22%

profile of v4, /device:TPU:0, one launch (start us, length us, event | category | flops | bytes accessed | tf_op | source)
XLA Modules:
  0.0 563.3 jit_solution(3180852779219467285)
XLA Ops:
  6.7 121.7 %shard_map.178 = (bf16[8,2,3,16,2304]{4,3,2,1,0:T(8,128)(2,1)}, bf16[8,2,3,16,768]{4,3,2,1,0:T(8,128)(2,1)}, bf16[8,2,3,16,1536]{4,3,2,1,0:T(8,128)(2,1)}, bf16[...) custom-call(bf16[2,3,16,2304]{3,2,1,0:T(8,128)(2,1)} %bitcast.167, ...), custom_call_target="tpu_custom_call" | custom-call | tf_op jit(solution)/shard_map/pallas_call | solution.py:602
  134.9 8.9 %shard_map.179 = bf16[2,128,768]{2,1,0:T(8,128)(2,1)} custom-call(bf16[2,128,2304]{2,1,0:T(8,128)(2,1)} %convolution_convert_fusion.1.refs_0_, s32[2,128,1]{2,1,0:T(8,128)} %copy.53.refs_1_), custom_call_target="tpu_custom_call" | custom-call | tf_op jit(solution)/shard_map/pallas_call | solution.py:151
  146.3 3.0 convolution_convert_fusion.refs_0_
  149.3 5.3 shard_map.180
  157.2 6.5 %fusion.24 = (u8[196,3072]{1,0:T(8,128)(4,1)S(1)}, u8[196,3072]{1,0:T(8,128)(4,1)S(1)}, f32[2,196,3072]{2,1,0:T(8,128)S(1)}) fusion(bf16[768,3072,1]{1,0,2:T(8,128)(2,1)} %bitcast.182, f32[2,196,768]{2,1,0:T(8,128)S(1)} %get-tuple-element.121, f32[768]{0:T(1024)S(1)} %mul.450, f32[2,196]{1,0:T(2,128)S(1)} %fusion.52, f32[2,196]{1,0:T(2,128)S(1)} %broadcast_multiply_fusion.1), kind=kOutput, calls=%fused_computation.104 | convolution fusion | flops 1865342976 | bytes 11950144 | tf_op jit(solution)/shard_map/bsd,de->bse/dot_general | solution.py:36
  163.7 12.3 %multiply_convert_fusion = (bf16[2,196,3072]{2,1,0:T(8,128)(2,1)S(1)}, f32[2,196,3072]{2,1,0:T(8,128)}) fusion(f32[2,196,3072]{2,1,0:T(8,128)S(1)} %get-tuple-element.122, u8[196,3072]{1,0:T(8,128)(4,1)S(1)} %get-tuple-element.77, u8[196,3072]{1,0:T(8,128)(4,1)S(1)} %get-tuple-element.76), kind=kLoop, calls=%fused_computation.17 | loop fusion | flops 84295680 | bytes 13246464 | tf_op jit(solution)/shard_map/convert_element_type | solution.py:21
  176.1 2.3 fusion.64
  180.7 2.3 convolution_convert_fusion.2.refs_1_
  183.0 9.3 %shard_map.181 = bf16[2,128,768]{2,1,0:T(8,128)(2,1)} custom-call(bf16[2,128,768]{2,1,0:T(8,128)(2,1)} %convolution_convert_fusion.6.refs_0_, bf16[2,196,1536]{2,1,0:T(8,128)(2,1)} %convolution_convert_fusion.2.refs_1_, s32[2,196,1]{2,1,0:T(8,128)} %copy.54.refs_1_.refs_2_), custom_call_target="tpu_custom_call" | custom-call | tf_op jit(solution)/shard_map/pallas_call | solution.py:151
  194.7 4.8 fusion.37
  199.5 8.0 %multiply_convert_fusion.1 = (bf16[2,128,3072]{2,1,0:T(8,128)(2,1)}, f32[2,128,3072]{2,1,0:T(8,128)S(1)}) fusion(f32[2,128,3072]{2,1,0:T(8,128)S(1)} %get-tuple-element.127, u8[128,3072]{1,0:T(8,128)(4,1)S(1)} %get-tuple-element.79, u8[128,3072]{1,0:T(8,128)(4,1)S(1)} %get-tuple-element.78), kind=kLoop, calls=%fused_computation.44 | loop fusion | flops 55050240 | bytes 8650752 | tf_op jit(solution)/shard_map/convert_element_type | solution.py:21
  214.7 10.6 %shard_map.182 = (bf16[2,128,768]{2,1,0:T(8,128)(2,1)}, bf16[2,196,1536]{2,1,0:T(8,128)(2,1)}) custom-call(bf16[2,128,768]{2,1,0:T(8,128)(2,1)} %convolution_convert_fusion.6.refs_0_, bf16[2,196,1536]{2,1,0:T(8,128)(2,1)} %convolution_convert_fusion.2.refs_1_, s32[2,196,1]{2,1,0:T(8,128)} %copy.54.refs_1_.refs_2_, ...), custom_call_target="tpu_custom_call" | custom-call | tf_op jit(solution)/shard_map/pallas_call | solution.py:167
  233.1 7.4 %add_convert_fusion.3 = bf16[2,196,3072]{2,1,0:T(8,128)(2,1)S(1)} fusion(f32[2,196,3072]{2,1,0:T(8,128)} %get-tuple-element.107, f32[2,196,3072]{2,1,0:T(8,128)S(1)} %bitcast.151, bf16[3072,768,1]{1,0,2:T(8,128)(2,1)} %bitcast.186, f32[2,196,768]{2,1,0:T(8,128)S(1)} %get-tuple-element.101, f32[2,196]{1,0:T(2,128)S(1)} %negate_multiply_fusion.4), kind=kOutput, calls=%fused_computation.16 | convolution fusion | flops 1867149312 | bytes 17966624 | tf_op jit(solution)/shard_map/bse,de->bsd/dot_general | solution.py:40
  240.5 2.3 multiply_reduce_fusion.1
  242.9 4.6 bitcast_convert_fusion.3
  247.5 4.4 bitcast_convert_fusion.1
  255.8 11.7 %shard_map.183 = bf16[2,196,2304]{2,1,0:T(8,128)(2,1)} custom-call(bf16[2,196,2304]{2,1,0:T(8,128)(2,1)} %convolution_convert_fusion.refs_0_, s32[2,196,1]{2,1,0:T(8,128)} %copy.54.refs_1_.refs_2_, bf16[2,196,768]{2,1,0:T(8,128)(2,1)} %convolution_convert_fusion.3.refs_2_), custom_call_target="tpu_custom_call" | custom-call | tf_op jit(solution)/shard_map/pallas_call | solution.py:167
  267.5 5.4 fusion.22
  273.0 3.9 bitcast_convert_fusion.5
  282.5 8.7 %shard_map.184 = bf16[2,128,2304]{2,1,0:T(8,128)(2,1)} custom-call(bf16[2,128,2304]{2,1,0:T(8,128)(2,1)} %convolution_convert_fusion.1.refs_0_, s32[2,128,1]{2,1,0:T(8,128)} %copy.53.refs_1_, bf16[2,128,768]{2,1,0:T(8,128)(2,1)} %convolution_convert_fusion.4.refs_2_), custom_call_target="tpu_custom_call" | custom-call | tf_op jit(solution)/shard_map/pallas_call | solution.py:167
  291.2 3.7 fusion.35
  299.5 4.2 broadcast_select_fusion.2
  304.1 5.2 broadcast_select_fusion.1
  309.6 3.8 broadcast_select_fusion.3
  313.7 5.0 broadcast_select_fusion
  326.7 2.9 collective-permute-done.3
  329.6 2.7 add_convert_fusion.6
  332.4 4.1 add_convert_fusion.4
  336.5 5.0 add_convert_fusion.2
  341.6 9.3 %add_convert_fusion.1 = bf16[768,3072]{1,0:T(8,128)(2,1)} fusion(bf16[768,3072]{1,0:T(8,128)(2,1)} %collective-permute-done.5, bf16[768,3072]{1,0:T(8,128)(2,1)} %bitcast_convert_fusion.3, bf16[768,3072]{1,0:T(8,128)(2,1)} %get-tuple-element.144, pred[]{:T(512)S(6)} %eq.2), kind=kLoop, calls=%fused_computation.5 | loop fusion | flops 11796480 | bytes 18874368 | tf_op jit(solution)/shard_map/convert_element_type | solution.py:21
  350.9 6.2 %add_convert_fusion = bf16[3072,768]{1,0:T(8,128)(2,1)} fusion(bf16[3072,768]{1,0:T(8,128)(2,1)} %collective-permute-done.6, bf16[3072,768]{1,0:T(8,128)(2,1)S(1)} %bitcast.141, bf16[3072,768]{1,0:T(8,128)(2,1)S(1)} %bitcast.143, pred[]{:T(512)S(6)} %eq.2), kind=kLoop, calls=%fused_computation.4 | loop fusion | flops 11796480 | bytes 18874368 | tf_op jit(solution)/shard_map/convert_element_type | solution.py:21
  357.1 196.5 %shard_map.185 = (f32[2,48,2304]{2,1,0:T(8,128)}, f32[2,48,768]{2,1,0:T(8,128)}, f32[2,48,1536]{2,1,0:T(8,128)}, f32[2,48,3072]{2,1,0:T(8,128)}, f32[2,192,768]{2,1,0:T(8,128)}, /*index=5*/f32[2,16,128]{2,1,0:T(8,128)}) custom-call(bf16[8,2,48,2304]{3,2,1,0:T(8,128)(2,1)} %bitcast.148, bf16[8,2,48,768]{3,2,1,0:T(8,128)(2,1)} %bitcast.152, ...), custom_call_target="tpu_custom_call" | custom-call | tf_op jit(solution)/shard_map/pallas_call | solution.py:415
  (288 shorter events, 68.8 us)
Async XLA Ops:
  3.9 126.5 %collective-permute-start = (bf16[2,452,384]{2,0,1:T(2,128)(2,1)S(1)}, bf16[2,452,384]{2,0,1:T(2,128)(2,1)S(1)}, u32[]{:S(2)}, u32[]{:S(2)}) collective-permute-start(bf16[2,452,384]{2,0,1:T(2,128)(2,1)S(1)} %copy.50), channel_id=1, source_target_pairs={{0,16},{16,0},{1,17},{17,1},{2,18},{18,2},{3,19},{19,3},{4,20},{20... | collective-permute-start | bytes 2082824 | tf_op jit(solution)/shard_map/ppermute | solution.py:17
  130.7 81.0 %copy-start.16 = (bf16[2,128,768]{2,1,0:T(8,128)(2,1)}, bf16[2,128,768]{2,1,0:T(8,128)(2,1)S(1)}, u32[]{:S(2)}) copy-start(bf16[2,128,768]{2,1,0:T(8,128)(2,1)S(1)} %pad_maximum_fusion.7) | copy-start | bytes 1179652
  156.8 19.2 %copy-start.5 = (f32[2,196,768]{2,1,0:T(8,128)}, f32[2,196,768]{2,1,0:T(8,128)S(1)}, u32[]{:S(2)}) copy-start(f32[2,196,768]{2,1,0:T(8,128)S(1)} %get-tuple-element.121) | copy-start | bytes 3612676
  156.9 19.2 %slice-start.16 = ((s8[4718592]{0:T(1024)(128)(4,1)}), s8[4194304]{0:T(1024)(128)(4,1)S(1)}, s32[]{:S(2)}) async-start(s8[4718592]{0:T(1024)(128)(4,1)} %bitcast.187), calls=%async_computation.16 | async-start | bytes 8388608
  157.2 18.9 %slice-start.17 = ((s8[4718592]{0:T(1024)(128)(4,1)}), s8[524288]{0:T(1024)(128)(4,1)S(1)}, s32[]{:S(2)}) async-start(s8[4718592]{0:T(1024)(128)(4,1)} %bitcast.187), calls=%async_computation.17 | async-start | bytes 1048576
  163.7 12.3 %copy-start.19 = (f32[2,196,3072]{2,1,0:T(8,128)}, f32[2,196,3072]{2,1,0:T(8,128)S(1)}, u32[]{:S(2)}) copy-start(f32[2,196,3072]{2,1,0:T(8,128)S(1)} %get-tuple-element.122) | copy-start | bytes 14450692
  192.3 15.2 %slice-start.10 = ((s8[4718592]{0:T(1024)(128)(4,1)}), s8[4194304]{0:T(1024)(128)(4,1)S(1)}, s32[]{:S(2)}) async-start(s8[4718592]{0:T(1024)(128)(4,1)} %bitcast.176), calls=%async_computation.10 | async-start | bytes 8388608
  194.7 12.9 %slice-start.11 = ((s8[4718592]{0:T(1024)(128)(4,1)}), s8[524288]{0:T(1024)(128)(4,1)S(1)}, s32[]{:S(2)}) async-start(s8[4718592]{0:T(1024)(128)(4,1)} %bitcast.176), calls=%async_computation.11 | async-start | bytes 1048576
  199.5 10.2 %slice-start.18 = ((s8[4718592]{0:T(1024)(128)(4,1)}), s8[4194304]{0:T(1024)(128)(4,1)S(1)}, s32[]{:S(2)}) async-start(s8[4718592]{0:T(1024)(128)(4,1)} %bitcast.191), calls=%async_computation.18 | async-start | bytes 8388608
  227.5 51.7 %copy-start.13 = (f32[2,128,768]{2,1,0:T(8,128)}, f32[2,128,768]{2,1,0:T(8,128)S(1)}, u32[]{:S(2)}) copy-start(f32[2,128,768]{2,1,0:T(8,128)S(1)} %get-tuple-element.130) | copy-start | bytes 2359300
  232.1 8.4 %slice-start.14 = ((s8[4718592]{0:T(1024)(128)(4,1)}), s8[524288]{0:T(1024)(128)(4,1)S(1)}, s32[]{:S(2)}) async-start(s8[4718592]{0:T(1024)(128)(4,1)} %bitcast.183), calls=%async_computation.14 | async-start | bytes 1048576
  232.6 19.8 %copy-start.7 = (f32[2,196,768]{2,1,0:T(8,128)}, f32[2,196,768]{2,1,0:T(8,128)S(1)}, u32[]{:S(2)}) copy-start(f32[2,196,768]{2,1,0:T(8,128)S(1)} %get-tuple-element.101) | copy-start | bytes 3612676
  233.1 7.5 %copy-start.6 = (f32[2,196,768]{2,1,0:T(8,128)S(1)}, f32[2,196,768]{2,1,0:T(8,128)}, u32[]{:S(2)}) copy-start(f32[2,196,768]{2,1,0:T(8,128)} %copy-done.5) | copy-start | bytes 3612676
  233.1 7.5 %slice-start.15 = ((s8[4718592]{0:T(1024)(128)(4,1)}), s8[4194304]{0:T(1024)(128)(4,1)S(1)}, s32[]{:S(2)}) async-start(s8[4718592]{0:T(1024)(128)(4,1)} %bitcast.183), calls=%async_computation.15 | async-start | bytes 8388608
  267.5 9.4 %slice-start.12 = ((s8[4718592]{0:T(1024)(128)(4,1)}), s8[4194304]{0:T(1024)(128)(4,1)S(1)}, s32[]{:S(2)}) async-start(s8[4718592]{0:T(1024)(128)(4,1)} %bitcast.179), calls=%async_computation.12 | async-start | bytes 8388608
  297.2 22.4 %collective-permute-start.7 = (bf16[3,768]{1,0:T(4,128)(2,1)S(1)}, bf16[3,768]{1,0:T(4,128)(2,1)S(1)}, u32[]{:S(2)}, u32[]{:S(2)}) collective-permute-start(bf16[3,768]{1,0:T(4,128)(2,1)S(1)} %broadcast_select_fusion.13), channel_id=1, source_target_pairs={{0,16},{16,0},{1,17},{17,1},{2,18},{18,2},{3,19},{19,3},{4,20},{20... | collective-permute-start | bytes 13832 | tf_op jit(solution)/shard_map/ppermute | solution.py:17
  298.5 23.2 %collective-permute-start.1 = (bf16[2,452,384]{2,0,1:T(2,128)(2,1)S(1)}, bf16[2,452,384]{2,0,1:T(2,128)(2,1)}, u32[]{:S(2)}, u32[]{:S(2)}) collective-permute-start(bf16[2,452,384]{2,0,1:T(2,128)(2,1)S(1)} %copy.59), channel_id=1, source_target_pairs={{0,16},{16,0},{1,17},{17,1},{2,18},{18,2},{3,19},{19,3},{4,20},{20... | collective-permute-start | bytes 2082824 | tf_op jit(solution)/shard_map/ppermute | solution.py:17
  303.7 32.8 %collective-permute-start.2 = (bf16[768,2304]{1,0:T(8,128)(2,1)}, bf16[768,2304]{1,0:T(8,128)(2,1)}, u32[]{:S(2)}, u32[]{:S(2)}) collective-permute-start(bf16[768,2304]{1,0:T(8,128)(2,1)} %get-tuple-element.137), channel_id=1, source_target_pairs={{0,16},{16,0},{1,17},{17,1},{2,18},{18,2},{3,19},{19,3},{4,20},{20... | collective-permute-start | bytes 10616840 | tf_op jit(solution)/shard_map/ppermute | solution.py:17
  309.3 32.2 %collective-permute-start.5 = (bf16[768,3072]{1,0:T(8,128)(2,1)}, bf16[768,3072]{1,0:T(8,128)(2,1)}, u32[]{:S(2)}, u32[]{:S(2)}) collective-permute-start(bf16[768,3072]{1,0:T(8,128)(2,1)} %get-tuple-element.143), channel_id=1, source_target_pairs={{0,16},{16,0},{1,17},{17,1},{2,18},{18,2},{3,19},{19,3},{4,20},{20... | collective-permute-start | bytes 14155784 | tf_op jit(solution)/shard_map/ppermute | solution.py:17
  313.3 19.0 %collective-permute-start.4 = (bf16[768,1536]{1,0:T(8,128)(2,1)}, bf16[768,1536]{1,0:T(8,128)(2,1)}, u32[]{:S(2)}, u32[]{:S(2)}) collective-permute-start(bf16[768,1536]{1,0:T(8,128)(2,1)} %get-tuple-element.141), channel_id=1, source_target_pairs={{0,16},{16,0},{1,17},{17,1},{2,18},{18,2},{3,19},{19,3},{4,20},{20... | collective-permute-start | bytes 7077896 | tf_op jit(solution)/shard_map/ppermute | solution.py:17
  319.6 31.2 %collective-permute-start.6 = (bf16[3072,768]{1,0:T(8,128)(2,1)}, bf16[3072,768]{1,0:T(8,128)(2,1)}, u32[]{:S(2)}, u32[]{:S(2)}) collective-permute-start(bf16[3072,768]{1,0:T(8,128)(2,1)} %get-tuple-element.145), channel_id=1, source_target_pairs={{0,16},{16,0},{1,17},{17,1},{2,18},{18,2},{3,19},{19,3},{4,20},{20... | collective-permute-start | bytes 14155784 | tf_op jit(solution)/shard_map/ppermute | solution.py:17
  321.7 7.9 %collective-permute-start.3 = (bf16[768,768]{1,0:T(8,128)(2,1)}, bf16[768,768]{1,0:T(8,128)(2,1)}, u32[]{:S(2)}, u32[]{:S(2)}) collective-permute-start(bf16[768,768]{1,0:T(8,128)(2,1)} %get-tuple-element.139), channel_id=1, source_target_pairs={{0,16},{16,0},{1,17},{17,1},{2,18},{18,2},{3,19},{19,3},{4,20},{20... | collective-permute-start | bytes 3538952 | tf_op jit(solution)/shard_map/ppermute | solution.py:17
  325.3 7.0 %copy-start.26 = (bf16[768,768]{1,0:T(8,128)(2,1)S(1)}, bf16[768,768]{1,0:T(8,128)(2,1)}, u32[]{:S(2)}) copy-start(bf16[768,768]{1,0:T(8,128)(2,1)} %bitcast_convert_fusion.8) | copy-start | bytes 3538948
  325.3 7.0 %copy-start.28 = (bf16[768,768]{1,0:T(8,128)(2,1)S(1)}, bf16[768,768]{1,0:T(8,128)(2,1)}, u32[]{:S(2)}) copy-start(bf16[768,768]{1,0:T(8,128)(2,1)} %bitcast_convert_fusion.7) | copy-start | bytes 3538948
  325.3 7.0 %copy-start.38 = (bf16[768,1536]{1,0:T(8,128)(2,1)S(1)}, bf16[768,1536]{1,0:T(8,128)(2,1)}, u32[]{:S(2)}) copy-start(bf16[768,1536]{1,0:T(8,128)(2,1)} %get-tuple-element.142) | copy-start | bytes 7077892
  341.5 9.3 %slice-start.2 = ((s8[4718592]{0:T(1024)(128)(4,1)}), s8[4194304]{0:T(1024)(128)(4,1)S(1)}, s32[]{:S(2)}) async-start(s8[4718592]{0:T(1024)(128)(4,1)} %bitcast.140), calls=%async_computation.2 | async-start | bytes 8388608
  341.5 9.3 %slice-start.4 = ((s8[4718592]{0:T(1024)(128)(4,1)}), s8[4194304]{0:T(1024)(128)(4,1)S(1)}, s32[]{:S(2)}) async-start(s8[4718592]{0:T(1024)(128)(4,1)} %bitcast.142), calls=%async_computation.4 | async-start | bytes 8388608
  341.5 9.3 %slice-start.3 = ((s8[4718592]{0:T(1024)(128)(4,1)}), s8[524288]{0:T(1024)(128)(4,1)S(1)}, s32[]{:S(2)}) async-start(s8[4718592]{0:T(1024)(128)(4,1)} %bitcast.140), calls=%async_computation.3 | async-start | bytes 1048576
  341.5 9.3 %slice-start.5 = ((s8[4718592]{0:T(1024)(128)(4,1)}), s8[524288]{0:T(1024)(128)(4,1)S(1)}, s32[]{:S(2)}) async-start(s8[4718592]{0:T(1024)(128)(4,1)} %bitcast.142), calls=%async_computation.5 | async-start | bytes 1048576
  553.6 7.2 %copy-start.47 = (f32[2,48,3072]{2,1,0:T(8,128)S(1)}, f32[2,48,3072]{2,1,0:T(8,128)}, u32[]{:S(2)}) copy-start(f32[2,48,3072]{2,1,0:T(8,128)} %get-tuple-element.46) | copy-start | bytes 3538948
  553.6 8.2 %copy-start.46 = (f32[2,192,768]{2,1,0:T(8,128)S(1)}, f32[2,192,768]{2,1,0:T(8,128)}, u32[]{:S(2)}) copy-start(f32[2,192,768]{2,1,0:T(8,128)} %get-tuple-element.47) | copy-start | bytes 3538948
  555.0 7.8 %copy-start.1 = (s32[4,196]{1,0:T(4,128)S(1)}, s32[4,196]{1,0:T(4,128)}, u32[]{:S(2)}) copy-start(s32[4,196]{1,0:T(4,128)} %param.13) | copy-start | bytes 9412
  (55 other events, 191.0 us)

commit v5 on v4

--- a/solution.py
+++ b/solution.py
@@ -312,11 +312,12 @@
 
 
 def reduce_kernel(size, reps, kinds, *refs):
-    grads, outs = refs[:kinds], refs[kinds : 2 * kinds]
-    slots, sides = refs[2 * kinds : 3 * kinds], refs[3 * kinds : 4 * kinds]
-    send, recv, side_send, side_recv = refs[4 * kinds :]
+    firsts, seconds, outs, owned, paired, slots, sides = (
+        refs[at * kinds : (at + 1) * kinds] for at in range(7)
+    )
+    send, recv, side_send, side_recv, keep, pair_send, pair_recv = refs[7 * kinds :]
     place = ring_place(lax.axis_index("dp"), size)
-    replica = lax.axis_index("rep")
+    replica, section = lax.axis_index("rep"), lax.axis_index("section")
     targets = (
         ring_shard((place + 1) % size, size),
         ring_shard((place + size - 1) % size, size),
@@ -333,11 +334,55 @@
             device_id={"rep": (replica + other) % reps},
             device_id_type=MESH_IDS,
         )
-    pl.semaphore_wait(barrier, 1 + reps)
+    pl.semaphore_signal(
+        barrier, inc=1, device_id={"section": 1 - section}, device_id_type=MESH_IDS
+    )
+    pl.semaphore_wait(barrier, 2 + reps)
+
+    def chunk_of(way, step):
+        return ring_shard((place + signs[way] * (step + 1) + 2 * size) % size, size)
+
+    def load(source, kind, way, step):
+        at = chunk_of(way, step)
+        return pltpu.make_async_copy(
+            source[kind].at[at, way], owned[kind].at[at, way], keep.at[kind, way, step]
+        )
+
+    def pair(source, kind, way, step):
+        at = chunk_of(way, step)
+        return pltpu.make_async_remote_copy(
+            src_ref=source[kind].at[at, way],
+            dst_ref=paired[kind].at[at, way],
+            send_sem=pair_send.at[kind],
+            recv_sem=pair_recv.at[kind, way, step],
+            device_id={"section": 1 - section},
+            device_id_type=MESH_IDS,
+        )
+
+    def spread(mine, theirs):
+        def issue(step, carry):
+            for kind in range(kinds):
+                for way in range(2):
+                    pair(theirs, kind, way, step).start()
+                    load(mine, kind, way, step).start()
+            return carry
+
+        lax.fori_loop(0, size, issue, 0)
+
+    @pl.when(section == 0)
+    def _():
+        spread(firsts, seconds)
+
+    @pl.when(section == 1)
+    def _():
+        spread(seconds, firsts)
 
     def own(kind, way, step):
-        chunk = (place + signs[way] * (step + 1) + 2 * size) % size
-        return grads[kind].at[ring_shard(chunk, size), way]
+        load(owned, kind, way, step).wait()
+        pair(owned, kind, way, step).wait_recv()
+        at = chunk_of(way, step)
+        mine, other = owned[kind].at[at, way], paired[kind].at[at, way]
+        return mine, mine[...].astype(jnp.float32) + other[...].astype(jnp.float32)
 
     def hop(kind, way, step, source):
         return pltpu.make_async_remote_copy(
@@ -361,14 +406,14 @@
 
     def add(kind, way, step):
         slot = slots[kind].at[step, way]
-        mine = own(kind, way, step + 1)
-        slot[...] = (slot[...].astype(jnp.float32) + mine[...].astype(jnp.float32)).astype(
-            jnp.bfloat16
-        )
+        _, mine = own(kind, way, step + 1)
+        slot[...] = (slot[...].astype(jnp.float32) + mine).astype(jnp.bfloat16)
 
     for kind in range(kinds):
         for way in range(2):
-            hop(kind, way, 0, own(kind, way, 0)).start()
+            source, total = own(kind, way, 0)
+            source[...] = total.astype(jnp.bfloat16)
+            hop(kind, way, 0, source).start()
 
     def walk(step, carry):
         for kind in range(kinds):
@@ -402,26 +447,30 @@
     for kind in range(kinds):
         for other in range(1, reps):
             side(kind, other).wait_send()
-
-
-def reduce_all(grads):
+        pltpu.make_async_copy(owned[kind], owned[kind], pair_send.at[kind]).wait()
+
+
+def reduce_all(firsts, seconds):
     size, reps = lax.axis_size("dp"), lax.axis_size("rep")
-    kinds = len(grads)
-    pieces = [g.shape[1:] for g in grads]
-    scratch = [pltpu.VMEM((size - 1,) + p, jnp.bfloat16) for p in pieces]
+    kinds = len(firsts)
+    pieces = [g.shape[1:] for g in firsts]
+    scratch = [pltpu.VMEM(g.shape, jnp.bfloat16) for g in firsts] * 2
+    scratch += [pltpu.VMEM((size - 1,) + p, jnp.bfloat16) for p in pieces]
     scratch += [pltpu.VMEM((max(reps - 1, 1),) + p, jnp.bfloat16) for p in pieces]
     scratch += [pltpu.SemaphoreType.DMA((kinds, 2, size - 1))] * 2
     scratch += [pltpu.SemaphoreType.DMA((kinds, max(reps - 1, 1)))] * 2
+    scratch += [pltpu.SemaphoreType.DMA((kinds, 2, size)), pltpu.SemaphoreType.DMA((kinds,))]
+    scratch += [pltpu.SemaphoreType.DMA((kinds, 2, size))]
     return pl.pallas_call(
         functools.partial(reduce_kernel, size, reps, kinds),
         out_shape=[jax.ShapeDtypeStruct(p, jnp.float32) for p in pieces],
-        in_specs=[pl.BlockSpec(memory_space=pltpu.VMEM)] * kinds,
+        in_specs=[pl.BlockSpec(memory_space=pl.ANY)] * (2 * kinds),
         out_specs=[pl.BlockSpec(memory_space=pltpu.VMEM)] * kinds,
         scratch_shapes=scratch,
         compiler_params=pltpu.CompilerParams(
-            collective_id=0, has_side_effects=True, vmem_limit_bytes=60 * 1024 * 1024
+            collective_id=0, has_side_effects=True, vmem_limit_bytes=63 * 1024 * 1024
         ),
-    )(*grads)
+    )(*firsts, *seconds)
 
 
 def by_shard(total, dimension):
@@ -616,14 +665,6 @@
     return tuple(weights) + (gains.transpose(1, 0, 2).reshape(rows, -1),)
 
 
-def swap_blocks(first, second, section, dimension):
-    first, second = to_low(first), to_low(second)
-    incoming = partner(jnp.where(section == 0, second, first), "section", 0)
-    kept = jnp.where(section == 0, first, second)
-    total = to_low(kept.astype(jnp.float32) + incoming.astype(jnp.float32))
-    return by_shard(total, dimension)
-
-
 def local(
     patches,
     captions,
@@ -667,10 +708,10 @@
         section,
     )
     reduced = reduce_all(
-        [
-            swap_blocks(first, second, section, dimension)
-            for first, second, dimension in zip(enc_grads, dec_grads, (0, 0, 0, 0, 0, 1))
-        ]
+        *(
+            [by_shard(to_low(g), dimension) for g, dimension in zip(grads, (0, 0, 0, 0, 0, 1))]
+            for grads in (enc_grads, dec_grads)
+        )
     )
     summed = tuple(part.reshape(1, -1, part.shape[-1]) for part in reduced[:-1])
     summed += (reduced[-1][:1, :rows, :width],)

time: 569 us -> 540 us (0.949)
  other arithmetic: 61.7 us -> 40.8 us
    convert_element_type x12 -> x6, other arithmetic: 49 us -> 23.7 us  [to_low(): return values.astype(jnp.bfloat16)]
    unnamed x166 -> x130, local copies, waits for them, and re-layouts: 17.3 us -> 12.7 us
  transfers between devices with their start and end apart: 8 -> 2, of which waited for: 1 -> 0; matrix products, arithmetic and copies ran while one was open for 9% -> 3% of each run, Pallas kernels for 22% -> 59%
where the time goes in v5:
time: 540 us; the launch traced here: 534 us
  Pallas kernels  372 us (69%)
  matrix products  98.8 us (18%)
  other arithmetic  40.8 us (8%)
  local copies, waits for them, and re-layouts  19.8 us (4%)
    pallas_call x1, Pallas kernels, reduce_all(): pl.pallas_call(functools.partial(reduce_kernel, size, reps, kinds), out_s...  195 us
    pallas_call x1, Pallas kernels, gather_all(): pl.pallas_call(functools.partial(gather_kernel, size, reps, kinds, cuts),...  122 us
    dot_general x11, matrix products, weight_grad(): jnp.einsum('bsd,bse->de', acts, grads, preferred_element_type=jnp.float32)  34.9 us
    dot_general x11, matrix products, back_project(): jnp.einsum('bse,de->bsd', grads, weight, preferred_element_type=jnp.float32)  33 us
    pallas_call x3, Pallas kernels, attend_back(): pl.pallas_call(functools.partial(attend_back_kernel, causal, width, joint...  31.3 us
    dot_general x11, matrix products, project(): jnp.einsum('bsd,de->bse', acts, weight, preferred_element_type=jnp.float32)  30.9 us
    convert_element_type x6, other arithmetic, to_low(): return values.astype(jnp.bfloat16)  23.7 us
    pallas_call x3, Pallas kernels, attend(): pl.pallas_call(functools.partial(attend_kernel, causal, width, joint, sca...  23.6 us
  transfers between devices with their start and end apart: 2, of which 0 were waited for; matrix products, arithmetic and copies ran while one was open for 3% of the time, Pallas kernels for 59%

profile of v5, /device:TPU:0, one launch (start us, length us, event | category | flops | bytes accessed | tf_op | source)
XLA Modules:
  0.0 534.1 jit_solution(3002804978595567775)
XLA Ops:
  6.7 121.7 %shard_map.178 = (bf16[8,2,3,16,2304]{4,3,2,1,0:T(8,128)(2,1)}, bf16[8,2,3,16,768]{4,3,2,1,0:T(8,128)(2,1)}, bf16[8,2,3,16,1536]{4,3,2,1,0:T(8,128)(2,1)}, bf16[...) custom-call(bf16[2,3,16,2304]{3,2,1,0:T(8,128)(2,1)} %bitcast.176, ...), custom_call_target="tpu_custom_call" | custom-call | tf_op jit(solution)/shard_map/pallas_call | solution.py:651
  132.9 2.2 convolution_convert_fusion.1.refs_0_
  135.0 9.0 %shard_map.179 = bf16[2,128,768]{2,1,0:T(8,128)(2,1)} custom-call(bf16[2,128,2304]{2,1,0:T(8,128)(2,1)} %convolution_convert_fusion.1.refs_0_, s32[2,128,1]{2,1,0:T(8,128)} %copy.54.refs_1_), custom_call_target="tpu_custom_call" | custom-call | tf_op jit(solution)/shard_map/pallas_call | solution.py:151
  144.0 2.1 fusion.62
  146.5 3.1 convolution_convert_fusion.refs_0_
  149.6 5.3 shard_map.180
  154.9 2.2 fusion.63
  157.4 6.5 %fusion.24 = (u8[196,3072]{1,0:T(8,128)(4,1)S(1)}, u8[196,3072]{1,0:T(8,128)(4,1)S(1)}, f32[2,196,3072]{2,1,0:T(8,128)S(1)}) fusion(bf16[768,3072,1]{1,0,2:T(8,128)(2,1)} %bitcast.190, f32[2,196,768]{2,1,0:T(8,128)S(1)} %get-tuple-element.121, f32[768]{0:T(1024)S(1)} %mul.450, f32[2,196]{1,0:T(2,128)S(1)} %fusion.52, f32[2,196]{1,0:T(2,128)S(1)} %broadcast_multiply_fusion.1), kind=kOutput, calls=%fused_computation.95 | convolution fusion | flops 1865342976 | bytes 11950144 | tf_op jit(solution)/shard_map/bsd,de->bse/dot_general | solution.py:36
  163.9 12.3 %multiply_convert_fusion = (bf16[2,196,3072]{2,1,0:T(8,128)(2,1)S(1)}, f32[2,196,3072]{2,1,0:T(8,128)}) fusion(f32[2,196,3072]{2,1,0:T(8,128)S(1)} %get-tuple-element.122, u8[196,3072]{1,0:T(8,128)(4,1)S(1)} %get-tuple-element.77, u8[196,3072]{1,0:T(8,128)(4,1)S(1)} %get-tuple-element.76), kind=kLoop, calls=%fused_computation.14 | loop fusion | flops 84295680 | bytes 13246464 | tf_op jit(solution)/shard_map/convert_element_type | solution.py:21
  176.3 2.3 fusion.64
  180.9 2.3 convolution_convert_fusion.2.refs_1_
  183.2 9.3 %shard_map.181 = bf16[2,128,768]{2,1,0:T(8,128)(2,1)} custom-call(bf16[2,128,768]{2,1,0:T(8,128)(2,1)} %convolution_convert_fusion.6.refs_0_, bf16[2,196,1536]{2,1,0:T(8,128)(2,1)} %convolution_convert_fusion.2.refs_1_, s32[2,196,1]{2,1,0:T(8,128)} %copy.55.refs_1_.refs_2_), custom_call_target="tpu_custom_call" | custom-call | tf_op jit(solution)/shard_map/pallas_call | solution.py:151
  194.9 4.8 fusion.37
  199.7 8.0 %multiply_convert_fusion.1 = (bf16[2,128,3072]{2,1,0:T(8,128)(2,1)}, f32[2,128,3072]{2,1,0:T(8,128)S(1)}) fusion(f32[2,128,3072]{2,1,0:T(8,128)S(1)} %get-tuple-element.127, u8[128,3072]{1,0:T(8,128)(4,1)S(1)} %get-tuple-element.79, u8[128,3072]{1,0:T(8,128)(4,1)S(1)} %get-tuple-element.78), kind=kLoop, calls=%fused_computation.37 | loop fusion | flops 55050240 | bytes 8650752 | tf_op jit(solution)/shard_map/convert_element_type | solution.py:21
  214.9 11.0 %shard_map.182 = (bf16[2,128,768]{2,1,0:T(8,128)(2,1)}, bf16[2,196,1536]{2,1,0:T(8,128)(2,1)}) custom-call(bf16[2,128,768]{2,1,0:T(8,128)(2,1)} %convolution_convert_fusion.6.refs_0_, bf16[2,196,1536]{2,1,0:T(8,128)(2,1)} %convolution_convert_fusion.2.refs_1_, s32[2,196,1]{2,1,0:T(8,128)} %copy.55.refs_1_.refs_2_, ...), custom_call_target="tpu_custom_call" | custom-call | tf_op jit(solution)/shard_map/pallas_call | solution.py:167
  226.0 3.9 multiply_reduce_fusion
  229.9 3.0 bitcast_convert_fusion.6
  241.5 7.7 %add_convert_fusion = bf16[2,196,3072]{2,1,0:T(8,128)(2,1)} fusion(f32[2,196,3072]{2,1,0:T(8,128)S(1)} %bitcast.153, f32[2,196,3072]{2,1,0:T(8,128)S(1)} %bitcast.151, bf16[3072,768,1]{1,0,2:T(8,128)(2,1)} %bitcast.194, f32[2,196,768]{2,1,0:T(8,128)S(1)} %get-tuple-element.101, f32[2,196]{1,0:T(2,128)S(1)} %negate_multiply_fusion.4), kind=kOutput, calls=%fused_computation.13 | convolution fusion | flops 1867149312 | bytes 17966624 | tf_op jit(solution)/shard_map/bse,de->bsd/dot_general | solution.py:40
  249.3 4.1 multiply_reduce_fusion.1
  258.5 4.6 bitcast_convert_fusion.2
  263.1 11.6 %shard_map.183 = bf16[2,196,2304]{2,1,0:T(8,128)(2,1)} custom-call(bf16[2,196,2304]{2,1,0:T(8,128)(2,1)} %convolution_convert_fusion.refs_0_, s32[2,196,1]{2,1,0:T(8,128)} %copy.55.refs_1_.refs_2_, bf16[2,196,768]{2,1,0:T(8,128)(2,1)} %convolution_convert_fusion.3.refs_2_), custom_call_target="tpu_custom_call" | custom-call | tf_op jit(solution)/shard_map/pallas_call | solution.py:167
  274.7 5.4 %fusion.22 = (f32[2,196]{1,0:T(2,128)S(1)}, f32[2,196,768]{2,1,0:T(8,128)}) fusion(bf16[2,196,768]{2,1,0:T(8,128)(2,1)S(1)} %get-tuple-element.109, f32[768]{0:T(1024)S(1)} %mul.444, f32[2,196]{1,0:T(2,128)S(1)} %broadcast_multiply_fusion.2, bf16[2,196,2304]{2,1,0:T(8,128)(2,1)} %shard_map.183, bf16[768,2304,1]{1,0,2:T(8,128)(2,1)} %bitcast.204), kind=kOutput, calls=%fused_computation.83 | convolution fusion | flops 1388770944 | bytes 7157824 | tf_op jit(solution)/shard_map/bse,de->bsd/dot_general | solution.py:40
  280.1 4.0 bitcast_convert_fusion.5
  284.1 8.7 %shard_map.184 = bf16[2,128,2304]{2,1,0:T(8,128)(2,1)} custom-call(bf16[2,128,2304]{2,1,0:T(8,128)(2,1)} %convolution_convert_fusion.1.refs_0_, s32[2,128,1]{2,1,0:T(8,128)} %copy.54.refs_1_, bf16[2,128,768]{2,1,0:T(8,128)(2,1)} %convolution_convert_fusion.4.refs_2_), custom_call_target="tpu_custom_call" | custom-call | tf_op jit(solution)/shard_map/pallas_call | solution.py:167
  292.8 3.7 fusion.35
  296.5 3.1 bitcast_convert_fusion.4
  299.6 3.7 bitcast_convert_fusion.1
  303.4 2.1 fusion.18
  305.5 3.7 bitcast_convert_fusion
  312.2 2.7 add_convert_fusion.2
  322.8 6.2 %bitcast_convert_fusion.3 = bf16[768,3072]{1,0:T(8,128)(2,1)} fusion(bf16[2,196,3072]{2,1,0:T(8,128)(2,1)} %add_convert_fusion, f32[2,196,768]{2,1,0:T(8,128)S(1)} %copy-done.4, f32[768]{0:T(1024)S(1)} %mul.450, f32[2,196]{1,0:T(2,128)S(1)} %fusion.52, f32[2,196]{1,0:T(2,128)S(1)} %broadcast_multiply_fusion.1), kind=kOutput, calls=%fused_computation.3 | convolution fusion | flops 1853251584 | bytes 8337472 | tf_op jit(solution)/shard_map/bsd,bse->de/dot_general | solution.py:44
  329.0 195.3 %shard_map.185 = (f32[2,48,2304]{2,1,0:T(8,128)}, f32[2,48,768]{2,1,0:T(8,128)}, f32[2,48,1536]{2,1,0:T(8,128)}, f32[2,48,3072]{2,1,0:T(8,128)}, f32[2,192,768]{2,1,0:T(8,128)}, /*index=5*/f32[2,16,128]{2,1,0:T(8,128)}) custom-call(bf16[8,2,48,2304]{3,2,1,0:T(8,128)(2,1)} %bitcast.161, bf16[8,2,48,768]{3,2,1,0:T(8,128)(2,1)} %bitcast.167, ...), custom_call_target="tpu_custom_call" | custom-call | tf_op jit(solution)/shard_map/pallas_call | solution.py:464
  (232 shorter events, 56.8 us)
Async XLA Ops:
  0.6 4.6 copy-start
  1.8 4.2 copy-start.41
  3.9 126.5 %collective-permute-start = (bf16[2,452,384]{2,0,1:T(2,128)(2,1)S(1)}, bf16[2,452,384]{2,0,1:T(2,128)(2,1)S(1)}, u32[]{:S(2)}, u32[]{:S(2)}) collective-permute-start(bf16[2,452,384]{2,0,1:T(2,128)(2,1)S(1)} %copy.51), channel_id=1, source_target_pairs={{0,16},{16,0},{1,17},{17,1},{2,18},{18,2},{3,19},{19,3},{4,20},{20... | collective-permute-start | bytes 2082824 | tf_op jit(solution)/shard_map/ppermute | solution.py:17
  130.7 81.2 %copy-start.10 = (bf16[2,128,768]{2,1,0:T(8,128)(2,1)}, bf16[2,128,768]{2,1,0:T(8,128)(2,1)S(1)}, u32[]{:S(2)}) copy-start(bf16[2,128,768]{2,1,0:T(8,128)(2,1)S(1)} %pad_maximum_fusion.7) | copy-start | bytes 1179652
  157.1 19.2 %copy-start.2 = (f32[2,196,768]{2,1,0:T(8,128)}, f32[2,196,768]{2,1,0:T(8,128)S(1)}, u32[]{:S(2)}) copy-start(f32[2,196,768]{2,1,0:T(8,128)S(1)} %get-tuple-element.121) | copy-start | bytes 3612676
  157.1 19.2 %slice-start.10 = ((s8[4718592]{0:T(1024)(128)(4,1)}), s8[4194304]{0:T(1024)(128)(4,1)S(1)}, s32[]{:S(2)}) async-start(s8[4718592]{0:T(1024)(128)(4,1)} %bitcast.195), calls=%async_computation.10 | async-start | bytes 8388608
  157.4 18.9 %slice-start.11 = ((s8[4718592]{0:T(1024)(128)(4,1)}), s8[524288]{0:T(1024)(128)(4,1)S(1)}, s32[]{:S(2)}) async-start(s8[4718592]{0:T(1024)(128)(4,1)} %bitcast.195), calls=%async_computation.11 | async-start | bytes 1048576
  163.9 12.3 %copy-start.13 = (f32[2,196,3072]{2,1,0:T(8,128)}, f32[2,196,3072]{2,1,0:T(8,128)S(1)}, u32[]{:S(2)}) copy-start(f32[2,196,3072]{2,1,0:T(8,128)S(1)} %get-tuple-element.122) | copy-start | bytes 14450692
  192.5 15.2 %slice-start.4 = ((s8[4718592]{0:T(1024)(128)(4,1)}), s8[4194304]{0:T(1024)(128)(4,1)S(1)}, s32[]{:S(2)}) async-start(s8[4718592]{0:T(1024)(128)(4,1)} %bitcast.184), calls=%async_computation.4 | async-start | bytes 8388608
  194.9 12.9 %slice-start.5 = ((s8[4718592]{0:T(1024)(128)(4,1)}), s8[524288]{0:T(1024)(128)(4,1)S(1)}, s32[]{:S(2)}) async-start(s8[4718592]{0:T(1024)(128)(4,1)} %bitcast.184), calls=%async_computation.5 | async-start | bytes 1048576
  199.7 10.2 %slice-start.12 = ((s8[4718592]{0:T(1024)(128)(4,1)}), s8[4194304]{0:T(1024)(128)(4,1)S(1)}, s32[]{:S(2)}) async-start(s8[4718592]{0:T(1024)(128)(4,1)} %bitcast.199), calls=%async_computation.12 | async-start | bytes 8388608
  226.0 3.9 copy-start.15
  226.0 3.9 copy-start.46
  233.5 4.3 copy-start.20
  233.5 8.0 %slice-start.2 = ((s8[4915200]{0:T(1024)(128)(4,1)}), s8[4194304]{0:T(1024)(128)(4,1)S(1)}, s32[]{:S(2)}) async-start(s8[4915200]{0:T(1024)(128)(4,1)} %bitcast.152), calls=%async_computation.2 | async-start | bytes 8388608
  235.6 5.8 %slice-start = ((s8[4915200]{0:T(1024)(128)(4,1)}), s8[4194304]{0:T(1024)(128)(4,1)S(1)}, s32[]{:S(2)}) async-start(s8[4915200]{0:T(1024)(128)(4,1)} %bitcast.150), calls=%async_computation | async-start | bytes 8388608
  236.5 4.9 slice-start.3
  237.8 3.7 slice-start.1
  240.9 8.3 %slice-start.8 = ((s8[4718592]{0:T(1024)(128)(4,1)}), s8[524288]{0:T(1024)(128)(4,1)S(1)}, s32[]{:S(2)}) async-start(s8[4718592]{0:T(1024)(128)(4,1)} %bitcast.191), calls=%async_computation.8 | async-start | bytes 1048576
  241.4 17.1 %copy-start.5 = (f32[2,196,768]{2,1,0:T(8,128)}, f32[2,196,768]{2,1,0:T(8,128)S(1)}, u32[]{:S(2)}) copy-start(f32[2,196,768]{2,1,0:T(8,128)S(1)} %get-tuple-element.101) | copy-start | bytes 3612676
  241.5 7.7 %copy-start.3 = (f32[2,196,768]{2,1,0:T(8,128)S(1)}, f32[2,196,768]{2,1,0:T(8,128)}, u32[]{:S(2)}) copy-start(f32[2,196,768]{2,1,0:T(8,128)} %copy-done.2) | copy-start | bytes 3612676
  241.5 7.7 %slice-start.9 = ((s8[4718592]{0:T(1024)(128)(4,1)}), s8[4194304]{0:T(1024)(128)(4,1)S(1)}, s32[]{:S(2)}) async-start(s8[4718592]{0:T(1024)(128)(4,1)} %bitcast.191), calls=%async_computation.9 | async-start | bytes 8388608
  274.7 5.4 %copy-start.28 = (bf16[2,196,2304]{2,1,0:T(8,128)(2,1)S(1)}, bf16[2,196,2304]{2,1,0:T(8,128)(2,1)}, u32[]{:S(2)}) copy-start(bf16[2,196,2304]{2,1,0:T(8,128)(2,1)} %shard_map.183) | copy-start | bytes 5419012
  292.7 3.7 copy-start.17
  292.8 10.6 %slice-start.6 = ((s8[4718592]{0:T(1024)(128)(4,1)}), s8[4194304]{0:T(1024)(128)(4,1)S(1)}, s32[]{:S(2)}) async-start(s8[4718592]{0:T(1024)(128)(4,1)} %bitcast.187), calls=%async_computation.6 | async-start | bytes 8388608
  296.5 6.9 %slice-start.7 = ((s8[4718592]{0:T(1024)(128)(4,1)}), s8[524288]{0:T(1024)(128)(4,1)S(1)}, s32[]{:S(2)}) async-start(s8[4718592]{0:T(1024)(128)(4,1)} %bitcast.187), calls=%async_computation.7 | async-start | bytes 1048576
  299.6 3.7 copy-start.7
  314.9 4.5 copy-start.18
  314.9 4.5 copy-start.19
  319.0 3.8 copy-start.4
  319.0 206.5 %collective-permute-start.1 = (bf16[2,452,384]{2,0,1:T(2,128)(2,1)}, bf16[2,452,384]{2,0,1:T(2,128)(2,1)S(1)}, u32[]{:S(2)}, u32[]{:S(2)}) collective-permute-start(bf16[2,452,384]{2,0,1:T(2,128)(2,1)} %copy.60), channel_id=1, source_target_pairs={{0,16},{16,0},{1,17},{17,1},{2,18},{18,2},{3,19},{19,3},{4,20},{20... | collective-permute-start | bytes 2082824 | tf_op jit(solution)/shard_map/ppermute | solution.py:17
  527.1 3.8 copy-start.38
  (31 other events, 74.1 us)

commit v6 on v5

--- a/solution.py
+++ b/solution.py
@@ -311,11 +311,15 @@
     return 2 * row + column
 
 
-def reduce_kernel(size, reps, kinds, *refs):
+def reduce_kernel(size, reps, kinds, early, *refs):
     firsts, seconds, outs, owned, paired, slots, sides = (
         refs[at * kinds : (at + 1) * kinds] for at in range(7)
     )
-    send, recv, side_send, side_recv, keep, pair_send, pair_recv = refs[7 * kinds :]
+    crossed = dict(zip(early, refs[7 * kinds :]))
+    late = [kind for kind in range(kinds) if kind not in early]
+    send, recv, side_send, side_recv, keep, pair_send, pair_recv, cross_send, cross_recv = refs[
+        7 * kinds + len(early) :
+    ]
     place = ring_place(lax.axis_index("dp"), size)
     replica, section = lax.axis_index("rep"), lax.axis_index("section")
     targets = (
@@ -377,12 +381,44 @@
     def _():
         spread(seconds, firsts)
 
-    def own(kind, way, step):
+    def part_of(kind):
+        return replica if kind in early else 0
+
+    def settled(kind, way, step):
         load(owned, kind, way, step).wait()
         pair(owned, kind, way, step).wait_recv()
+
+    def both(kind, way, step, part):
         at = chunk_of(way, step)
-        mine, other = owned[kind].at[at, way], paired[kind].at[at, way]
+        mine, other = owned[kind].at[at, way, part], paired[kind].at[at, way, part]
         return mine, mine[...].astype(jnp.float32) + other[...].astype(jnp.float32)
+
+    def cross(kind, way, step):
+        at = chunk_of(way, step)
+        return pltpu.make_async_remote_copy(
+            src_ref=owned[kind].at[at, way, 1 - replica],
+            dst_ref=crossed[kind].at[at, way],
+            send_sem=cross_send.at[kind],
+            recv_sem=cross_recv.at[kind, way, step],
+            device_id={"rep": 1 - replica},
+            device_id_type=MESH_IDS,
+        )
+
+    def give(step):
+        for kind in early:
+            for way in range(2):
+                settled(kind, way, step)
+                source, total = both(kind, way, step, 1 - replica)
+                source[...] = total.astype(jnp.bfloat16)
+                cross(kind, way, step).start()
+
+    def own(kind, way, step):
+        if kind not in early:
+            settled(kind, way, step)
+            return both(kind, way, step, 0)
+        cross(kind, way, step).wait_recv()
+        source, total = both(kind, way, step, replica)
+        return source, total + crossed[kind][chunk_of(way, step), way].astype(jnp.float32)
 
     def hop(kind, way, step, source):
         return pltpu.make_async_remote_copy(
@@ -409,33 +445,63 @@
         _, mine = own(kind, way, step + 1)
         slot[...] = (slot[...].astype(jnp.float32) + mine).astype(jnp.bfloat16)
 
-    for kind in range(kinds):
-        for way in range(2):
-            source, total = own(kind, way, 0)
-            source[...] = total.astype(jnp.bfloat16)
-            hop(kind, way, 0, source).start()
-
-    def walk(step, carry):
-        for kind in range(kinds):
+    def begin(group):
+        for kind in group:
+            for way in range(2):
+                source, total = own(kind, way, 0)
+                source[...] = total.astype(jnp.bfloat16)
+                hop(kind, way, 0, source).start()
+
+    def advance(group, step, last):
+        for kind in group:
             for way in range(2):
                 hop(kind, way, step, slots[kind].at[step, way]).wait_recv()
                 add(kind, way, step)
-                hop(kind, way, step + 1, slots[kind].at[step, way]).start()
+                if not last:
+                    hop(kind, way, step + 1, slots[kind].at[step, way]).start()
+
+    def finish(group):
+        advance(group, size - 2, True)
+        for kind in group:
+            for other in range(1, reps):
+                side(kind, other).start()
+
+    begin(late)
+
+    def walk_late(step, carry):
+        if early:
+
+            @pl.when(step < size // 2)
+            def _():
+                give(2 * step)
+                give(2 * step + 1)
+
+        advance(late, step, False)
         return carry
 
-    lax.fori_loop(0, size - 2, walk, 0)
-    for kind in range(kinds):
-        for way in range(2):
-            hop(kind, way, size - 2, slots[kind].at[size - 2, way]).wait_recv()
-            add(kind, way, size - 2)
-        for other in range(1, reps):
-            side(kind, other).start()
-    for kind in range(kinds):
+    lax.fori_loop(0, size - 2, walk_late, 0)
+    finish(late)
+    if early:
+        begin(early)
+
+        def walk_early(step, carry):
+            advance(early, step, False)
+            return carry
+
+        lax.fori_loop(0, size - 2, walk_early, 0)
+        finish(early)
+    for kind in late:
         total = slots[kind][size - 2].astype(jnp.float32)
         for other in range(1, reps):
             side(kind, other).wait_recv()
             total += sides[kind][other - 1].astype(jnp.float32)
-        outs[kind][...] = total
+        outs[kind][:, 0] = total
+    for kind in early:
+        side(kind, 1).wait_recv()
+        for way in range(2):
+            mine, theirs = outs[kind].at[way, replica], outs[kind].at[way, 1 - replica]
+            mine[...] = slots[kind][size - 2, way].astype(jnp.float32)
+            theirs[...] = sides[kind][0, way].astype(jnp.float32)
 
     def drain(step, carry):
         for kind in range(kinds):
@@ -448,22 +514,27 @@
         for other in range(1, reps):
             side(kind, other).wait_send()
         pltpu.make_async_copy(owned[kind], owned[kind], pair_send.at[kind]).wait()
+    for kind in early:
+        pltpu.make_async_copy(crossed[kind], crossed[kind], cross_send.at[kind]).wait()
 
 
 def reduce_all(firsts, seconds):
     size, reps = lax.axis_size("dp"), lax.axis_size("rep")
     kinds = len(firsts)
-    pieces = [g.shape[1:] for g in firsts]
+    early = [kind for kind in range(kinds) if firsts[kind].shape[2] > 1]
+    pieces = [(2,) + g.shape[3:] for g in firsts]
     scratch = [pltpu.VMEM(g.shape, jnp.bfloat16) for g in firsts] * 2
     scratch += [pltpu.VMEM((size - 1,) + p, jnp.bfloat16) for p in pieces]
     scratch += [pltpu.VMEM((max(reps - 1, 1),) + p, jnp.bfloat16) for p in pieces]
+    scratch += [pltpu.VMEM((size,) + pieces[kind], jnp.bfloat16) for kind in early]
     scratch += [pltpu.SemaphoreType.DMA((kinds, 2, size - 1))] * 2
     scratch += [pltpu.SemaphoreType.DMA((kinds, max(reps - 1, 1)))] * 2
     scratch += [pltpu.SemaphoreType.DMA((kinds, 2, size)), pltpu.SemaphoreType.DMA((kinds,))]
     scratch += [pltpu.SemaphoreType.DMA((kinds, 2, size))]
+    scratch += [pltpu.SemaphoreType.DMA((kinds,)), pltpu.SemaphoreType.DMA((kinds, 2, size))]
     return pl.pallas_call(
-        functools.partial(reduce_kernel, size, reps, kinds),
-        out_shape=[jax.ShapeDtypeStruct(p, jnp.float32) for p in pieces],
+        functools.partial(reduce_kernel, size, reps, kinds, early),
+        out_shape=[jax.ShapeDtypeStruct(g.shape[1:], jnp.float32) for g in firsts],
         in_specs=[pl.BlockSpec(memory_space=pl.ANY)] * (2 * kinds),
         out_specs=[pl.BlockSpec(memory_space=pltpu.VMEM)] * kinds,
         scratch_shapes=scratch,
@@ -473,13 +544,15 @@
     )(*firsts, *seconds)
 
 
-def by_shard(total, dimension):
-    size = lax.axis_size("dp")
+def by_shard(total, dimension, early):
+    size, reps = lax.axis_size("dp"), lax.axis_size("rep")
     if dimension == 0:
-        return total.reshape(size, 2, total.shape[0] // (2 * size), total.shape[1])
+        half = total.shape[0] // (2 * size)
+        cut = 2 if early and reps == 2 and half % 16 == 0 else 1
+        return total.reshape(size, 2, cut, half // cut, total.shape[1])
     rows, width = total.shape
-    part = total.reshape(rows, size, width // size).transpose(1, 0, 2)[:, None]
-    return jnp.pad(part, ((0, 0), (0, 1), (0, 16 - rows), (0, 128 - width // size)))
+    part = total.reshape(rows, size, width // size).transpose(1, 0, 2)[:, None, None]
+    return jnp.pad(part, ((0, 0), (0, 1), (0, 0), (0, 16 - rows), (0, 128 - width // size)))
 
 
 def gather_kernel(size, reps, kinds, cuts, *refs):
@@ -709,12 +782,15 @@
     )
     reduced = reduce_all(
         *(
-            [by_shard(to_low(g), dimension) for g, dimension in zip(grads, (0, 0, 0, 0, 0, 1))]
+            [
+                by_shard(to_low(g), dimension, at in (1, 2, 3))
+                for at, (g, dimension) in enumerate(zip(grads, (0, 0, 0, 0, 0, 1)))
+            ]
             for grads in (enc_grads, dec_grads)
         )
     )
     summed = tuple(part.reshape(1, -1, part.shape[-1]) for part in reduced[:-1])
-    summed += (reduced[-1][:1, :rows, :width],)
+    summed += (reduced[-1][0, :, :rows, :width],)
     return (
         results[:, count : count + length],
         results[:, count + length :],

time: 540 us -> 486 us (0.900)
  Pallas kernels: 372 us -> 320 us
    pallas_call x1, Pallas kernels: 195 us -> 143 us  [reduce_all(): pl.pallas_call(functools.partial(reduce_kernel, size, reps, kinds, early)...]
    unnamed x130 -> x134, local copies, waits for them, and re-layouts: 12.7 us -> 12.1 us
  transfers between devices with their start and end apart: 2 -> 2, of which waited for: 0 -> 0; matrix products, arithmetic and copies ran while one was open for 3% -> 3% of each run, Pallas kernels for 59% -> 55%
where the time goes in v6:
time: 486 us; the launch traced here: 480 us
  Pallas kernels  320 us (66%)
  matrix products  97.2 us (20%)
  other arithmetic  41.1 us (8%)
  local copies, waits for them, and re-layouts  19.2 us (4%)
    pallas_call x1, Pallas kernels, reduce_all(): pl.pallas_call(functools.partial(reduce_kernel, size, reps, kinds, early)...  143 us
    pallas_call x1, Pallas kernels, gather_all(): pl.pallas_call(functools.partial(gather_kernel, size, reps, kinds, cuts),...  122 us
    dot_general x11, matrix products, weight_grad(): jnp.einsum('bsd,bse->de', acts, grads, preferred_element_type=jnp.float32)  33.2 us
    dot_general x11, matrix products, back_project(): jnp.einsum('bse,de->bsd', grads, weight, preferred_element_type=jnp.float32)  33.1 us
    pallas_call x3, Pallas kernels, attend_back(): pl.pallas_call(functools.partial(attend_back_kernel, causal, width, joint...  31.3 us
    dot_general x11, matrix products, project(): jnp.einsum('bsd,de->bse', acts, weight, preferred_element_type=jnp.float32)  31 us
    convert_element_type x6, other arithmetic, to_low(): return values.astype(jnp.bfloat16)  24.1 us
    pallas_call x3, Pallas kernels, attend(): pl.pallas_call(functools.partial(attend_kernel, causal, width, joint, sca...  23.6 us
  transfers between devices with their start and end apart: 2, of which 0 were waited for; matrix products, arithmetic and copies ran while one was open for 3% of the time, Pallas kernels for 55%

profile of v6, /device:TPU:0, one launch (start us, length us, event | category | flops | bytes accessed | tf_op | source)
XLA Modules:
  0.0 480.0 jit_solution(9013076993196293353)
XLA Ops:
  6.7 121.7 %shard_map.178 = (bf16[8,2,3,16,2304]{4,3,2,1,0:T(8,128)(2,1)}, bf16[8,2,3,16,768]{4,3,2,1,0:T(8,128)(2,1)}, bf16[8,2,3,16,1536]{4,3,2,1,0:T(8,128)(2,1)}, bf16[...) custom-call(bf16[2,3,16,2304]{3,2,1,0:T(8,128)(2,1)} %bitcast.178, ...), custom_call_target="tpu_custom_call" | custom-call | tf_op jit(solution)/shard_map/pallas_call | solution.py:724
  132.9 2.2 convolution_convert_fusion.1.refs_0_
  135.0 9.0 %shard_map.179 = bf16[2,128,768]{2,1,0:T(8,128)(2,1)} custom-call(bf16[2,128,2304]{2,1,0:T(8,128)(2,1)} %convolution_convert_fusion.1.refs_0_, s32[2,128,1]{2,1,0:T(8,128)} %copy.54.refs_1_), custom_call_target="tpu_custom_call" | custom-call | tf_op jit(solution)/shard_map/pallas_call | solution.py:151
  144.0 2.1 fusion.62
  146.5 3.1 convolution_convert_fusion.refs_0_
  149.6 5.3 %shard_map.180 = bf16[2,196,768]{2,1,0:T(8,128)(2,1)} custom-call(bf16[2,196,2304]{2,1,0:T(8,128)(2,1)} %convolution_convert_fusion.refs_0_, s32[2,196,1]{2,1,0:T(8,128)} %copy.55.refs_1_.refs_2_), custom_call_target="tpu_custom_call" | custom-call | tf_op jit(solution)/shard_map/pallas_call | solution.py:151
  154.9 2.2 fusion.63
  157.4 6.5 %fusion.24 = (u8[196,3072]{1,0:T(8,128)(4,1)S(1)}, u8[196,3072]{1,0:T(8,128)(4,1)S(1)}, f32[2,196,3072]{2,1,0:T(8,128)S(1)}) fusion(bf16[768,3072,1]{1,0,2:T(8,128)(2,1)} %bitcast.192, f32[2,196,768]{2,1,0:T(8,128)S(1)} %get-tuple-element.121, f32[768]{0:T(1024)S(1)} %mul.450, f32[2,196]{1,0:T(2,128)S(1)} %fusion.52, f32[2,196]{1,0:T(2,128)S(1)} %broadcast_multiply_fusion.1), kind=kOutput, calls=%fused_computation.95 | convolution fusion | flops 1865342976 | bytes 11950144 | tf_op jit(solution)/shard_map/bsd,de->bse/dot_general | solution.py:36
  163.9 12.3 %multiply_convert_fusion = (bf16[2,196,3072]{2,1,0:T(8,128)(2,1)S(1)}, f32[2,196,3072]{2,1,0:T(8,128)}) fusion(f32[2,196,3072]{2,1,0:T(8,128)S(1)} %get-tuple-element.122, u8[196,3072]{1,0:T(8,128)(4,1)S(1)} %get-tuple-element.77, u8[196,3072]{1,0:T(8,128)(4,1)S(1)} %get-tuple-element.76), kind=kLoop, calls=%fused_computation.14 | loop fusion | flops 84295680 | bytes 13246464 | tf_op jit(solution)/shard_map/convert_element_type | solution.py:21
  176.3 2.3 fusion.64
  180.9 2.3 convolution_convert_fusion.2.refs_1_
  183.2 9.3 %shard_map.181 = bf16[2,128,768]{2,1,0:T(8,128)(2,1)} custom-call(bf16[2,128,768]{2,1,0:T(8,128)(2,1)} %convolution_convert_fusion.6.refs_0_, bf16[2,196,1536]{2,1,0:T(8,128)(2,1)} %convolution_convert_fusion.2.refs_1_, s32[2,196,1]{2,1,0:T(8,128)} %copy.55.refs_1_.refs_2_), custom_call_target="tpu_custom_call" | custom-call | tf_op jit(solution)/shard_map/pallas_call | solution.py:151
  194.9 4.8 fusion.37
  199.7 8.0 %multiply_convert_fusion.1 = (bf16[2,128,3072]{2,1,0:T(8,128)(2,1)}, f32[2,128,3072]{2,1,0:T(8,128)S(1)}) fusion(f32[2,128,3072]{2,1,0:T(8,128)S(1)} %get-tuple-element.127, u8[128,3072]{1,0:T(8,128)(4,1)S(1)} %get-tuple-element.79, u8[128,3072]{1,0:T(8,128)(4,1)S(1)} %get-tuple-element.78), kind=kLoop, calls=%fused_computation.37 | loop fusion | flops 55050240 | bytes 8650752 | tf_op jit(solution)/shard_map/convert_element_type | solution.py:21
  214.9 11.0 %shard_map.182 = (bf16[2,128,768]{2,1,0:T(8,128)(2,1)}, bf16[2,196,1536]{2,1,0:T(8,128)(2,1)}) custom-call(bf16[2,128,768]{2,1,0:T(8,128)(2,1)} %convolution_convert_fusion.6.refs_0_, bf16[2,196,1536]{2,1,0:T(8,128)(2,1)} %convolution_convert_fusion.2.refs_1_, s32[2,196,1]{2,1,0:T(8,128)} %copy.55.refs_1_.refs_2_, ...), custom_call_target="tpu_custom_call" | custom-call | tf_op jit(solution)/shard_map/pallas_call | solution.py:167
  225.9 3.9 multiply_reduce_fusion
  229.8 3.0 bitcast_convert_fusion.6
  241.5 7.8 %add_convert_fusion = bf16[2,196,3072]{2,1,0:T(8,128)(2,1)} fusion(f32[2,196,3072]{2,1,0:T(8,128)S(1)} %bitcast.155, f32[2,196,3072]{2,1,0:T(8,128)S(1)} %bitcast.153, bf16[3072,768,1]{1,0,2:T(8,128)(2,1)} %bitcast.196, f32[2,196,768]{2,1,0:T(8,128)S(1)} %get-tuple-element.101, f32[2,196]{1,0:T(2,128)S(1)} %negate_multiply_fusion.4), kind=kOutput, calls=%fused_computation.13 | convolution fusion | flops 1867149312 | bytes 17966624 | tf_op jit(solution)/shard_map/bse,de->bsd/dot_general | solution.py:40
  249.3 4.1 multiply_reduce_fusion.1
  258.0 4.7 bitcast_convert_fusion.3
  262.7 4.5 bitcast_convert_fusion.2
  267.2 8.5 %shard_map.184 = bf16[2,128,2304]{2,1,0:T(8,128)(2,1)} custom-call(bf16[2,128,2304]{2,1,0:T(8,128)(2,1)} %convolution_convert_fusion.1.refs_0_, s32[2,128,1]{2,1,0:T(8,128)} %copy.54.refs_1_, bf16[2,128,768]{2,1,0:T(8,128)(2,1)} %convolution_convert_fusion.4.refs_2_), custom_call_target="tpu_custom_call" | custom-call | tf_op jit(solution)/shard_map/pallas_call | solution.py:167
  275.7 3.7 fusion.35
  279.5 3.1 bitcast_convert_fusion.4
  282.6 3.7 bitcast_convert_fusion.1
  286.3 2.1 fusion.18
  288.4 3.7 bitcast_convert_fusion
  294.1 11.8 %shard_map.183 = bf16[2,196,2304]{2,1,0:T(8,128)(2,1)} custom-call(bf16[2,196,2304]{2,1,0:T(8,128)(2,1)} %convolution_convert_fusion.refs_0_, s32[2,196,1]{2,1,0:T(8,128)} %copy.55.refs_1_.refs_2_, bf16[2,196,768]{2,1,0:T(8,128)(2,1)} %convolution_convert_fusion.3.refs_2_), custom_call_target="tpu_custom_call" | custom-call | tf_op jit(solution)/shard_map/pallas_call | solution.py:167
  305.9 5.3 %fusion.22 = (f32[2,196]{1,0:T(2,128)S(1)}, f32[2,196,768]{2,1,0:T(8,128)}) fusion(bf16[2,196,768]{2,1,0:T(8,128)(2,1)S(1)} %get-tuple-element.109, f32[768]{0:T(1024)S(1)} %mul.444, f32[2,196]{1,0:T(2,128)S(1)} %broadcast_multiply_fusion.2, bf16[2,196,2304]{2,1,0:T(8,128)(2,1)} %shard_map.183, bf16[768,2304,1]{1,0,2:T(8,128)(2,1)} %bitcast.204), kind=kOutput, calls=%fused_computation.83 | convolution fusion | flops 1388770944 | bytes 7157824 | tf_op jit(solution)/shard_map/bse,de->bsd/dot_general | solution.py:40
  313.3 2.3 add_convert_fusion.2
  323.1 4.0 bitcast_convert_fusion.5
  327.1 143.2 %shard_map.185 = (f32[2,1,48,2304]{3,2,1,0:T(8,128)}, f32[2,2,24,768]{3,2,1,0:T(8,128)}, f32[2,2,24,1536]{3,2,1,0:T(8,128)}, f32[2,2,24,3072]{3,2,1,0:T(8,128)},...) custom-call(bf16[8,2,1,48,2304]{4,3,2,1,0:T(8,128)(2,1)} %bitcast.163, bf16[8,2,2,24,768]{4,3,2,1,0:T(8,128)(2,1)} %bitcast.169, ...), custom_call_target="tpu_custom_call" | custom-call | tf_op jit(solution)/shard_map/pallas_call | solution.py:535
  (236 shorter events, 56.9 us)
Async XLA Ops:
  0.6 4.6 copy-start
  1.8 4.2 copy-start.42
  3.9 126.5 %collective-permute-start = (bf16[2,452,384]{2,0,1:T(2,128)(2,1)S(1)}, bf16[2,452,384]{2,0,1:T(2,128)(2,1)S(1)}, u32[]{:S(2)}, u32[]{:S(2)}) collective-permute-start(bf16[2,452,384]{2,0,1:T(2,128)(2,1)S(1)} %copy.51), channel_id=1, source_target_pairs={{0,16},{16,0},{1,17},{17,1},{2,18},{18,2},{3,19},{19,3},{4,20},{20... | collective-permute-start | bytes 2082824 | tf_op jit(solution)/shard_map/ppermute | solution.py:17
  130.7 81.2 %copy-start.10 = (bf16[2,128,768]{2,1,0:T(8,128)(2,1)}, bf16[2,128,768]{2,1,0:T(8,128)(2,1)S(1)}, u32[]{:S(2)}) copy-start(bf16[2,128,768]{2,1,0:T(8,128)(2,1)S(1)} %pad_maximum_fusion.7) | copy-start | bytes 1179652
  157.1 19.2 %copy-start.2 = (f32[2,196,768]{2,1,0:T(8,128)}, f32[2,196,768]{2,1,0:T(8,128)S(1)}, u32[]{:S(2)}) copy-start(f32[2,196,768]{2,1,0:T(8,128)S(1)} %get-tuple-element.121) | copy-start | bytes 3612676
  157.1 19.2 %slice-start.10 = ((s8[4718592]{0:T(1024)(128)(4,1)}), s8[4194304]{0:T(1024)(128)(4,1)S(1)}, s32[]{:S(2)}) async-start(s8[4718592]{0:T(1024)(128)(4,1)} %bitcast.197), calls=%async_computation.10 | async-start | bytes 8388608
  157.4 18.9 %slice-start.11 = ((s8[4718592]{0:T(1024)(128)(4,1)}), s8[524288]{0:T(1024)(128)(4,1)S(1)}, s32[]{:S(2)}) async-start(s8[4718592]{0:T(1024)(128)(4,1)} %bitcast.197), calls=%async_computation.11 | async-start | bytes 1048576
  163.9 12.3 %copy-start.13 = (f32[2,196,3072]{2,1,0:T(8,128)}, f32[2,196,3072]{2,1,0:T(8,128)S(1)}, u32[]{:S(2)}) copy-start(f32[2,196,3072]{2,1,0:T(8,128)S(1)} %get-tuple-element.122) | copy-start | bytes 14450692
  192.5 15.2 %slice-start.4 = ((s8[4718592]{0:T(1024)(128)(4,1)}), s8[4194304]{0:T(1024)(128)(4,1)S(1)}, s32[]{:S(2)}) async-start(s8[4718592]{0:T(1024)(128)(4,1)} %bitcast.186), calls=%async_computation.4 | async-start | bytes 8388608
  194.9 12.9 %slice-start.5 = ((s8[4718592]{0:T(1024)(128)(4,1)}), s8[524288]{0:T(1024)(128)(4,1)S(1)}, s32[]{:S(2)}) async-start(s8[4718592]{0:T(1024)(128)(4,1)} %bitcast.186), calls=%async_computation.5 | async-start | bytes 1048576
  199.7 10.2 %slice-start.12 = ((s8[4718592]{0:T(1024)(128)(4,1)}), s8[4194304]{0:T(1024)(128)(4,1)S(1)}, s32[]{:S(2)}) async-start(s8[4718592]{0:T(1024)(128)(4,1)} %bitcast.201), calls=%async_computation.12 | async-start | bytes 8388608
  225.9 3.9 copy-start.15
  225.9 3.9 copy-start.47
  233.4 4.3 copy-start.20
  233.4 8.0 %slice-start.2 = ((s8[4915200]{0:T(1024)(128)(4,1)}), s8[4194304]{0:T(1024)(128)(4,1)S(1)}, s32[]{:S(2)}) async-start(s8[4915200]{0:T(1024)(128)(4,1)} %bitcast.154), calls=%async_computation.2 | async-start | bytes 8388608
  235.6 5.8 %slice-start = ((s8[4915200]{0:T(1024)(128)(4,1)}), s8[4194304]{0:T(1024)(128)(4,1)S(1)}, s32[]{:S(2)}) async-start(s8[4915200]{0:T(1024)(128)(4,1)} %bitcast.152), calls=%async_computation | async-start | bytes 8388608
  236.5 4.9 %slice-start.3 = ((s8[4915200]{0:T(1024)(128)(4,1)}), s8[720896]{0:T(1024)(128)(4,1)S(1)}, s32[]{:S(2)}) async-start(s8[4915200]{0:T(1024)(128)(4,1)} %bitcast.154), calls=%async_computation.3 | async-start | bytes 1441792
  240.9 8.4 %slice-start.8 = ((s8[4718592]{0:T(1024)(128)(4,1)}), s8[524288]{0:T(1024)(128)(4,1)S(1)}, s32[]{:S(2)}) async-start(s8[4718592]{0:T(1024)(128)(4,1)} %bitcast.193), calls=%async_computation.8 | async-start | bytes 1048576
  241.4 21.3 %copy-start.4 = (f32[2,196,768]{2,1,0:T(8,128)}, f32[2,196,768]{2,1,0:T(8,128)S(1)}, u32[]{:S(2)}) copy-start(f32[2,196,768]{2,1,0:T(8,128)S(1)} %get-tuple-element.101) | copy-start | bytes 3612676
  241.5 7.8 %copy-start.3 = (f32[2,196,768]{2,1,0:T(8,128)S(1)}, f32[2,196,768]{2,1,0:T(8,128)}, u32[]{:S(2)}) copy-start(f32[2,196,768]{2,1,0:T(8,128)} %copy-done.2) | copy-start | bytes 3612676
  241.5 7.8 %slice-start.9 = ((s8[4718592]{0:T(1024)(128)(4,1)}), s8[4194304]{0:T(1024)(128)(4,1)S(1)}, s32[]{:S(2)}) async-start(s8[4718592]{0:T(1024)(128)(4,1)} %bitcast.193), calls=%async_computation.9 | async-start | bytes 8388608
  253.9 8.8 %copy-start.6 = (f32[2,196,768]{2,1,0:T(8,128)}, f32[2,196,768]{2,1,0:T(8,128)S(1)}, u32[]{:S(2)}) copy-start(f32[2,196,768]{2,1,0:T(8,128)S(1)} %get-tuple-element.99) | copy-start | bytes 3612676
  258.0 4.7 copy-start.23
  275.7 3.7 copy-start.17
  275.7 10.5 %slice-start.6 = ((s8[4718592]{0:T(1024)(128)(4,1)}), s8[4194304]{0:T(1024)(128)(4,1)S(1)}, s32[]{:S(2)}) async-start(s8[4718592]{0:T(1024)(128)(4,1)} %bitcast.189), calls=%async_computation.6 | async-start | bytes 8388608
  279.5 6.8 %slice-start.7 = ((s8[4718592]{0:T(1024)(128)(4,1)}), s8[524288]{0:T(1024)(128)(4,1)S(1)}, s32[]{:S(2)}) async-start(s8[4718592]{0:T(1024)(128)(4,1)} %bitcast.189), calls=%async_computation.7 | async-start | bytes 1048576
  282.6 3.7 copy-start.7
  305.9 7.4 %copy-start.5 = (f32[2,196,768]{2,1,0:T(8,128)S(1)}, f32[2,196,768]{2,1,0:T(8,128)}, u32[]{:S(2)}) copy-start(f32[2,196,768]{2,1,0:T(8,128)} %copy-done.4) | copy-start | bytes 3612676
  315.6 4.6 copy-start.18
  315.6 4.5 copy-start.19
  319.8 151.8 %collective-permute-start.1 = (bf16[2,452,384]{2,0,1:T(2,128)(2,1)}, bf16[2,452,384]{2,0,1:T(2,128)(2,1)S(1)}, u32[]{:S(2)}, u32[]{:S(2)}) collective-permute-start(bf16[2,452,384]{2,0,1:T(2,128)(2,1)} %copy.60), channel_id=1, source_target_pairs={{0,16},{16,0},{1,17},{17,1},{2,18},{18,2},{3,19},{19,3},{4,20},{20... | collective-permute-start | bytes 2082824 | tf_op jit(solution)/shard_map/ppermute | solution.py:17
  473.1 3.8 copy-start.39
  (33 other events, 82.1 us)
